TPU v7x, 32 devices: a whole 2x2x4 slice. The times are simulated.
32 devices in a mesh: seq: 8 (over z, x), fsdp: 4 (over y, core).
Axes of the slice: x: 2, y: 2, z: 4, core: 2. Of those that a mesh axis runs over, the one named last changes fastest.
Arguments:
- tokens: bfloat16 [4, 2048, 2048], P('fsdp', 'seq'), may hold values from -6 to 6
- routes: int32 [4, 2048, 8], P('fsdp', 'seq'), may hold values from 0 to 31, all different within a row; in each aligned block of 256 rows (0 to 255, 256 to 511, ..., all dimensions but the last counted through in order) at most 96 rows name the same one
- route_weights: float32 [4, 2048, 8], P('fsdp', 'seq'), may hold values from 0.05 to 0.5
- cotangent: bfloat16 [4, 2048, 2048], P('fsdp', 'seq'), may hold values from -6 to 6
- attn_gain: bfloat16 [2048], P('fsdp'), may hold values from 0.099609375 to 1.8984375
- query_gain: bfloat16 [2048], P('fsdp'), may hold values from 0.099609375 to 1.8984375
- key_gain: bfloat16 [2048], P('fsdp'), may hold values from 0.099609375 to 1.8984375
- ffn_gain: bfloat16 [2048], P('fsdp'), may hold values from 0.099609375 to 1.8984375
- w_query: bfloat16 [2048, 2048], P('fsdp'), may hold values from -0.125 to 0.125
- w_key: bfloat16 [2048, 2048], P('fsdp'), may hold values from -0.125 to 0.125
- w_value: bfloat16 [2048, 2048], P('fsdp'), may hold values from -0.125 to 0.125
- w_out: bfloat16 [2048, 2048], P('fsdp'), may hold values from -2 to 2
- w_gate: bfloat16 [2048, 32, 1024], P('fsdp', 'seq'), may hold values from -0.125 to 0.125
- w_up: bfloat16 [2048, 32, 1024], P('fsdp', 'seq'), may hold values from -0.125 to 0.125
- w_down: bfloat16 [2048, 32, 1024], P('fsdp', 'seq'), may hold values from -0.5 to 0.5
Outputs:
- block_out: bfloat16 [4, 2048, 2048], P('fsdp', 'seq')
- tokens_grad: float32 [4, 2048, 2048], P('fsdp', 'seq')
- attn_gain_grad: float32 [2048], P(('seq', 'fsdp'))
- query_gain_grad: float32 [2048], P(('seq', 'fsdp'))
- key_gain_grad: float32 [2048], P(('seq', 'fsdp'))
- ffn_gain_grad: float32 [2048], P(('seq', 'fsdp'))
- w_query_grad: float32 [2048, 2048], P(('seq', 'fsdp'))
- w_key_grad: float32 [2048, 2048], P(('seq', 'fsdp'))
- w_value_grad: float32 [2048, 2048], P(('seq', 'fsdp'))
- w_out_grad: float32 [2048, 2048], P(('seq', 'fsdp'))
- w_gate_grad: float32 [2048, 32, 1024], P('fsdp', 'seq')
- w_up_grad: float32 [2048, 32, 1024], P('fsdp', 'seq')
- w_down_grad: float32 [2048, 32, 1024], P('fsdp', 'seq')
Inputs may be any that keep to these rules, and one draw needn't show every extreme that they name: `routes`: the 8 experts of a token differ. Among the 256 tokens of one device (aligned blocks in sequence order) no expert is named more than 96 times, and in every draw some expert is named exactly 96 times there.
All inputs are finite; a program needn't handle non-finite values.
Results may differ from a plain program's by a relative error of at most 0.017.
Values may be sent and summed in bfloat16 or wider, within the bound.
A program may use at most 448 MiB of HBM per device.

v0:
```python
import functools
import jax
import jax.numpy as jnp
from jax import lax
from jax.experimental import pallas as pl
from jax.experimental.pallas import tpu as pltpu
from jax.sharding import PartitionSpec as P


MESH = pl.DeviceIdType.MESH
ANY = pl.ANY
H = 16
epsilon = 1e-05


def work(us):
    return pl.CostEstimate(flops=int(us * 6e8), bytes_accessed=0, transcendentals=0)


def greet(peers):
    barrier = pltpu.get_barrier_semaphore()
    for peer in peers:
        pl.semaphore_signal(barrier, inc=1, device_id={"seq": peer}, device_id_type=MESH)
    pl.semaphore_wait(barrier, len(peers))


def push(src, dst, send, recv, peer):
    return pltpu.make_async_remote_copy(
        src_ref=src, dst_ref=dst, send_sem=send, recv_sem=recv,
        device_id={"seq": peer}, device_id_type=MESH)


def gather_kernel(n, pieces, by_index, own, out, send_sem, recv_sem, copy_sem):
    pair = 2
    lines = n // pair
    me = lax.axis_index("seq")
    a, b = me // pair, me % pair
    column = [((a + k) % lines) * pair + b for k in range(1, lines)]
    across = a * pair + (1 - b)
    greet(column + [across])
    rows = own.shape[0] // pieces
    if by_index:
        here = [((a + lines - k) % lines) * pair + b for k in range(lines)]
        there = [((a + lines - k) % lines) * pair + 1 - b for k in range(lines)]
        sent = [me] * lines
        relayed = here
    else:
        here, there = list(range(lines)), list(range(lines, n))
        sent = here
        relayed = there
    local = pltpu.make_async_copy(own, out.at[here[0]], copy_sem)
    local.start()

    def piece(p):
        return pl.ds(p * rows, rows)

    sends = []
    for p in range(pieces):
        for k in range(lines):
            peer = across if k == 0 else column[k - 1]
            place = relayed[0] if k == 0 else sent[k]
            copy = push(own.at[piece(p)], out.at[place, piece(p)], send_sem.at[k, p], recv_sem.at[k, p], peer)
            copy.start()
            sends.append(copy)
    relays = []
    for p in range(pieces):
        for k in range(1, lines):
            push(own.at[piece(p)], out.at[here[k], piece(p)], send_sem.at[k, p], recv_sem.at[k, p], across).wait_recv()
            slot = lines + k - 1
            copy = push(
                out.at[here[k], piece(p)], out.at[relayed[k], piece(p)], send_sem.at[slot, p], recv_sem.at[slot, p], across
            )
            copy.start()
            relays.append(copy)
    for p in range(pieces):
        push(own.at[piece(p)], out.at[there[0], piece(p)], send_sem.at[0, p], recv_sem.at[0, p], across).wait_recv()
    for copy in relays:
        copy.wait_recv()
    for copy in sends + relays:
        copy.wait_send()
    local.wait()


def gather_rows(x, n, pieces, by_index, collective_id):
    slots = n // 2 + n // 2 - 1
    return pl.pallas_call(
        functools.partial(gather_kernel, n, pieces, by_index),
        out_shape=jax.ShapeDtypeStruct((n,) + x.shape, x.dtype),
        in_specs=[pl.BlockSpec(memory_space=pltpu.VMEM)],
        out_specs=pl.BlockSpec(memory_space=ANY),
        scratch_shapes=[
            pltpu.SemaphoreType.DMA((slots, pieces)),
            pltpu.SemaphoreType.DMA((slots, pieces)),
            pltpu.SemaphoreType.DMA,
        ],
        compiler_params=pltpu.CompilerParams(collective_id=collective_id, has_side_effects=True),
        cost_estimate=work(105),
        name="gather_rows",
    )(x)


def reduce_kernel(n, pieces, by_index, part, out, mine, got, sums, landed, send_sem, recv_sem, load_sem):
    pair = 2
    lines = n // pair
    me = lax.axis_index("seq")
    a, b = me // pair, me % pair
    column = [((a + lines - k) % lines) * pair + b for k in range(1, lines)]
    across = a * pair + (1 - b)
    greet(column + [across])
    rows = out.shape[0] // pieces
    order = list(range(1, lines)) + [0]
    if by_index:
        here = [((a + lines - k) % lines) * pair + b for k in range(lines)]
        there = [((a + lines - k) % lines) * pair + 1 - b for k in range(lines)]
    else:
        here, there = list(range(lines)), list(range(lines, n))

    def piece(p):
        return pl.ds(p * rows, rows)

    firsts, loads = {}, {}
    for k in order:
        for p in range(pieces):
            copy = push(part.at[there[k], piece(p)], got.at[k, piece(p)],
                        send_sem.at[k, p], recv_sem.at[k, p], across)
            copy.start()
            firsts[k, p] = copy
            load = pltpu.make_async_copy(part.at[here[k], piece(p)], mine.at[k, piece(p)], load_sem.at[k, p])
            load.start()
            loads[k, p] = load
    seconds = {}
    for k in order:
        for p in range(pieces):
            firsts[k, p].wait_recv()
            loads[k, p].wait()
            total = mine[k, piece(p)].astype(jnp.float32) + got[k, piece(p)].astype(jnp.float32)
            if k:
                sums[k - 1, piece(p)] = total.astype(jnp.bfloat16)
                slot = lines + k - 1
                copy = push(sums.at[k - 1, piece(p)], landed.at[k - 1, piece(p)],
                            send_sem.at[slot, p], recv_sem.at[slot, p], column[k - 1])
                copy.start()
                seconds[k, p] = copy
            else:
                for j in range(1, lines):
                    seconds[j, p].wait_recv()
                    total += landed[j - 1, piece(p)].astype(jnp.float32)
                out[piece(p), :] = total
    for copy in list(firsts.values()) + list(seconds.values()):
        copy.wait_send()


def reduce_rows(part, n, pieces, by_index, collective_id):
    _, rows, width = part.shape
    lines = n // 2
    slots = lines + lines - 1
    return pl.pallas_call(
        functools.partial(reduce_kernel, n, pieces, by_index),
        out_shape=jax.ShapeDtypeStruct((rows, width), jnp.float32),
        in_specs=[pl.BlockSpec(memory_space=ANY)],
        out_specs=pl.BlockSpec(memory_space=pltpu.VMEM),
        scratch_shapes=[
            pltpu.VMEM((lines, rows, width), jnp.bfloat16),
            pltpu.VMEM((lines, rows, width), jnp.bfloat16),
            pltpu.VMEM((lines - 1, rows, width), jnp.bfloat16),
            pltpu.VMEM((lines - 1, rows, width), jnp.bfloat16),
            pltpu.SemaphoreType.DMA((slots, pieces)),
            pltpu.SemaphoreType.DMA((slots, pieces)),
            pltpu.SemaphoreType.DMA((lines, pieces)),
        ],
        compiler_params=pltpu.CompilerParams(collective_id=collective_id, has_side_effects=True),
        cost_estimate=work(98),
        name="reduce_rows",
    )(part)


def reduce_terms_kernel(
    n, pieces, tile, part, x, first, second, out, first_term, second_term,
    mine, got, sums, landed, x_buf, g_buf, o_buf, send_sem, recv_sem, load_sem, x_sem, g_sem, o_sem
):
    pair = 2
    lines = n // pair
    me = lax.axis_index("seq")
    a, b = me // pair, me % pair
    across = a * pair + (1 - b)
    greet([((a + lines - k) % lines) * pair + b for k in range(1, lines)] + [across])
    rows = out.shape[0] // pieces
    experts, _, width = x.shape
    tiles = width // tile
    jobs = experts * tiles
    terms = (first_term, second_term)

    def piece(p):
        return pl.ds(pl.multiple_of(p * rows, rows), rows)

    def first_copy(k, p):
        return push(part.at[lines + k, piece(p)], got.at[k, piece(p)], send_sem.at[k, p], recv_sem.at[k, p], across)

    def load(k, p):
        return pltpu.make_async_copy(part.at[k, piece(p)], mine.at[k, piece(p)], load_sem.at[k, p])

    def second_copy(k, p):
        peer = ((a + lines - k) % lines) * pair + b
        slot = lines + k - 1
        return push(sums.at[k - 1, piece(p)], landed.at[k - 1, piece(p)], send_sem.at[slot, p], recv_sem.at[slot, p], peer)

    def x_copy(j):
        cols = pl.ds(pl.multiple_of(j % tiles * tile, tile), tile)
        return pltpu.make_async_copy(x.at[j // tiles, :, cols], x_buf.at[j % 2], x_sem.at[j % 2])

    def g_copies(e):
        return [
            pltpu.make_async_copy(g.at[e], g_buf.at[e % 2, i], g_sem.at[e % 2, i]) for i, g in enumerate((first, second))
        ]

    def o_copies(j):
        place = pl.ds(pl.multiple_of(j % tiles * tile, tile), tile)
        return [
            pltpu.make_async_copy(o_buf.at[j % 2, i], o.at[j // tiles, place, :], o_sem.at[j % 2, i])
            for i, o in enumerate(terms)
        ]

    for k in list(range(1, lines)) + [0]:
        for p in range(pieces):
            first_copy(k, p).start()
            load(k, p).start()
    x_copy(0).start()
    for copy in g_copies(0):
        copy.start()

    def add(k, p):
        first_copy(k, p).wait_recv()
        load(k, p).wait()
        return mine[k, piece(p)].astype(jnp.float32) + got[k, piece(p)].astype(jnp.float32)

    def step(s):
        k, p = 1 + s // pieces, s % pieces
        sums[k - 1, piece(p)] = add(k, p).astype(jnp.bfloat16)
        second_copy(k, p).start()

    def job(j):
        @pl.when(j + 1 < jobs)
        def _():
            x_copy(j + 1).start()

        @pl.when(j % tiles == 0)
        def _():
            for copy in g_copies(j // tiles):
                copy.wait()

            @pl.when(j // tiles + 1 < experts)
            def _():
                for copy in g_copies(j // tiles + 1):
                    copy.start()

        @pl.when(j >= 2)
        def _():
            for copy in o_copies(j - 2):
                copy.wait()

        x_copy(j).wait()
        for i in range(2):
            o_buf[j % 2, i] = down_rows(x_buf[j % 2], g_buf[j // tiles % 2, i]).astype(jnp.bfloat16)
        for copy in o_copies(j):
            copy.start()

    steps = (lines - 1) * pieces
    per = steps * 2 // jobs

    def both(t, _):
        for i in range(per):
            step(t * per + i)
            if i == 0:
                job(2 * t)
            if i == per - 1:
                job(2 * t + 1)
        return 0

    lax.fori_loop(0, jobs // 2, both, 0)
    for copy in o_copies(jobs - 2) + o_copies(jobs - 1):
        copy.wait()

    def finish(p, _):
        total = add(0, p)
        for k in range(1, lines):
            second_copy(k, p).wait_recv()
            total += landed[k - 1, piece(p)].astype(jnp.float32)
        out[piece(p), :] = total
        return 0

    lax.fori_loop(0, pieces, finish, 0)
    for p in range(pieces):
        for k in range(lines):
            first_copy(k, p).wait_send()
        for k in range(1, lines):
            second_copy(k, p).wait_send()


def reduce_terms(part, x, first, second, n, pieces, tile, collective_id):
    _, rows, width = part.shape
    experts, tokens, _ = x.shape
    hidden = first.shape[2]
    lines = n // 2
    slots = lines + lines - 1
    hbm = pl.BlockSpec(memory_space=ANY)
    term = jax.ShapeDtypeStruct((experts, width, hidden), jnp.bfloat16)
    return pl.pallas_call(
        functools.partial(reduce_terms_kernel, n, pieces, tile),
        out_shape=(jax.ShapeDtypeStruct((rows, width), jnp.float32), term, term),
        in_specs=[hbm] * 4,
        out_specs=[pl.BlockSpec(memory_space=pltpu.VMEM), hbm, hbm],
        scratch_shapes=[
            pltpu.VMEM((lines, rows, width), jnp.bfloat16),
            pltpu.VMEM((lines, rows, width), jnp.bfloat16),
            pltpu.VMEM((lines - 1, rows, width), jnp.bfloat16),
            pltpu.VMEM((lines - 1, rows, width), jnp.bfloat16),
            pltpu.VMEM((2, tokens, tile), jnp.bfloat16),
            pltpu.VMEM((2, 2, tokens, hidden), jnp.bfloat16),
            pltpu.VMEM((2, 2, tile, hidden), jnp.bfloat16),
            pltpu.SemaphoreType.DMA((slots, pieces)),
            pltpu.SemaphoreType.DMA((slots, pieces)),
            pltpu.SemaphoreType.DMA((lines, pieces)),
            pltpu.SemaphoreType.DMA((2,)),
            pltpu.SemaphoreType.DMA((2, 2)),
            pltpu.SemaphoreType.DMA((2, 2)),
        ],
        compiler_params=pltpu.CompilerParams(
            collective_id=collective_id, has_side_effects=True, vmem_limit_bytes=50 << 20
        ),
        cost_estimate=work(105),
        name="reduce_terms",
    )(part, x, first, second)


def gains_kernel(n, groups, sent, own, out, taken, summed, landed, send_sem, recv_sem, side_send, side_recv):
    me, group = lax.axis_index("seq"), lax.axis_index("fsdp")
    barrier = pltpu.get_barrier_semaphore()
    peers = [(me + k) % n for k in range(1, n)]
    mates = [(group + k) % groups for k in range(1, groups)]
    for peer in peers:
        pl.semaphore_signal(barrier, inc=1, device_id={"seq": peer}, device_id_type=MESH)
    for mate in mates:
        pl.semaphore_signal(barrier, inc=1, device_id={"fsdp": mate}, device_id_type=MESH)
    pl.semaphore_wait(barrier, n - 1 + groups - 1)
    copies = []
    for k in range(1, n):
        copy = push(sent.at[peers[k - 1]], taken.at[k - 1], send_sem.at[k - 1], recv_sem.at[k - 1], peers[k - 1])
        copy.start()
        copies.append(copy)
    total = sent[me] + own[...]
    for k in range(1, n):
        copies[k - 1].wait_recv()
        total = total + taken[k - 1]
    summed[...] = total
    sides = []
    for k in range(1, groups):
        side = pltpu.make_async_remote_copy(
            src_ref=summed, dst_ref=landed.at[k - 1], send_sem=side_send.at[k - 1], recv_sem=side_recv.at[k - 1],
            device_id={"fsdp": mates[k - 1]}, device_id_type=MESH)
        side.start()
        sides.append(side)
    for k in range(1, groups):
        sides[k - 1].wait_recv()
        total = total + landed[k - 1]
    out[...] = total
    for copy in copies + sides:
        copy.wait_send()


def sum_gains(sent, own, n, groups, collective_id):
    shape = own.shape
    return pl.pallas_call(
        functools.partial(gains_kernel, n, groups),
        out_shape=jax.ShapeDtypeStruct(shape, own.dtype),
        in_specs=[pl.BlockSpec(memory_space=pltpu.VMEM)] * 2,
        out_specs=pl.BlockSpec(memory_space=pltpu.VMEM),
        scratch_shapes=[
            pltpu.VMEM((n - 1,) + shape, own.dtype),
            pltpu.VMEM(shape, own.dtype),
            pltpu.VMEM((groups - 1,) + shape, own.dtype),
            pltpu.SemaphoreType.DMA((n - 1,)),
            pltpu.SemaphoreType.DMA((n - 1,)),
            pltpu.SemaphoreType.DMA((groups - 1,)),
            pltpu.SemaphoreType.DMA((groups - 1,)),
        ],
        compiler_params=pltpu.CompilerParams(collective_id=collective_id, has_side_effects=True),
        cost_estimate=work(10),
        name="sum_gains",
    )(sent, own)


def widen_kernel(x_ref, o_ref):
    for e in range(x_ref.shape[0]):
        o_ref[:, e, :] = x_ref[e].astype(jnp.float32)


def widen(x):
    experts, rows, columns = x.shape
    step = min(128, rows)
    return pl.pallas_call(
        widen_kernel,
        grid=(rows // step,),
        out_shape=jax.ShapeDtypeStruct((rows, experts, columns), jnp.float32),
        in_specs=[pl.BlockSpec((experts, step, columns), lambda i: (0, i, 0))],
        out_specs=pl.BlockSpec((step, experts, columns), lambda i: (i, 0, 0)),
        cost_estimate=work(5),
        name="widen",
    )(x)


def masked(block):
    keys = lax.broadcasted_iota(jnp.int32, (block, block), 0)
    rows = lax.broadcasted_iota(jnp.int32, (block, block), 1)
    return keys <= rows


def across_lanes(a, b):
    return lax.dot_general(a, b, (((1,), (1,)), ((), ())), preferred_element_type=jnp.float32)


def down_rows(a, b):
    return lax.dot_general(a, b, (((0,), (0,)), ((), ())), preferred_element_type=jnp.float32)


LOG2E = 1.4426950408889634


def attend_kernel(block, scale, q_ref, k_ref, v_ref, o_ref, lse_ref, s_ref, acc_ref):
    length, _ = q_ref.shape

    def rows(i):
        return pl.ds(pl.multiple_of(i * block, block), block)

    def one_block(i, _):
        q = q_ref[rows(i), :]
        diag = across_lanes(k_ref[rows(i), :], q) * (scale * LOG2E)
        diag = jnp.where(masked(block), diag, -1e30)
        s_ref[rows(i), :] = diag
        peak = jnp.max(diag, axis=0, keepdims=True)

        def score(j, peak):
            s = across_lanes(k_ref[rows(j), :], q) * (scale * LOG2E)
            s_ref[rows(j), :] = s
            return jnp.maximum(peak, jnp.max(s, axis=0, keepdims=True))

        peak = lax.fori_loop(0, i, score, peak)
        acc_ref[...] = jnp.zeros_like(acc_ref)

        def weigh(j, total):
            p = jnp.exp2(s_ref[rows(j), :] - peak)
            acc_ref[...] += down_rows(v_ref[rows(j), :], p.astype(jnp.bfloat16))
            return total + jnp.sum(p, axis=0, keepdims=True)

        total = lax.fori_loop(0, i + 1, weigh, jnp.zeros_like(peak))
        o_ref[rows(i), :] = (acc_ref[...] / total).T.astype(o_ref.dtype)
        lse_ref[0, :, rows(i)] = peak + jnp.log2(total)
        return 0

    lax.fori_loop(0, length // block, one_block, 0)


def attend(q, k, v, heads, block, scale):
    length, width = q.shape
    dim = width // heads
    spec = pl.BlockSpec((length, dim), lambda h: (0, h))
    return pl.pallas_call(
        functools.partial(attend_kernel, block, scale),
        grid=(heads,),
        out_shape=(
            jax.ShapeDtypeStruct(q.shape, q.dtype),
            jax.ShapeDtypeStruct((heads, 1, length), jnp.float32),
        ),
        in_specs=[spec] * 3,
        out_specs=[spec, pl.BlockSpec((1, 1, length), lambda h: (h, 0, 0))],
        scratch_shapes=[
            pltpu.VMEM((length, block), jnp.float32),
            pltpu.VMEM((dim, block), jnp.float32),
        ],
        cost_estimate=work(25),
        name="attend",
    )(q, k, v)


def attend_back_kernel(
    block, scale, q_ref, k_ref, v_ref, g_ref, o_ref, lse_ref, dq_ref, dk_ref, dv_ref, dk_acc, dv_acc, dq_acc
):
    length, dim = q_ref.shape
    dk_acc[...] = jnp.zeros_like(dk_acc)
    dv_acc[...] = jnp.zeros_like(dv_acc)

    def rows(i):
        return pl.ds(pl.multiple_of(i * block, block), block)

    def one_block(i, _):
        q, g = q_ref[rows(i), :], g_ref[rows(i), :]
        lse = lse_ref[0, :, rows(i)]
        products = g.astype(jnp.float32) * o_ref[rows(i), :].astype(jnp.float32)
        shift = lax.dot_general(
            jnp.ones((8, dim), jnp.float32), products, (((1,), (1,)), ((), ())),
            precision=lax.Precision.HIGHEST, preferred_element_type=jnp.float32,
        )[:1]

        def pair(j, keep):
            k, v = k_ref[rows(j), :], v_ref[rows(j), :]
            p = jnp.exp2(across_lanes(k, q) * (scale * LOG2E) - lse)
            if keep is not None:
                p = jnp.where(keep, p, 0.0)
            ds = (p * (across_lanes(v, g) - shift) * scale).astype(jnp.bfloat16)
            dv_acc[rows(j), :] += jnp.dot(p.astype(jnp.bfloat16), g, preferred_element_type=jnp.float32)
            dk_acc[rows(j), :] += jnp.dot(ds, q, preferred_element_type=jnp.float32)
            dq_acc[...] += down_rows(k, ds)

        dq_acc[...] = jnp.zeros_like(dq_acc)
        pair(i, masked(block))

        def body(j, _):
            pair(j, None)
            return 0

        lax.fori_loop(0, i, body, 0)
        dq_ref[rows(i), :] = dq_acc[...].T.astype(dq_ref.dtype)
        return 0

    lax.fori_loop(0, length // block, one_block, 0)
    dk_ref[...] = dk_acc[...].astype(dk_ref.dtype)
    dv_ref[...] = dv_acc[...].astype(dv_ref.dtype)


def attend_back(q, k, v, g, o, lse, heads, block, scale):
    length, width = q.shape
    dim = width // heads
    spec = pl.BlockSpec((length, dim), lambda h: (0, h))
    return pl.pallas_call(
        functools.partial(attend_back_kernel, block, scale),
        grid=(heads,),
        out_shape=(jax.ShapeDtypeStruct(q.shape, q.dtype),) * 3,
        in_specs=[spec] * 5 + [pl.BlockSpec((1, 1, length), lambda h: (h, 0, 0))],
        out_specs=[spec] * 3,
        scratch_shapes=[
            pltpu.VMEM((length, dim), jnp.float32),
            pltpu.VMEM((length, dim), jnp.float32),
            pltpu.VMEM((dim, block), jnp.float32),
        ],
        cost_estimate=work(60),
        name="attend_back",
    )(q, k, v, g, o, lse)


def project_kernel(
    n, groups, pieces, own, w_query, w_key, w_value, gain_own,
    normed, proj, squares, w_ref, gains, held, send_sem, recv_sem, side_send, side_recv, copy_sem
):
    pair = 2
    lines = n // pair
    me, group = lax.axis_index("seq"), lax.axis_index("fsdp")
    a, b = me // pair, me % pair
    column = [((a + k) % lines) * pair + b for k in range(1, lines)]
    back = [((a + lines - k) % lines) * pair + b for k in range(1, lines)]
    across = a * pair + (1 - b)
    mates = [(group + k) % groups for k in range(1, groups)]
    barrier = pltpu.get_barrier_semaphore()
    for peer in column + [across]:
        pl.semaphore_signal(barrier, inc=1, device_id={"seq": peer}, device_id_type=MESH)
    for mate in mates:
        pl.semaphore_signal(barrier, inc=1, device_id={"fsdp": mate}, device_id_type=MESH)
    pl.semaphore_wait(barrier, lines + groups - 1)
    rows, _ = own.shape
    step = rows // pieces
    span = w_ref.shape[1] // 3
    shard = w_query.shape[0]

    def piece(p):
        return pl.ds(p * step, step)

    sends = []
    for p in range(pieces):
        for k in range(lines):
            peer = across if k == 0 else column[k - 1]
            copy = push(own.at[piece(p)], held.at[me, piece(p)], send_sem.at[k, p], recv_sem.at[k, p], peer)
            copy.start()
            sends.append(copy)

    shard_rows = pl.ds(pl.multiple_of(group * shard, shard), shard)
    mine = pl.ds(pl.multiple_of(me * span, span), span)
    blocks = [
        (w.at[:, mine], w_ref.at[shard_rows, part * span : (part + 1) * span])
        for part, w in enumerate((w_query, w_key, w_value))
    ]
    blocks.append((gain_own, gains.at[:, shard_rows]))
    locals_, sides = [], []
    for i, (src, dst) in enumerate(blocks):
        for k in range(1, groups):
            side = pltpu.make_async_remote_copy(
                src_ref=src, dst_ref=dst, send_sem=side_send.at[i, k - 1], recv_sem=side_recv.at[i, k - 1],
                device_id={"fsdp": mates[k - 1]}, device_id_type=MESH)
            side.start()
            sides.append(side)
        local = pltpu.make_async_copy(src, dst, copy_sem.at[i])
        local.start()
        locals_.append(local)

    def project(src, chunk):
        x = chunk[...].astype(jnp.float32)
        factor = lax.rsqrt(jnp.mean(x * x, axis=-1, keepdims=True) + epsilon)
        place = pl.ds(pl.multiple_of(src * rows, rows), rows)
        normed[place, :] = (x * factor * gains[0:1, :]).astype(jnp.bfloat16)
        for part in range(3):
            cols = slice(part * span, (part + 1) * span)
            out = jnp.dot(normed[place, :], w_ref[:, cols], preferred_element_type=jnp.float32)
            proj[place, cols] = out
            if part < 2:
                sums = lax.dot_general(
                    jnp.ones((8, span), jnp.float32), out * out, (((1,), (1,)), ((), ())),
                    precision=lax.Precision.HIGHEST, preferred_element_type=jnp.float32,
                )
                squares[pl.ds(part * n + src, 1), :] = sums[:1]

    relays = []
    for p in range(pieces):
        for k in range(1, lines):
            src = back[k - 1]
            push(own.at[piece(p)], held.at[src, piece(p)], send_sem.at[k, p], recv_sem.at[k, p], across).wait_recv()
            slot = lines + k - 1
            copy = push(held.at[src, piece(p)], held.at[src, piece(p)], send_sem.at[slot, p], recv_sem.at[slot, p], across)
            copy.start()
            relays.append(copy)
    for copy in locals_:
        copy.wait()
    for side in sides:
        side.wait_recv()
    project(me, own)
    for p in range(pieces):
        push(own.at[piece(p)], held.at[across, piece(p)], send_sem.at[0, p], recv_sem.at[0, p], across).wait_recv()
    project(across, held.at[across])
    for k in range(1, lines):
        project(back[k - 1], held.at[back[k - 1]])
    for k in range(1, lines):
        for p in range(pieces):
            relays[p * (lines - 1) + k - 1].wait_recv()
        src = ((a + lines - k) % lines) * pair + 1 - b
        project(src, held.at[src])
    for copy in sends + relays + sides:
        copy.wait_send()


def project_rows(x, w_query, w_key, w_value, gains, n, groups, pieces, collective_id):
    rows, width = x.shape
    span = w_query.shape[1] // n
    slots = n // 2 + n // 2 - 1
    vmem = pl.BlockSpec(memory_space=pltpu.VMEM)
    hbm = pl.BlockSpec(memory_space=ANY)
    return pl.pallas_call(
        functools.partial(project_kernel, n, groups, pieces),
        out_shape=(
            jax.ShapeDtypeStruct((n * rows, width), jnp.bfloat16),
            jax.ShapeDtypeStruct((n * rows, 3 * span), jnp.float32),
            jax.ShapeDtypeStruct((2 * n, rows), jnp.float32),
            jax.ShapeDtypeStruct((width, 3 * span), jnp.bfloat16),
            jax.ShapeDtypeStruct((8, width), jnp.float32),
        ),
        in_specs=[vmem, hbm, hbm, hbm, vmem],
        out_specs=[vmem] * 5,
        scratch_shapes=[
            pltpu.VMEM((n, rows, width), jnp.bfloat16),
            pltpu.SemaphoreType.DMA((slots, pieces)),
            pltpu.SemaphoreType.DMA((slots, pieces)),
            pltpu.SemaphoreType.DMA((4, groups - 1)),
            pltpu.SemaphoreType.DMA((4, groups - 1)),
            pltpu.SemaphoreType.DMA((4,)),
        ],
        compiler_params=pltpu.CompilerParams(
            collective_id=collective_id, has_side_effects=True, vmem_limit_bytes=50 << 20
        ),
        cost_estimate=work(110),
        name="project_rows",
    )(x, w_query, w_key, w_value, gains)


def as_columns(row, lanes):
    return jnp.broadcast_to(row, (lanes, row.shape[1])).T


def turn_tables(c, near_cos, near_sin, far_cos, far_sin):
    far_c, far_s = far_cos[pl.ds(c, 1), :], far_sin[pl.ds(c, 1), :]
    cosine = near_cos[...] * far_c - near_sin[...] * far_s
    sine = near_sin[...] * far_c + near_cos[...] * far_s
    first = lax.broadcasted_iota(jnp.int32, sine.shape, 1) < sine.shape[1] // 2
    return cosine, jnp.where(first, -sine, sine)


def add_over_seq(n, own, landed, send_sem, recv_sem, peers):
    copies = []
    for k in range(1, n):
        copy = push(own, landed.at[k - 1], send_sem.at[k - 1], recv_sem.at[k - 1], peers[k - 1])
        copy.start()
        copies.append(copy)
    return copies


def rotate_kernel(
    n, full, squares, sent, proj, gains, near_cos, near_sin, far_cos, far_sin,
    queries, keys, values, factors, taken, landed, send_sem, recv_sem, copy_sem
):
    me = lax.axis_index("seq")
    peers = [(me + k) % n for k in range(1, n)]
    greet(peers)
    local = pltpu.make_async_copy(sent.at[me], taken.at[me], copy_sem)
    local.start()
    copies = add_over_seq(n, squares, landed, send_sem.at[0], recv_sem.at[0], peers)
    swaps = []
    for k in range(1, n):
        swap = push(sent.at[peers[k - 1]], taken.at[me], send_sem.at[1, k - 1], recv_sem.at[1, k - 1], peers[k - 1])
        swap.start()
        swaps.append(swap)
    span = queries.shape[1]
    rows = squares.shape[1]
    lanes = near_cos.shape[1]
    total = squares[...]
    for k in range(1, n):
        copies[k - 1].wait_recv()
        total = total + landed[k - 1]
    factors[...] = lax.rsqrt(total / full + epsilon)

    def chunk(c, _):
        place = pl.ds(pl.multiple_of(c * rows, rows), rows)
        cosine, sine = turn_tables(c, near_cos, near_sin, far_cos, far_sin)
        for part, out in ((0, queries), (1, keys)):
            factor = as_columns(factors[pl.ds(part * n + c, 1), :], lanes)
            for h in range(span // lanes):
                cols = slice(part * span + h * lanes, part * span + (h + 1) * lanes)
                x = proj[place, cols] * factor * gains[part : part + 1, h * lanes : (h + 1) * lanes]
                turned = x * cosine + pltpu.roll(x, lanes // 2, 1) * sine
                out[place, h * lanes : (h + 1) * lanes] = turned.astype(jnp.bfloat16)
        values[place, :] = proj[place, 2 * span :].astype(jnp.bfloat16)
        return 0

    lax.fori_loop(0, n, chunk, 0)
    for copy in copies:
        copy.wait_send()
    for swap in swaps:
        swap.wait()
    local.wait()


def rotate_rows(squares, sent, proj, gains, tables, n, full, collective_id):
    length, outs = proj.shape
    span = outs // 3
    vmem = pl.BlockSpec(memory_space=pltpu.VMEM)
    heads = jax.ShapeDtypeStruct((length, span), jnp.bfloat16)
    return pl.pallas_call(
        functools.partial(rotate_kernel, n, full),
        out_shape=(
            heads, heads, heads,
            jax.ShapeDtypeStruct(squares.shape, jnp.float32),
            jax.ShapeDtypeStruct(sent.shape, sent.dtype),
        ),
        in_specs=[vmem] * 8,
        out_specs=[vmem] * 5,
        scratch_shapes=[
            pltpu.VMEM((n - 1,) + squares.shape, jnp.float32),
            pltpu.SemaphoreType.DMA((2, n - 1)),
            pltpu.SemaphoreType.DMA((2, n - 1)),
            pltpu.SemaphoreType.DMA,
        ],
        compiler_params=pltpu.CompilerParams(
            collective_id=collective_id, has_side_effects=True, vmem_limit_bytes=40 << 20
        ),
        cost_estimate=work(15),
        name="rotate_rows",
    )(squares, sent, proj, gains, *tables)


def heads_back_kernel(
    n, full, dq, dk, dv, proj, factors, gains, near_cos, near_sin, far_cos, far_sin,
    grads, gain_grads, sums, landed, send_sem, recv_sem
):
    me = lax.axis_index("seq")
    peers = [(me + k) % n for k in range(1, n)]
    greet(peers)
    span = dq.shape[1]
    rows = sums.shape[1]
    lanes = near_cos.shape[1]
    count = span // lanes

    def parts(c, part, h, grad):
        place = pl.ds(pl.multiple_of(c * rows, rows), rows)
        cosine, sine = turn_tables(c, near_cos, near_sin, far_cos, far_sin)
        g = grad[place, h * lanes : (h + 1) * lanes].astype(jnp.float32)
        up = g * cosine + pltpu.roll(g * sine, lanes // 2, 1)
        factor = as_columns(factors[pl.ds(part * n + c, 1), :], lanes)
        cols = slice(part * span + h * lanes, part * span + (h + 1) * lanes)
        normal = proj[place, cols] * factor
        weighted = up * gains[part : part + 1, h * lanes : (h + 1) * lanes]
        return place, cols, up, factor, normal, weighted

    def first(c, _):
        for part, grad in ((0, dq), (1, dk)):
            products = 0.0
            for h in range(count):
                _, _, _, _, normal, weighted = parts(c, part, h, grad)
                products = products + weighted * normal
            total = lax.dot_general(
                jnp.ones((8, lanes), jnp.float32), products, (((1,), (1,)), ((), ())),
                precision=lax.Precision.HIGHEST, preferred_element_type=jnp.float32,
            )
            sums[pl.ds(part * n + c, 1), :] = total[:1]
        return 0

    lax.fori_loop(0, n, first, 0)
    copies = add_over_seq(n, sums, landed, send_sem, recv_sem, peers)
    gain_grads[...] = jnp.zeros_like(gain_grads)

    def gain_sum(c, _):
        for part, grad in ((0, dq), (1, dk)):
            for h in range(count):
                _, _, up, _, normal, _ = parts(c, part, h, grad)
                cell = (slice(part + 2, part + 3), slice(h * lanes, (h + 1) * lanes))
                gain_grads[cell] += jnp.sum(up * normal, axis=0, keepdims=True)
        place = pl.ds(pl.multiple_of(c * rows, rows), rows)
        grads[place, 2 * span :] = dv[place, :]
        return 0

    lax.fori_loop(0, n, gain_sum, 0)
    total = sums[...]
    for k in range(1, n):
        copies[k - 1].wait_recv()
        total = total + landed[k - 1]
    landed[0] = total / full

    def last(c, _):
        for part, grad in ((0, dq), (1, dk)):
            mean = as_columns(landed[0, pl.ds(part * n + c, 1), :], lanes)
            for h in range(count):
                place, cols, _, factor, normal, weighted = parts(c, part, h, grad)
                grads[place, cols] = (factor * (weighted - normal * mean)).astype(jnp.bfloat16)
        return 0

    lax.fori_loop(0, n, last, 0)
    for copy in copies:
        copy.wait_send()


def heads_back(dq, dk, dv, proj, factors, gains, tables, n, full, collective_id):
    length, span = dq.shape
    vmem = pl.BlockSpec(memory_space=pltpu.VMEM)
    return pl.pallas_call(
        functools.partial(heads_back_kernel, n, full),
        out_shape=(
            jax.ShapeDtypeStruct((length, 3 * span), jnp.bfloat16),
            jax.ShapeDtypeStruct((8, span), jnp.float32),
        ),
        in_specs=[vmem] * 10,
        out_specs=[vmem] * 2,
        scratch_shapes=[
            pltpu.VMEM(factors.shape, jnp.float32),
            pltpu.VMEM((n - 1,) + factors.shape, jnp.float32),
            pltpu.SemaphoreType.DMA((n - 1,)),
            pltpu.SemaphoreType.DMA((n - 1,)),
        ],
        compiler_params=pltpu.CompilerParams(
            collective_id=collective_id, has_side_effects=True, vmem_limit_bytes=40 << 20
        ),
        cost_estimate=work(20),
        name="heads_back",
    )(dq, dk, dv, proj, factors, gains, *tables)


def turn_parts(rows, n, dim):
    half = dim // 2
    frequency = jnp.power(10000.0, -2.0 * jnp.arange(half, dtype=jnp.float32) / dim)
    frequency = jnp.concatenate([frequency, frequency])[None]
    near = jnp.arange(rows, dtype=jnp.float32)[:, None] * frequency
    far = (rows * jnp.arange(n)).astype(jnp.float32)[:, None] * frequency
    return jnp.cos(near), jnp.sin(near), jnp.cos(far), jnp.sin(far)


def inverse_norm(values):
    return lax.rsqrt(jnp.mean(values * values, axis=-1, keepdims=True) + epsilon)


def norm_backward(values, factor, gain, upstream):
    normal = values * factor
    weighted = upstream * gain
    gain_term = jnp.sum(upstream * normal, axis=0)
    back = factor * (weighted - normal * jnp.mean(weighted * normal, axis=-1, keepdims=True))
    return (back, gain_term)


def across_pairs(lines, pair):
    return [(a * pair + b, a * pair + 1 - b) for a in range(lines) for b in range(pair)]


def along_lines(lines, pair, k):
    return [(a * pair + b, (a + k) % lines * pair + b) for a in range(lines) for b in range(pair)]


def by_place(v, n):
    lines = n // 2
    me = lax.axis_index("seq")
    a, b = me // 2, me % 2
    column = [((a + lines - k) % lines) * 2 for k in range(lines)]
    order = jnp.stack([c + b for c in column] + [c + 1 - b for c in column])
    return v[order]


def gather_column(x, n):
    lines = n // 2
    return [lax.ppermute(x, "seq", along_lines(lines, 2, k)) for k in range(1, lines)]


def gather_across(column, n):
    return [lax.ppermute(c, "seq", across_pairs(n // 2, 2)) for c in column]


def reduce_column(v, k, n):
    return lax.ppermute(v, "seq", along_lines(n // 2, 2, n // 2 - k))


def local(
    tokens, routes, route_weights, cotangent, attn_gain, query_gain, key_gain, ffn_gain,
    w_query, w_key, w_value, w_out, w_gate, w_up, w_down,
):
    n = lax.axis_size("seq")
    groups = lax.axis_size("fsdp")
    me = lax.axis_index("seq")
    width = tokens.shape[-1]
    own_tokens = tokens.reshape(-1, width)
    rows = own_tokens.shape[0]
    length = rows * n
    picks = routes.shape[-1]
    local_experts = w_gate.shape[1]
    experts = local_experts * n
    capacity = 3 * rows * picks // (2 * experts)
    head_dim = width // H
    heads = H // n
    span = heads * head_dim
    part = width // (n * groups)
    scale = head_dim ** (-0.5)
    bf, f32 = jnp.bfloat16, jnp.float32
    barrier = lax.optimization_barrier

    own_gains = jnp.stack([attn_gain, query_gain, key_gain, ffn_gain]).astype(f32)
    own_gains = jnp.pad(own_gains, ((0, 4), (0, 0)))
    full_out = lax.all_gather(w_out, "fsdp", axis=0, tiled=True)
    by_expert = lambda w: lax.all_gather(jnp.swapaxes(w, 0, 1), "fsdp", axis=1, tiled=True)
    full_gate = by_expert(w_gate)
    normed, proj, squares, w_heads, gains = project_rows(
        own_tokens, w_query, w_key, w_value, own_gains, n, groups, 8, 0
    )
    w_up, w_down, squares = barrier((w_up, w_down, squares))
    full_up, full_down = by_expert(w_up), by_expert(w_down)
    gain_attn, gain_ffn = gains[0], gains[3]
    head_gains = lax.dynamic_slice(gains, (1, me * span), (2, span))

    expert_ids = jnp.arange(experts, dtype=jnp.int32)
    named = routes.reshape(rows, picks)[None] == expert_ids[:, None, None]
    mixing = route_weights.reshape(rows, picks)[None]
    sent = jnp.sum(jnp.where(named, mixing, 0.0), axis=-1).reshape(n, local_experts, rows)
    tables = turn_parts(rows, n, head_dim)
    queries, keys, values, factors, weights = rotate_rows(
        squares, sent, proj, head_gains, tables, n, width, 1
    )
    block = min(512, length)
    heads_out, log_totals = attend(queries, keys, values, heads, block, scale)
    context = lax.all_to_all(heads_out, "seq", split_axis=0, concat_axis=1, tiled=True)
    inputs = own_tokens.astype(f32)
    mid = inputs + jnp.dot(context, full_out, preferred_element_type=f32)
    norm_two = inverse_norm(mid)
    ffn_in = (mid * norm_two * gain_ffn).astype(bf)

    ffn_all = gather_rows(ffn_in, n, 8, False, 2)
    cot_own, ffn_all = barrier((cotangent.reshape(rows, width), ffn_all))
    half = rows // 2
    cot_halves = [cot_own[:half], cot_own[half:]]
    cot_columns = [gather_column(v, n) for v in cot_halves]
    cot_others = [gather_across([v], n) for v in cot_halves]
    weights = by_place(weights, n)
    taken = weights > 0
    tri = (jnp.arange(rows)[:, None] <= jnp.arange(rows)[None, :]).astype(bf)
    rank = jnp.einsum("cet,tu->ceu", taken.astype(bf), tri, preferred_element_type=f32) - 1.0
    slot_ids = jnp.arange(capacity, dtype=f32)
    hit = (rank[:, :, None, :] == slot_ids[None, None, :, None]) & taken[:, :, None, :]
    place = hit.astype(bf)
    slot_weight = jnp.sum(jnp.where(hit, weights[:, :, None, :], 0.0), axis=-1)
    slot_weight = jnp.swapaxes(slot_weight, 0, 1)[..., None]
    place_rows = lambda v: jnp.einsum("cert,ctd->ecrd", place, v, preferred_element_type=f32)
    unplace = lambda v: jnp.einsum("cert,ecrd->ctd", place, v, preferred_element_type=f32).astype(bf)
    received = place_rows(ffn_all).astype(bf)
    gate = jnp.einsum("ecrd,edf->ecrf", received, full_gate, preferred_element_type=f32)
    received, gate, cot_columns[0] = barrier((received, gate, cot_columns[0]))
    cot_others[0] += gather_across(cot_columns[0], n)
    up_part = jnp.einsum("ecrd,edf->ecrf", received, full_up, preferred_element_type=f32)
    sigmoid_gate = jax.nn.sigmoid(gate)
    activated = gate * sigmoid_gate
    hidden = (activated * up_part).astype(bf)
    expert_out = jnp.einsum("ecrf,edf->ecrd", hidden, full_down, preferred_element_type=f32)
    expert_out = (expert_out * slot_weight).astype(bf)
    expert_out, cot_columns[1], cot_others[0] = barrier((expert_out, cot_columns[1], cot_others[0]))
    cot_others[1] += gather_across(cot_columns[1], n)
    ffn_part = unplace(expert_out)
    ffn_part, cot_others = barrier((ffn_part, cot_others))
    cot_all = jnp.stack(
        [jnp.concatenate(v) for v in zip(*(([h] + c + o) for h, c, o in zip(cot_halves, cot_columns, cot_others)))]
    )
    lines = n // 2
    ffn_got = {k: gather_across([ffn_part[lines + k]], n)[0] for k in list(range(1, lines)) + [0]}
    ffn_sum = lambda k: (ffn_part[k].astype(f32) + ffn_got[k].astype(f32)).astype(bf)

    out_grad = cotangent.reshape(rows, width).astype(f32)
    down_received = (place_rows(cot_all) * slot_weight).astype(bf)
    hidden_grad = jnp.einsum("ecrd,edf->ecrf", down_received, full_down, preferred_element_type=f32)
    slope = sigmoid_gate * (1.0 + gate * (1.0 - sigmoid_gate))
    gate_grad = (hidden_grad * up_part * slope).astype(bf)
    up_grad = (hidden_grad * activated).astype(bf)
    early = list(range(1, lines - 1))
    gate_grad, up_grad, got = barrier((gate_grad, up_grad, [ffn_got[k] for k in early]))
    ffn_got.update(zip(early, got))
    ffn_pieces = [reduce_column(ffn_sum(k), k, n) for k in early]
    rows_gate = jnp.einsum("ecrf,edf->ecrd", gate_grad, full_gate, preferred_element_type=f32)
    rows_gate, ffn_got[lines - 1] = barrier((rows_gate, ffn_got[lines - 1]))
    ffn_pieces.append(reduce_column(ffn_sum(lines - 1), lines - 1, n))
    rows_up = jnp.einsum("ecrf,edf->ecrd", up_grad, full_up, preferred_element_type=f32)
    rows_part = unplace((rows_gate + rows_up).astype(bf))
    rows_part, down_received, hidden = barrier((rows_part, down_received, hidden))
    down_term = jnp.einsum("ecrd,ecrf->edf", down_received, hidden, preferred_element_type=f32)
    scatter = lambda v: lax.psum_scatter(v, "fsdp", scatter_dimension=1, tiled=True)
    rows_part, ffn_pieces, ffn_got[0], down_term = barrier(
        (rows_part, ffn_pieces, ffn_got[0], down_term.astype(bf))
    )
    by_slot = lambda v: v.reshape(local_experts, n * capacity, v.shape[-1])
    ffn_in_grad, gate_term, up_term = reduce_terms(
        rows_part, by_slot(received), by_slot(gate_grad), by_slot(up_grad), n, 8, 512, 4
    )
    scattered = [scatter(down_term)]
    scattered += [scatter(gate_term), scatter(up_term)]
    mid_back, ffn_gain_term = norm_backward(mid, norm_two, gain_ffn, ffn_in_grad)
    mid_grad = out_grad + mid_back
    branch_grad = mid_grad.astype(bf)

    branch_all = gather_rows(branch_grad, n, 8, True, 5).reshape(length, width)
    out_rows = lax.dynamic_slice_in_dim(full_out, me * span, span, 0)
    heads_grad = jnp.einsum("te,de->td", branch_all, out_rows, preferred_element_type=f32).astype(bf)
    out_term = jnp.einsum("td,te->de", heads_out, branch_all, preferred_element_type=f32).astype(bf)
    query_back, key_back, value_back = attend_back(
        queries, keys, values, heads_grad, heads_out, log_totals, heads, block, scale
    )
    proj_grad, gain_terms = heads_back(
        query_back, key_back, value_back, proj, factors, head_gains, tables, n, width, 6
    )
    normed_part = jnp.einsum("te,de->td", proj_grad, w_heads, preferred_element_type=f32).astype(bf)
    head_term = jnp.einsum("td,te->de", normed, proj_grad, preferred_element_type=f32).astype(bf)
    head_term = head_term.reshape(n, groups, part, 3 * span).swapaxes(0, 1)
    normed_part, out_term, head_term = barrier((normed_part, out_term, head_term))
    block_out = mid + sum(piece.astype(f32) for piece in [ffn_part[0], ffn_got[0]] + ffn_pieces)
    normed_grad = reduce_rows(normed_part.reshape(n, rows, width), n, 8, True, 7)
    out_term, head_term, (down_sum, gate_sum, up_sum), normed_grad = barrier(
        (out_term, head_term, scattered, normed_grad)
    )
    out_sum = lax.psum_scatter(out_term, "fsdp", scatter_dimension=0, tiled=True).astype(f32)
    gate_sum, up_sum, down_sum = widen(gate_sum), widen(up_sum), widen(down_sum)
    input_back, attn_gain_term = norm_backward(inputs, inverse_norm(inputs), gain_attn, normed_grad)
    tokens_grad = mid_grad + input_back
    head_term = lax.psum_scatter(head_term, "fsdp", scatter_dimension=0, tiled=True)
    head_term = head_term.reshape(n, part, 3, span)
    head_term = lax.all_to_all(head_term, "seq", split_axis=0, concat_axis=0, tiled=True)
    head_sums = [
        head_term[:, :, i].swapaxes(0, 1).reshape(part, width).astype(f32) for i in range(3)
    ]
    by_span = lambda v: v.reshape(n, 1, span)
    sent_gains = jnp.concatenate([by_span(attn_gain_term), by_span(ffn_gain_term)], axis=1)
    sent_gains = jnp.pad(sent_gains, ((0, 0), (0, 6), (0, 0)))
    gain_sums = sum_gains(sent_gains, gain_terms, n, groups, 8)
    gain_sums = lax.dynamic_slice_in_dim(gain_sums, lax.axis_index("fsdp") * part, part, 1)
    return (
        block_out.astype(bf).reshape(tokens.shape),
        tokens_grad.reshape(tokens.shape),
        gain_sums[0],
        gain_sums[2],
        gain_sums[3],
        gain_sums[1],
        head_sums[0],
        head_sums[1],
        head_sums[2],
        out_sum,
        gate_sum,
        up_sum,
        down_sum,
    )


def solution(mesh):
    rows3 = P("fsdp", "seq", None)
    both = P(("seq", "fsdp"))
    both2 = P(("seq", "fsdp"), None)
    placed = (rows3,) * 4 + (P("fsdp"),) * 4 + (P("fsdp", None),) * 4 + (rows3,) * 3
    return jax.shard_map(
        local,
        mesh=mesh,
        in_specs=placed,
        out_specs=(rows3,) * 2 + (both,) * 4 + (both2,) * 4 + (rows3,) * 3,
        check_vma=False,
    )
```

profile of v0, /device:TPU:0, one launch (start us, length us, event | category | flops | bytes accessed | tf_op | source)
XLA Modules:
  0.0 1294.6 jit_solution(14103237791502157203)
XLA Ops:
  8.0 5.7 copy.147
  14.0 120.2 %project_rows.1 = (bf16[2048,2048]{1,0:T(8,128)(2,1)}, f32[2048,768]{1,0:T(8,128)}, f32[16,256]{1,0:T(8,128)S(1)}, bf16[2048,768]{1,0:T(8,128)(2,1)}, f32[8,2048]{1,0:T(8,128)S(1)}) custom-call(bf16[256,2048]{1,0:T(8,128)(2,1)S(1)} %bitcast.212, bf16[512,2048]{1,0:T(8,128)(2,1)S(1)} %copy-done.14, bf16[512,2048]{1,0:T(8,128)(2,1)} %w_key.1, ...), custom_call_target="tpu_custom_call" | custom-call | flops 65999998976 | tf_op jit(solution)/shard_map/project_rows/pallas_call | solution.py:652
  134.2 3.4 copy.146
  137.7 5.6 copy.145
  144.4 2.9 copy-done.15
  147.2 11.6 rotate_rows.1
  161.9 15.9 %attend.1 = (bf16[2048,256]{1,0:T(8,128)(2,1)}, f32[2,1,2048]{2,1,0:T(1,128)}) custom-call(bf16[2048,256]{1,0:T(8,128)(2,1)} %copy-done.17, bf16[2048,256]{1,0:T(8,128)(2,1)} %copy-done.18, bf16[2048,256]{1,0:T(8,128)(2,1)} %copy-done.19), custom_call_target="tpu_custom_call" | custom-call | flops 15000000512 | tf_op jit(solution)/shard_map/attend/pallas_call | solution.py:466
  177.7 2.3 copy.95
  180.0 4.5 all-to-all-start
  187.6 20.8 %all-to-all-done = bf16[8,256,256]{1,2,0:T(8,128)(2,1)S(1)} async-done(((bf16[8,256,256]{1,2,0:T(8,128)(2,1)}), bf16[8,256,256]{1,2,0:T(8,128)(2,1)S(1)}, u32[]{:S(2)}, u32[]{:S(2)}) %all-to-all-start) | async-done | bytes 1048608 | tf_op jit(solution)/shard_map/all_to_all | solution.py:965
  208.4 5.8 multiply_reduce_fusion.2
  216.8 108.1 %gather_rows.2 = bf16[8,256,2048]{2,1,0:T(8,128)(2,1)} custom-call(bf16[256,2048]{1,0:T(8,128)(2,1)} %multiply_convert_fusion.4.own), custom_call_target="tpu_custom_call" | custom-call | flops 62999998464 | tf_op jit(solution)/shard_map/gather_rows/pallas_call | solution.py:86
  325.8 3.4 collective-permute-start
  329.2 3.3 collective-permute-start.1
  335.6 21.5 %convert_bitcast_fusion = bf16[4,8,96,2048]{3,2,0,1:T(8,128)(2,1)} fusion(bf16[8,256,2048]{2,1,0:T(8,128)(2,1)} %gather_rows.2, f32[8,4,256]{2,1,0:T(4,128)S(1)} %copy.97, pred[8,4,256]{2,1,0:T(4,128)(4,1)S(1)} %broadcast_compare_fusion), kind=kOutput, calls=%fused_computation.30 | convolution fusion | flops 3229089792 | bytes 21012480 | tf_op jit(solution)/shard_map/cert,ctd->ecrd/dot_general | solution.py:986
  357.1 22.6 %fusion.7 = f32[4,8,96,1024]{3,2,1,0:T(8,128)} fusion(bf16[4,2048,1024]{2,1,0:T(8,128)(2,1)} %all-gather.7.cloned.1.call-done, bf16[4,8,96,2048]{3,2,0,1:T(8,128)(2,1)} %convert_bitcast_fusion), kind=kOutput, calls=%fused_computation.13 | convolution fusion | flops 12884901888 | bytes 41943040 | tf_op jit(solution)/shard_map/ecrd,edf->ecrf/dot_general | solution.py:989
  379.7 2.3 collective-permute-start.5
  384.0 26.9 %multiply_convert_fusion.3 = (bf16[4,8,96,1024]{3,2,1,0:T(8,128)(2,1)}, f32[4,8,96,1024]{3,2,1,0:T(8,128)}) fusion(f32[4,8,96,1024]{3,2,1,0:T(8,128)} %fusion.7, bf16[4,2048,1024]{2,1,0:T(8,128)(2,1)} %all-gather.9.cloned.1.call-done, bf16[4,8,96,2048]{3,2,0,1:T(8,128)(2,1)} %convert_bitcast_fusion), kind=kOutput, calls=%fused_computation.27 | convolution fusion | flops 12903776256 | bytes 60817408 | tf_op jit(solution)/shard_map/ecrd,edf->ecrf/dot_general | solution.py:992
  413.0 11.5 all-gather.11.cloned.1.call-done
  424.5 19.5 %multiply_convert_fusion = bf16[4,8,96,2048]{3,2,1,0:T(8,128)(2,1)} fusion(f32[4,8,96]{2,1,0:T(8,128)S(1)} %copy-done.40, bf16[4,8,96,1024]{3,2,1,0:T(8,128)(2,1)} %get-tuple-element.127, bf16[4,2048,1024]{2,1,0:T(8,128)(2,1)} %all-gather.11.cloned.1.call-done), kind=kOutput, calls=%fused_computation.5 | convolution fusion | flops 12897484800 | bytes 35663872 | tf_op jit(solution)/shard_map/ecrf,edf->ecrd/dot_general | solution.py:996
  444.1 10.7 copy.101
  456.2 11.4 bitcast_convert_fusion.2
  471.3 2.1 fusion.52
  473.5 2.1 fusion.53
  475.6 6.9 collective-permute-done.11
  482.5 11.2 collective-permute-done.12
  493.7 10.2 collective-permute-done.13
  505.0 2.1 fusion.55
  507.1 2.1 fusion.56
  511.4 10.2 fusion
  521.6 4.4 slice_bitcast_fusion
  530.0 28.9 %multiply_convert_fusion.1 = (bf16[4,8,96,1024]{3,2,1,0:T(8,128)(2,1)}, bf16[4,8,96,1024]{3,2,1,0:T(8,128)(2,1)}) fusion(f32[4,8,96,1024]{3,2,1,0:T(8,128)} %fusion.7, f32[4,8,96,1024]{3,2,1,0:T(8,128)} %get-tuple-element.188, bf16[4,8,96,2048]{3,2,1,0:T(8,128)(2,1)} %fusion, bf16[4,2048,1024]{2,1,0:T(8,128)(2,1)} %all-gather.11.cloned.1.call-done), kind=kOutput, calls=%fused_computation.25 | convolution fusion | flops 12925796352 | bytes 67108864 | tf_op jit(solution)/shard_map/ecrd,edf->ecrf/dot_general | solution.py:1011
  558.9 15.7 %collective-permute-done.15 = bf16[256,2048]{1,0:T(8,128)(2,1)S(1)} collective-permute-done((bf16[256,2048]{1,0:T(8,128)(2,1)}, bf16[256,2048]{1,0:T(8,128)(2,1)S(1)}, u32[]{:S(2)}, u32[]{:S(2)}) %collective-permute-start.15) | collective-permute-done | bytes 1048608 | tf_op jit(solution)/shard_map/ppermute | solution.py:912
  574.7 21.9 %fusion.5 = f32[4,8,96,2048]{3,2,1,0:T(8,128)} fusion(bf16[4,8,96,1024]{3,2,1,0:T(8,128)(2,1)} %get-tuple-element.119, bf16[4,2048,1024]{2,1,0:T(8,128)(2,1)} %all-gather.7.cloned.1.call-done), kind=kOutput, calls=%fused_computation.11 | convolution fusion | flops 12884901888 | bytes 48234496 | tf_op jit(solution)/shard_map/ecrf,edf->ecrd/dot_general | solution.py:1019
  597.1 24.3 %fusion.1 = f32[4,8,96,2048]{3,2,1,0:T(8,128)} fusion(bf16[4,8,96,1024]{3,2,1,0:T(8,128)(2,1)S(1)} %copy-done.49, bf16[4,2048,1024]{2,1,0:T(8,128)(2,1)} %all-gather.9.cloned.1.call-done), kind=kOutput, calls=%fused_computation.7 | convolution fusion | flops 12884901888 | bytes 48234496 | tf_op jit(solution)/shard_map/ecrf,edf->ecrd/dot_general | solution.py:1022
  621.4 21.2 %bitcast_convert_fusion.1.part = bf16[8,256,2048]{2,1,0:T(8,128)(2,1)} fusion(f32[8,4,256]{2,1,0:T(4,128)S(1)} %copy.97, pred[8,4,256]{2,1,0:T(4,128)(4,1)S(1)} %broadcast_compare_fusion, f32[4,8,96,2048]{3,2,1,0:T(8,128)} %fusion.5, f32[4,8,96,2048]{3,2,1,0:T(8,128)} %fusion.1), kind=kOutput, calls=%fused_computation.6 | convolution fusion | flops 3239575552 | bytes 58761216 | tf_op jit(solution)/shard_map/cert,ecrd->ctd/dot_general | solution.py:987
  642.7 4.5 fusion.42
  647.2 3.3 collective-permute-start.17
  651.6 19.8 %bitcast_convert_fusion = bf16[4,2048,1024]{2,1,0:T(8,128)(2,1)} fusion(bf16[4,8,96,2048]{3,2,1,0:T(8,128)(2,1)} %fusion, bf16[4,8,96,1024]{3,2,1,0:T(8,128)(2,1)} %get-tuple-element.127), kind=kOutput, calls=%fused_computation.1 | convolution fusion | flops 12893290496 | bytes 35651584 | tf_op jit(solution)/shard_map/ecrd,ecrf->edf/dot_general | solution.py:1025
  671.4 2.9 collective-permute-done.17
  674.3 62.1 %collective-permute-done.18 = bf16[256,2048]{1,0:T(8,128)(2,1)S(1)} collective-permute-done((bf16[256,2048]{1,0:T(8,128)(2,1)}, bf16[256,2048]{1,0:T(8,128)(2,1)S(1)}, u32[]{:S(2)}, u32[]{:S(2)}) %collective-permute-start.18) | collective-permute-done | bytes 1048608 | tf_op jit(solution)/shard_map/ppermute | solution.py:916
  737.5 98.2 %reduce_terms.1 = (f32[256,2048]{1,0:T(8,128)S(1)}, bf16[4,2048,1024]{2,1,0:T(8,128)(2,1)}, bf16[4,2048,1024]{2,1,0:T(8,128)(2,1)}) custom-call(bf16[8,256,2048]{2,1,0:T(8,128)(2,1)} %bitcast_convert_fusion.1.part, bf16[4,768,2048]{2,1,0:T(8,128)(2,1)} %bitcast.222, bf16[4,768,1024]{2,1,0:T(8,128)(2,1)} %bitcast.243, bf16[4,768,1024]{2,1,0:T(8,128)(2,1)} %bitcast.242), custom_call_target="tpu_custom_call" | custom-call | flops 62999998464 | tf_op jit(solution)/shard_map/reduce_terms/pallas_call | solution.py:307
  837.1 2.8 multiply_reduce_fusion
  840.4 3.4 fusion.74.own
  843.9 108.2 %gather_rows.3 = bf16[8,256,2048]{2,1,0:T(8,128)(2,1)} custom-call(bf16[256,2048]{1,0:T(8,128)(2,1)} %fusion.74.own), custom_call_target="tpu_custom_call" | custom-call | flops 62999998464 | tf_op jit(solution)/shard_map/gather_rows/pallas_call | solution.py:86
  952.1 7.1 convolution_convert_fusion.3.g_ref
  959.2 22.1 %attend_back.1 = (bf16[2048,256]{1,0:T(8,128)(2,1)}, bf16[2048,256]{1,0:T(8,128)(2,1)}, bf16[2048,256]{1,0:T(8,128)(2,1)}) custom-call(bf16[2048,256]{1,0:T(8,128)(2,1)} %copy-done.17, bf16[2048,256]{1,0:T(8,128)(2,1)} %copy-done.18, bf16[2048,256]{1,0:T(8,128)(2,1)} %copy-done.19, bf16[2048,256]{1,0:T(8,128)(2,1)} %convolution_convert_fusion.3.g_ref, ...), custom_call_target="tpu_custom_call" | custom-call | flops 35999997952 | tf_op jit(solution)/shard_map/attend_back/pallas_call | solution.py:533
  981.4 4.0 copy-done.16
  989.0 17.5 %heads_back.1 = (bf16[2048,768]{1,0:T(8,128)(2,1)S(1)}, f32[8,256]{1,0:T(8,128)S(1)}) custom-call(bf16[2048,256]{1,0:T(8,128)(2,1)S(1)} %copy-done.20, bf16[2048,256]{1,0:T(8,128)(2,1)S(1)} %copy-done.21, bf16[2048,256]{1,0:T(8,128)(2,1)S(1)} %copy-done.22, f32[2048,768]{1,0:T(8,128)S(1)} %copy-done.16, f32[16,256]{1,0:T(8,128)S(1)} %get-tuple-element.138.factors, ...), custom_call_target="tpu_custom_call" | custom-call | flops 12000000000 | tf_op jit(solution)/shard_map/heads_back/pallas_call | solution.py:846
  1006.5 9.6 convolution_convert_fusion.1
  1018.1 3.4 convolution_convert_fusion.2
  1021.5 11.0 convolution_convert_fusion
  1032.6 99.3 %reduce_rows.1 = f32[256,2048]{1,0:T(8,128)} custom-call(bf16[8,256,2048]{2,1,0:T(8,128)(2,1)} %bitcast.241), custom_call_target="tpu_custom_call" | custom-call | flops 58800001024 | tf_op jit(solution)/shard_map/reduce_rows/pallas_call | solution.py:157
  1132.0 82.1 %reduce-scatter.6.cloned.1.call-done.x_ref = bf16[4,512,1024]{2,1,0:T(8,128)(2,1)} async-done(((bf16[4,2048,1024]{2,1,0:T(8,128)(2,1)}), bf16[4,512,1024]{2,1,0:T(8,128)(2,1)}) %reduce-scatter.6.cloned.1.call-update) | async-done | bytes 4194320 | tf_op jit(solution)/shard_map/reduce_scatter | solution.py:1026
  1214.5 2.3 fusion.40
  1217.4 11.2 sum_gains.1
  1229.9 6.6 widen.3
  1236.5 6.5 widen.4
  1243.1 11.5 reduce-scatter.12.cloned.1.call-done
  1254.6 2.5 reshape.457
  1258.1 5.5 all-to-all-start.1
  1263.7 6.8 widen.5
  1270.5 6.4 fusion.39
  1276.9 5.0 reduce-scatter.14.cloned.1.call-done
  (203 shorter events, 50.1 us)
Async XLA Ops:
  7.2 201.2 %all-gather.5.cloned.1.call-start = ((), (), s32[]{:S(2)}) async-start(), calls=%async_computation.7 | async-start | bytes 10485760 | tf_op jit(solution)/shard_map/all_gather | solution.py:944
  7.9 5.9 copy-start.46
  7.9 5.9 copy-start.47
  7.9 5.9 copy-start.48
  8.0 6.0 copy-start.2
  8.0 6.0 copy-start.14
  8.0 349.1 %all-gather.7.cloned.1.call-start = ((), (), s32[]{:S(2)}) async-start(), calls=%async_computation.8 | async-start | bytes 20971520 | tf_op jit(solution)/shard_map/all_gather | solution.py:945
  13.8 370.3 %all-gather.9.cloned.1.call-start = ((), (), s32[]{:S(2)}) async-start(), calls=%async_computation.9 | async-start | bytes 20971520 | tf_op jit(solution)/shard_map/all_gather | solution.py:945
  14.0 120.3 %copy-start.28 = (bf16[512,4,1024]{2,1,0:T(4,128)(2,1)S(1)}, bf16[512,4,1024]{2,1,0:T(4,128)(2,1)}, u32[]{:S(2)}) copy-start(bf16[512,4,1024]{2,1,0:T(4,128)(2,1)} %param.28) | copy-start | bytes 12582916
  137.7 286.9 %all-gather.11.cloned.1.call-start = ((), (), s32[]{:S(2)}) async-start(), calls=%async_computation.10 | async-start | bytes 20971520 | tf_op jit(solution)/shard_map/all_gather | solution.py:945
  143.7 15.2 %copy-start.12 = (f32[2,256]{1,0:T(2,128)}, f32[2,256]{1,0:T(2,128)S(1)}, u32[]{:S(2)}) copy-start(f32[2,256]{1,0:T(2,128)S(1)} %constant_dynamic-slice_fusion.1.gains) | copy-start | bytes 6148
  143.8 15.1 %copy-start.8 = (f32[8,128]{1,0:T(8,128)}, f32[8,128]{1,0:T(8,128)S(1)}, u32[]{:S(2)}) copy-start(f32[8,128]{1,0:T(8,128)S(1)} %get-tuple-element.181.far_sin) | copy-start | bytes 12292
  143.8 15.1 %copy-start.10 = (f32[8,128]{1,0:T(8,128)}, f32[8,128]{1,0:T(8,128)S(1)}, u32[]{:S(2)}) copy-start(f32[8,128]{1,0:T(8,128)S(1)} %get-tuple-element.182.far_cos) | copy-start | bytes 12292
  144.3 14.6 %copy-start.4 = (f32[256,128]{1,0:T(8,128)}, f32[256,128]{1,0:T(8,128)S(1)}, u32[]{:S(2)}) copy-start(f32[256,128]{1,0:T(8,128)S(1)} %get-tuple-element.183.near_sin) | copy-start | bytes 393220
  144.3 14.6 %copy-start.6 = (f32[256,128]{1,0:T(8,128)}, f32[256,128]{1,0:T(8,128)S(1)}, u32[]{:S(2)}) copy-start(f32[256,128]{1,0:T(8,128)S(1)} %get-tuple-element.184.near_cos) | copy-start | bytes 393220
  180.0 28.4 %all-to-all-start = ((bf16[8,256,256]{1,2,0:T(8,128)(2,1)}), bf16[8,256,256]{1,2,0:T(8,128)(2,1)S(1)}, u32[]{:S(2)}, u32[]{:S(2)}) async-start(bf16[8,256,256]{1,2,0:T(8,128)(2,1)} %copy.95), calls=%async_computation | async-start | bytes 2097152 | tf_op jit(solution)/shard_map/all_to_all | solution.py:965
  184.5 947.4 %reduce-scatter.10.cloned.1.call-start = ((), (), s32[]{:S(2)}) async-start(), calls=%async_computation.13 | async-start | bytes 20971520 | tf_op jit(solution)/shard_map/reduce_scatter | solution.py:1026
  187.6 26.7 %copy-start.32 = (f32[1,2048]{1,0:T(1,128)}, f32[1,2048]{1,0:T(1,128)S(1)}, u32[]{:S(2)}) copy-start(f32[1,2048]{1,0:T(1,128)S(1)} %get-tuple-element.176) | copy-start | bytes 24580
  216.8 108.1 %copy-start.25 = (bf16[1,256,2048]{2,1,0:T(8,128)(2,1)S(1)}, bf16[1,256,2048]{2,1,0:T(8,128)(2,1)}, u32[]{:S(2)}) copy-start(bf16[1,256,2048]{2,1,0:T(8,128)(2,1)} %param.18) | copy-start | bytes 3145732
  325.8 53.9 %collective-permute-start = (bf16[128,2048]{1,0:T(8,128)(2,1)}, bf16[128,2048]{1,0:T(8,128)(2,1)S(1)}, u32[]{:S(2)}, u32[]{:S(2)}) collective-permute-start(bf16[128,2048]{1,0:T(8,128)(2,1)} %get-tuple-element.171), channel_id=1, source_target_pairs={{0,8},{4,12},{8,16},{12,20},{16,24},{20,28},{24,0},{28,4},{1,9},{5... | collective-permute-start | bytes 1572872 | tf_op jit(solution)/shard_map/ppermute | solution.py:908
  329.2 52.8 %collective-permute-start.1 = (bf16[128,2048]{1,0:T(8,128)(2,1)}, bf16[128,2048]{1,0:T(8,128)(2,1)S(1)}, u32[]{:S(2)}, u32[]{:S(2)}) collective-permute-start(bf16[128,2048]{1,0:T(8,128)(2,1)} %get-tuple-element.171), channel_id=1, source_target_pairs={{0,16},{4,20},{8,24},{12,28},{16,0},{20,4},{24,8},{28,12},{1,17},{... | collective-permute-start | bytes 1572872 | tf_op jit(solution)/shard_map/ppermute | solution.py:908
  332.5 49.8 %collective-permute-start.2 = (bf16[128,2048]{1,0:T(8,128)(2,1)}, bf16[128,2048]{1,0:T(8,128)(2,1)}, u32[]{:S(2)}, u32[]{:S(2)}) collective-permute-start(bf16[128,2048]{1,0:T(8,128)(2,1)} %get-tuple-element.171), channel_id=1, source_target_pairs={{0,24},{4,28},{8,0},{12,4},{16,8},{20,12},{24,16},{28,20},{1,25},{... | collective-permute-start | bytes 1572872 | tf_op jit(solution)/shard_map/ppermute | solution.py:908
  332.5 78.4 %collective-permute-start.3 = (bf16[128,2048]{1,0:T(8,128)(2,1)S(1)}, bf16[128,2048]{1,0:T(8,128)(2,1)S(1)}, u32[]{:S(2)}, u32[]{:S(2)}) collective-permute-start(bf16[128,2048]{1,0:T(8,128)(2,1)S(1)} %get-tuple-element.170), channel_id=1, source_target_pairs={{0,8},{4,12},{8,16},{12,20},{16,24},{20,28},{24,0},{28,4},{1,9},{5... | collective-permute-start | bytes 1572872 | tf_op jit(solution)/shard_map/ppermute | solution.py:908
  334.5 76.7 %collective-permute-start.4 = (bf16[128,2048]{1,0:T(8,128)(2,1)S(1)}, bf16[128,2048]{1,0:T(8,128)(2,1)}, u32[]{:S(2)}, u32[]{:S(2)}) collective-permute-start(bf16[128,2048]{1,0:T(8,128)(2,1)S(1)} %get-tuple-element.170), channel_id=1, source_target_pairs={{0,16},{4,20},{8,24},{12,28},{16,0},{20,4},{24,8},{28,12},{1,17},{... | collective-permute-start | bytes 1572872 | tf_op jit(solution)/shard_map/ppermute | solution.py:908
  379.7 44.8 %copy-start.40 = (f32[4,8,96]{2,1,0:T(8,128)S(1)}, f32[4,8,96]{2,1,0:T(8,128)}, u32[]{:S(2)}) copy-start(f32[4,8,96]{2,1,0:T(8,128)} %copy.103) | copy-start | bytes 36868
  379.7 75.0 %collective-permute-start.5 = (bf16[128,2048]{1,0:T(8,128)(2,1)S(1)}, bf16[128,2048]{1,0:T(8,128)(2,1)S(1)}, u32[]{:S(2)}, u32[]{:S(2)}) collective-permute-start(bf16[128,2048]{1,0:T(8,128)(2,1)S(1)} %get-tuple-element.170), channel_id=1, source_target_pairs={{0,24},{4,28},{8,0},{12,4},{16,8},{20,12},{24,16},{28,20},{1,25},{... | collective-permute-start | bytes 1572872 | tf_op jit(solution)/shard_map/ppermute | solution.py:908
  382.0 74.2 %collective-permute-start.6 = (bf16[128,2048]{1,0:T(8,128)(2,1)}, bf16[128,2048]{1,0:T(8,128)(2,1)S(1)}, u32[]{:S(2)}, u32[]{:S(2)}) collective-permute-start(bf16[128,2048]{1,0:T(8,128)(2,1)} %get-tuple-element.171), channel_id=1, source_target_pairs={{0,4},{4,0},{8,12},{12,8},{16,20},{20,16},{24,28},{28,24},{1,5},{5... | collective-permute-start | bytes 1572872 | tf_op jit(solution)/shard_map/ppermute | solution.py:912
  382.3 73.9 %collective-permute-start.7 = (bf16[128,2048]{1,0:T(8,128)(2,1)S(1)}, bf16[128,2048]{1,0:T(8,128)(2,1)}, u32[]{:S(2)}, u32[]{:S(2)}) collective-permute-start(bf16[128,2048]{1,0:T(8,128)(2,1)S(1)} %collective-permute-done), channel_id=1, source_target_pairs={{0,4},{4,0},{8,12},{12,8},{16,20},{20,16},{24,28},{28,24},{1,5},{5... | collective-permute-start | bytes 1572872 | tf_op jit(solution)/shard_map/ppermute | solution.py:912
  410.9 45.3 %collective-permute-start.8 = (bf16[128,2048]{1,0:T(8,128)(2,1)S(1)}, bf16[128,2048]{1,0:T(8,128)(2,1)}, u32[]{:S(2)}, u32[]{:S(2)}) collective-permute-start(bf16[128,2048]{1,0:T(8,128)(2,1)S(1)} %collective-permute-done.1), channel_id=1, source_target_pairs={{0,4},{4,0},{8,12},{12,8},{16,20},{20,16},{24,28},{28,24},{1,5},{5... | collective-permute-start | bytes 1572872 | tf_op jit(solution)/shard_map/ppermute | solution.py:912
  411.2 45.0 %collective-permute-start.9 = (bf16[128,2048]{1,0:T(8,128)(2,1)}, bf16[128,2048]{1,0:T(8,128)(2,1)}, u32[]{:S(2)}, u32[]{:S(2)}) collective-permute-start(bf16[128,2048]{1,0:T(8,128)(2,1)} %collective-permute-done.2), channel_id=1, source_target_pairs={{0,4},{4,0},{8,12},{12,8},{16,20},{20,16},{24,28},{28,24},{1,5},{5... | collective-permute-start | bytes 1572872 | tf_op jit(solution)/shard_map/ppermute | solution.py:912
  454.7 20.8 %collective-permute-start.10 = (bf16[128,2048]{1,0:T(8,128)(2,1)S(1)}, bf16[128,2048]{1,0:T(8,128)(2,1)S(1)}, u32[]{:S(2)}, u32[]{:S(2)}) collective-permute-start(bf16[128,2048]{1,0:T(8,128)(2,1)S(1)} %get-tuple-element.170), channel_id=1, source_target_pairs={{0,4},{4,0},{8,12},{12,8},{16,20},{20,16},{24,28},{28,24},{1,5},{5... | collective-permute-start | bytes 1572872 | tf_op jit(solution)/shard_map/ppermute | solution.py:912
  467.7 14.8 %collective-permute-start.11 = (bf16[128,2048]{1,0:T(8,128)(2,1)S(1)}, bf16[128,2048]{1,0:T(8,128)(2,1)S(1)}, u32[]{:S(2)}, u32[]{:S(2)}) collective-permute-start(bf16[128,2048]{1,0:T(8,128)(2,1)S(1)} %collective-permute-done.3), channel_id=1, source_target_pairs={{0,4},{4,0},{8,12},{12,8},{16,20},{20,16},{24,28},{28,24},{1,5},{5... | collective-permute-start | bytes 1572872 | tf_op jit(solution)/shard_map/ppermute | solution.py:912
  468.2 25.5 %collective-permute-start.12 = (bf16[128,2048]{1,0:T(8,128)(2,1)}, bf16[128,2048]{1,0:T(8,128)(2,1)S(1)}, u32[]{:S(2)}, u32[]{:S(2)}) collective-permute-start(bf16[128,2048]{1,0:T(8,128)(2,1)} %collective-permute-done.4), channel_id=1, source_target_pairs={{0,4},{4,0},{8,12},{12,8},{16,20},{20,16},{24,28},{28,24},{1,5},{5... | collective-permute-start | bytes 1572872 | tf_op jit(solution)/shard_map/ppermute | solution.py:912
  469.7 34.2 %collective-permute-start.13 = (bf16[128,2048]{1,0:T(8,128)(2,1)S(1)}, bf16[128,2048]{1,0:T(8,128)(2,1)S(1)}, u32[]{:S(2)}, u32[]{:S(2)}) collective-permute-start(bf16[128,2048]{1,0:T(8,128)(2,1)S(1)} %collective-permute-done.5), channel_id=1, source_target_pairs={{0,4},{4,0},{8,12},{12,8},{16,20},{20,16},{24,28},{28,24},{1,5},{5... | collective-permute-start | bytes 1572872 | tf_op jit(solution)/shard_map/ppermute | solution.py:912
  525.9 33.0 %collective-permute-start.14 = (bf16[256,2048]{1,0:T(8,128)(2,1)}, bf16[256,2048]{1,0:T(8,128)(2,1)S(1)}, u32[]{:S(2)}, u32[]{:S(2)}) collective-permute-start(bf16[256,2048]{1,0:T(8,128)(2,1)} %get-tuple-element.164), channel_id=1, source_target_pairs={{0,4},{4,0},{8,12},{12,8},{16,20},{20,16},{24,28},{28,24},{1,5},{5... | collective-permute-start | bytes 3145736 | tf_op jit(solution)/shard_map/ppermute | solution.py:912
  526.5 48.2 %collective-permute-start.15 = (bf16[256,2048]{1,0:T(8,128)(2,1)}, bf16[256,2048]{1,0:T(8,128)(2,1)S(1)}, u32[]{:S(2)}, u32[]{:S(2)}) collective-permute-start(bf16[256,2048]{1,0:T(8,128)(2,1)} %get-tuple-element.163), channel_id=1, source_target_pairs={{0,4},{4,0},{8,12},{12,8},{16,20},{20,16},{24,28},{28,24},{1,5},{5... | collective-permute-start | bytes 3145736 | tf_op jit(solution)/shard_map/ppermute | solution.py:912
  528.0 69.2 %collective-permute-start.16 = (bf16[256,2048]{1,0:T(8,128)(2,1)}, bf16[256,2048]{1,0:T(8,128)(2,1)S(1)}, u32[]{:S(2)}, u32[]{:S(2)}) collective-permute-start(bf16[256,2048]{1,0:T(8,128)(2,1)} %get-tuple-element.162), channel_id=1, source_target_pairs={{0,4},{4,0},{8,12},{12,8},{16,20},{20,16},{24,28},{28,24},{1,5},{5... | collective-permute-start | bytes 3145736 | tf_op jit(solution)/shard_map/ppermute | solution.py:912
  528.5 142.9 %collective-permute-start.20 = (bf16[256,2048]{1,0:T(8,128)(2,1)}, bf16[256,2048]{1,0:T(8,128)(2,1)}, u32[]{:S(2)}, u32[]{:S(2)}) collective-permute-start(bf16[256,2048]{1,0:T(8,128)(2,1)} %get-tuple-element.161), channel_id=1, source_target_pairs={{0,4},{4,0},{8,12},{12,8},{16,20},{20,16},{24,28},{28,24},{1,5},{5... | collective-permute-start | bytes 3145736 | tf_op jit(solution)/shard_map/ppermute | solution.py:912
  574.7 22.5 %copy-start.49 = (bf16[4,8,96,1024]{3,2,1,0:T(8,128)(2,1)S(1)}, bf16[4,8,96,1024]{3,2,1,0:T(8,128)(2,1)}, u32[]{:S(2)}) copy-start(bf16[4,8,96,1024]{3,2,1,0:T(8,128)(2,1)} %get-tuple-element.121) | copy-start | bytes 18874372
  647.2 27.2 %collective-permute-start.17 = (bf16[256,2048]{1,0:T(8,128)(2,1)}, bf16[256,2048]{1,0:T(8,128)(2,1)S(1)}, u32[]{:S(2)}, u32[]{:S(2)}) collective-permute-start(bf16[256,2048]{1,0:T(8,128)(2,1)} %get-tuple-element.167), channel_id=1, source_target_pairs={{0,24},{4,28},{8,0},{12,4},{16,8},{20,12},{24,16},{28,20},{1,25},{... | collective-permute-start | bytes 3145736 | tf_op jit(solution)/shard_map/ppermute | solution.py:916
  650.5 86.0 %collective-permute-start.18 = (bf16[256,2048]{1,0:T(8,128)(2,1)}, bf16[256,2048]{1,0:T(8,128)(2,1)S(1)}, u32[]{:S(2)}, u32[]{:S(2)}) collective-permute-start(bf16[256,2048]{1,0:T(8,128)(2,1)} %get-tuple-element.166), channel_id=1, source_target_pairs={{0,16},{4,20},{8,24},{12,28},{16,0},{20,4},{24,8},{28,12},{1,17},{... | collective-permute-start | bytes 3145736 | tf_op jit(solution)/shard_map/ppermute | solution.py:916
  651.1 85.4 %collective-permute-start.19 = (bf16[256,2048]{1,0:T(8,128)(2,1)}, bf16[256,2048]{1,0:T(8,128)(2,1)S(1)}, u32[]{:S(2)}, u32[]{:S(2)}) collective-permute-start(bf16[256,2048]{1,0:T(8,128)(2,1)} %get-tuple-element.165), channel_id=1, source_target_pairs={{0,8},{4,12},{8,16},{12,20},{16,24},{20,28},{24,0},{28,4},{1,9},{5... | collective-permute-start | bytes 3145736 | tf_op jit(solution)/shard_map/ppermute | solution.py:916
  674.3 62.2 %copy-start.29 = (bf16[256,2048]{1,0:T(8,128)(2,1)}, bf16[256,2048]{1,0:T(8,128)(2,1)S(1)}, u32[]{:S(2)}) copy-start(bf16[256,2048]{1,0:T(8,128)(2,1)S(1)} %collective-permute-done.17) | copy-start | bytes 3145732
  736.5 99.1 %copy-start.31 = (bf16[256,2048]{1,0:T(8,128)(2,1)}, bf16[256,2048]{1,0:T(8,128)(2,1)S(1)}, u32[]{:S(2)}) copy-start(bf16[256,2048]{1,0:T(8,128)(2,1)S(1)} %collective-permute-done.19) | copy-start | bytes 3145732
  835.7 296.3 %reduce-scatter.8.cloned.1.call-start = ((), (), s32[]{:S(2)}) async-start(), calls=%async_computation.12 | async-start | bytes 20971520 | tf_op jit(solution)/shard_map/reduce_scatter | solution.py:1026
  836.3 377.8 %reduce-scatter.6.cloned.1.call-start = ((), (), s32[]{:S(2)}) async-start(), calls=%async_computation.11 | async-start | bytes 20971520 | tf_op jit(solution)/shard_map/reduce_scatter | solution.py:1026
  837.0 417.6 %reduce-scatter.12.cloned.1.call-start = ((), (), s32[]{:S(2)}) async-start(), calls=%async_computation.14 | async-start | bytes 3932160 | tf_op jit(solution)/shard_map/reduce_scatter | solution.py:1063
  959.2 22.1 %copy-start.5 = (f32[256,128]{1,0:T(8,128)S(1)}, f32[256,128]{1,0:T(8,128)}, u32[]{:S(2)}) copy-start(f32[256,128]{1,0:T(8,128)} %copy-done.4) | copy-start | bytes 393220
  959.2 22.1 %copy-start.7 = (f32[256,128]{1,0:T(8,128)S(1)}, f32[256,128]{1,0:T(8,128)}, u32[]{:S(2)}) copy-start(f32[256,128]{1,0:T(8,128)} %copy-done.6) | copy-start | bytes 393220
  959.2 22.1 %copy-start.9 = (f32[8,128]{1,0:T(8,128)S(1)}, f32[8,128]{1,0:T(8,128)}, u32[]{:S(2)}) copy-start(f32[8,128]{1,0:T(8,128)} %copy-done.8) | copy-start | bytes 12292
  959.2 22.2 %copy-start.11 = (f32[8,128]{1,0:T(8,128)S(1)}, f32[8,128]{1,0:T(8,128)}, u32[]{:S(2)}) copy-start(f32[8,128]{1,0:T(8,128)} %copy-done.10) | copy-start | bytes 12292
  959.2 22.2 %copy-start.13 = (f32[2,256]{1,0:T(2,128)S(1)}, f32[2,256]{1,0:T(2,128)}, u32[]{:S(2)}) copy-start(f32[2,256]{1,0:T(2,128)} %copy-done.12) | copy-start | bytes 6148
  989.0 29.1 %slice-start = ((s8[8388608]{0:T(1024)(128)(4,1)}), s8[4194304]{0:T(1024)(128)(4,1)S(1)}, s32[]{:S(2)}) async-start(s8[8388608]{0:T(1024)(128)(4,1)} %bitcast.214), calls=%async_computation.16 | async-start | bytes 8388608
  1006.5 9.7 copy-start.23
  1006.5 11.6 slice-start.1
  1032.6 181.6 %copy-start.3 = (bf16[1,256,2048]{2,1,0:T(8,128)(2,1)S(1)}, bf16[1,256,2048]{2,1,0:T(8,128)(2,1)}, u32[]{:S(2)}) copy-start(bf16[1,256,2048]{2,1,0:T(8,128)(2,1)} %param.15) | copy-start | bytes 3145732
  1032.6 181.9 %copy-start.35 = (f32[1,2048]{1,0:T(1,128)S(1)}, f32[1,2048]{1,0:T(1,128)}, u32[]{:S(2)}) copy-start(f32[1,2048]{1,0:T(1,128)} %get-tuple-element.175) | copy-start | bytes 24580
  1131.9 84.8 %copy-start.36 = (f32[2048]{0:T(1024)S(1)}, f32[2048]{0:T(1024)}, u32[]{:S(2)}) copy-start(f32[2048]{0:T(1024)} %get-tuple-element.155) | copy-start | bytes 24580
  1214.1 67.8 %reduce-scatter.14.cloned.1.call-start = ((), (), s32[]{:S(2)}) async-start(), calls=%async_computation.15 | async-start | bytes 1310720 | tf_op jit(solution)/shard_map/reduce_scatter | solution.py:1059
  1258.1 25.7 %all-to-all-start.1 = ((bf16[8,64,3,256]{3,1,2,0:T(8,128)(2,1)}), bf16[8,64,3,256]{3,1,2,0:T(8,128)(2,1)}, u32[]{:S(2)}, u32[]{:S(2)}) async-start(bf16[8,64,3,256]{3,1,2,0:T(8,128)(2,1)} %copy.109), calls=%async_computation.5 | async-start | bytes 1572864 | tf_op jit(solution)/shard_map/all_to_all | solution.py:1065
  1263.7 6.8 copy-start.1
  1263.7 6.8 copy-start.34
  1263.7 6.8 copy-start.39
  1263.7 6.8 copy-start.42
  (20 other events, 47.1 us)
Sparse Core Ops, SparseCore 0:
  9.5 92.6 all-gather.4
  104.4 104.6 all-gather.6
  211.2 105.8 all-gather.8
  318.6 105.8 all-gather.10
  835.8 123.0 reduce-scatter.9
  961.3 125.0 reduce-scatter.7
  1089.0 125.0 reduce-scatter.5
  1216.7 37.8 reduce-scatter.11
  1257.1 24.7 reduce-scatter.13
where the time goes:
time: 1310 us; the launch traced here: 1290 us
  Pallas kernels  632 us (48%)
  matrix products  266 us (20%)
  waiting for transfers between devices  243 us (19%)
  local copies, waits for them, and re-layouts  61.9 us (5%)
  other arithmetic  39 us (3%)
  starting transfers between devices  38 us (3%)
  between operations  15.2 us (1%)
    pallas_call x2, Pallas kernels, gather_rows(): pl.pallas_call(functools.partial(gather_kernel, n, pieces, by_index), out...  216 us
    pallas_call x1, Pallas kernels, project_rows(): pl.pallas_call(functools.partial(project_kernel, n, groups, pieces), out_...  120 us
    pallas_call x1, Pallas kernels, reduce_rows(): pl.pallas_call(functools.partial(reduce_kernel, n, pieces, by_index), out...  99.3 us
    pallas_call x1, Pallas kernels, reduce_terms(): pl.pallas_call(functools.partial(reduce_terms_kernel, n, pieces, tile), o...  98.2 us
    reduce_scatter x3, waiting for transfers between devices, local(): lax.psum_scatter(v, 'fsdp', scatter_dimension=1, tiled=True)  82.2 us
    ppermute x3, waiting for transfers between devices, reduce_column(): return lax.ppermute(v, 'seq', along_lines(n // 2, 2, n // 2 - k))  65.1 us
    ppermute x12, waiting for transfers between devices, gather_across(): return [lax.ppermute(c, 'seq', across_pairs(n // 2, 2)) for c in column]  44.6 us
    dot_general x2, matrix products, local(): jnp.einsum('cert,ecrd->ctd', place, v, preferred_element_type=f32)  32.7 us
  transfers between devices with their start and end apart: 32, of which 13 were waited for; matrix products, arithmetic and copies ran while one was open for 25% of the time, Pallas kernels for 41%

commit v1 on v0

--- a/solution.py
+++ b/solution.py
@@ -97,81 +97,6 @@
         cost_estimate=work(105),
         name="gather_rows",
     )(x)
-
-
-def reduce_kernel(n, pieces, by_index, part, out, mine, got, sums, landed, send_sem, recv_sem, load_sem):
-    pair = 2
-    lines = n // pair
-    me = lax.axis_index("seq")
-    a, b = me // pair, me % pair
-    column = [((a + lines - k) % lines) * pair + b for k in range(1, lines)]
-    across = a * pair + (1 - b)
-    greet(column + [across])
-    rows = out.shape[0] // pieces
-    order = list(range(1, lines)) + [0]
-    if by_index:
-        here = [((a + lines - k) % lines) * pair + b for k in range(lines)]
-        there = [((a + lines - k) % lines) * pair + 1 - b for k in range(lines)]
-    else:
-        here, there = list(range(lines)), list(range(lines, n))
-
-    def piece(p):
-        return pl.ds(p * rows, rows)
-
-    firsts, loads = {}, {}
-    for k in order:
-        for p in range(pieces):
-            copy = push(part.at[there[k], piece(p)], got.at[k, piece(p)],
-                        send_sem.at[k, p], recv_sem.at[k, p], across)
-            copy.start()
-            firsts[k, p] = copy
-            load = pltpu.make_async_copy(part.at[here[k], piece(p)], mine.at[k, piece(p)], load_sem.at[k, p])
-            load.start()
-            loads[k, p] = load
-    seconds = {}
-    for k in order:
-        for p in range(pieces):
-            firsts[k, p].wait_recv()
-            loads[k, p].wait()
-            total = mine[k, piece(p)].astype(jnp.float32) + got[k, piece(p)].astype(jnp.float32)
-            if k:
-                sums[k - 1, piece(p)] = total.astype(jnp.bfloat16)
-                slot = lines + k - 1
-                copy = push(sums.at[k - 1, piece(p)], landed.at[k - 1, piece(p)],
-                            send_sem.at[slot, p], recv_sem.at[slot, p], column[k - 1])
-                copy.start()
-                seconds[k, p] = copy
-            else:
-                for j in range(1, lines):
-                    seconds[j, p].wait_recv()
-                    total += landed[j - 1, piece(p)].astype(jnp.float32)
-                out[piece(p), :] = total
-    for copy in list(firsts.values()) + list(seconds.values()):
-        copy.wait_send()
-
-
-def reduce_rows(part, n, pieces, by_index, collective_id):
-    _, rows, width = part.shape
-    lines = n // 2
-    slots = lines + lines - 1
-    return pl.pallas_call(
-        functools.partial(reduce_kernel, n, pieces, by_index),
-        out_shape=jax.ShapeDtypeStruct((rows, width), jnp.float32),
-        in_specs=[pl.BlockSpec(memory_space=ANY)],
-        out_specs=pl.BlockSpec(memory_space=pltpu.VMEM),
-        scratch_shapes=[
-            pltpu.VMEM((lines, rows, width), jnp.bfloat16),
-            pltpu.VMEM((lines, rows, width), jnp.bfloat16),
-            pltpu.VMEM((lines - 1, rows, width), jnp.bfloat16),
-            pltpu.VMEM((lines - 1, rows, width), jnp.bfloat16),
-            pltpu.SemaphoreType.DMA((slots, pieces)),
-            pltpu.SemaphoreType.DMA((slots, pieces)),
-            pltpu.SemaphoreType.DMA((lines, pieces)),
-        ],
-        compiler_params=pltpu.CompilerParams(collective_id=collective_id, has_side_effects=True),
-        cost_estimate=work(98),
-        name="reduce_rows",
-    )(part)
 
 
 def reduce_terms_kernel(
@@ -332,6 +257,219 @@
     )(part, x, first, second)
 
 
+def reduce_sides_kernel(
+    n, groups, pieces, block, part, head, wide, narrow_a, narrow_b,
+    out, q_out, k_out, v_out, o_out, wide_a, wide_b,
+    mine, got, sums, landed, head_own, head_land, wide_own, wide_land, head_sum, head_got, x_buf, o_buf,
+    send_sem, recv_sem, load_sem, side_send, side_recv, side_load, swap_send, swap_recv, x_sem, o_sem
+):
+    pair = 2
+    lines = n // pair
+    me, group = lax.axis_index("seq"), lax.axis_index("fsdp")
+    a, b = me // pair, me % pair
+    across = a * pair + (1 - b)
+    peers = [(me + k) % n for k in range(1, n)]
+    mates = [(group + k) % groups for k in range(1, groups)]
+    barrier = pltpu.get_barrier_semaphore()
+    for peer in peers:
+        pl.semaphore_signal(barrier, inc=1, device_id={"seq": peer}, device_id_type=MESH)
+    for mate in mates:
+        pl.semaphore_signal(barrier, inc=1, device_id={"fsdp": mate}, device_id_type=MESH)
+    pl.semaphore_wait(barrier, n - 1 + groups - 1)
+    rows = out.shape[0] // pieces
+    experts, shard, _ = narrow_a.shape
+    blocks = shard // block
+
+    def piece(p):
+        return pl.ds(pl.multiple_of(p * rows, rows), rows)
+
+    def first_copy(k, p):
+        there = ((a + lines - k) % lines) * pair + 1 - b
+        return push(part.at[there, piece(p)], got.at[k, piece(p)], send_sem.at[k, p], recv_sem.at[k, p], across)
+
+    def load(k, p):
+        here = ((a + lines - k) % lines) * pair + b
+        return pltpu.make_async_copy(part.at[here, piece(p)], mine.at[k, piece(p)], load_sem.at[k, p])
+
+    def second_copy(k, p):
+        peer = ((a + lines - k) % lines) * pair + b
+        slot = lines + k - 1
+        return push(sums.at[k - 1, piece(p)], landed.at[k - 1, piece(p)], send_sem.at[slot, p], recv_sem.at[slot, p], peer)
+
+    def side_copy(i, k):
+        src, dst = ((head, head_land), (wide, wide_land))[i]
+        return pltpu.make_async_remote_copy(
+            src_ref=src.at[mates[k - 1]], dst_ref=dst.at[k - 1],
+            send_sem=side_send.at[i, k - 1], recv_sem=side_recv.at[i, k - 1],
+            device_id={"fsdp": mates[k - 1]}, device_id_type=MESH)
+
+    def job_refs(j, i):
+        place = pl.ds(pl.multiple_of(j * block, block), block)
+        return (narrow_a, narrow_b)[i].at[:, place, :], (wide_a, wide_b)[i].at[place]
+
+    def x_copy(j, i):
+        return pltpu.make_async_copy(job_refs(j, i)[0], x_buf.at[j % 2, i], x_sem.at[j % 2, i])
+
+    def o_copy(j, i):
+        return pltpu.make_async_copy(o_buf.at[j % 2, i], job_refs(j, i)[1], o_sem.at[j % 2, i])
+
+    for k in list(range(1, lines)) + [0]:
+        for p in range(pieces):
+            first_copy(k, p).start()
+            load(k, p).start()
+    own_copies = [
+        pltpu.make_async_copy(head.at[group], head_own, side_load.at[0]),
+        pltpu.make_async_copy(wide.at[group], wide_own, side_load.at[1]),
+    ]
+    for copy in own_copies:
+        copy.start()
+    for i in range(2):
+        for k in range(1, groups):
+            side_copy(i, k).start()
+        x_copy(0, i).start()
+
+    def add(k, p):
+        first_copy(k, p).wait_recv()
+        load(k, p).wait()
+        return mine[k, piece(p)].astype(jnp.float32) + got[k, piece(p)].astype(jnp.float32)
+
+    def step(s):
+        k, p = 1 + s // pieces, s % pieces
+        sums[k - 1, piece(p)] = add(k, p).astype(jnp.bfloat16)
+        second_copy(k, p).start()
+
+    def job(j, i):
+        @pl.when(j + 1 < blocks)
+        def _():
+            x_copy(j + 1, i).start()
+
+        @pl.when(j >= 2)
+        def _():
+            o_copy(j - 2, i).wait()
+
+        x_copy(j, i).wait()
+        for e in range(experts):
+            o_buf[j % 2, i, :, e, :] = x_buf[j % 2, i, e].astype(jnp.float32)
+        o_copy(j, i).start()
+
+    per = (lines - 1) * pieces // blocks
+
+    def both(t, _):
+        for i in range(per):
+            step(t * per + i)
+            if i == 0:
+                job(t, 0)
+            if i == per - 1:
+                job(t, 1)
+        return 0
+
+    lax.fori_loop(0, blocks, both, 0)
+    for i in range(2):
+        for j in range(max(0, blocks - 2), blocks):
+            o_copy(j, i).wait()
+
+    for copy in own_copies:
+        copy.wait()
+    total, side = head_own[...].astype(jnp.float32), wide_own[...].astype(jnp.float32)
+    for k in range(1, groups):
+        side_copy(0, k).wait_recv()
+        side_copy(1, k).wait_recv()
+        total = total + head_land[k - 1].astype(jnp.float32)
+        side = side + wide_land[k - 1].astype(jnp.float32)
+    o_out[...] = side
+    head_sum[...] = total.astype(jnp.bfloat16)
+    count = o_out.shape[0]
+
+    def swap(k):
+        place = pl.ds(pl.multiple_of(peers[k - 1] * count, count), count)
+        return push(head_sum.at[place], head_got.at[me], swap_send.at[k - 1], swap_recv.at[k - 1], peers[k - 1])
+
+    for k in range(1, n):
+        swap(k).start()
+    head_got[me] = head_sum[pl.ds(pl.multiple_of(me * count, count), count), :]
+
+    def finish(p, _):
+        total = add(0, p)
+        for k in range(1, lines):
+            second_copy(k, p).wait_recv()
+            total += landed[k - 1, piece(p)].astype(jnp.float32)
+        out[piece(p), :] = total
+        return 0
+
+    lax.fori_loop(0, pieces, finish, 0)
+    for k in range(1, n):
+        swap(k).wait_recv()
+    span = head.shape[2] // 3
+    for s in range(n):
+        for i, o in enumerate((q_out, k_out, v_out)):
+            o[:, s * span : (s + 1) * span] = head_got[s, :, i * span : (i + 1) * span].astype(jnp.float32)
+    for p in range(pieces):
+        for k in range(lines):
+            first_copy(k, p).wait_send()
+        for k in range(1, lines):
+            second_copy(k, p).wait_send()
+    for i in range(2):
+        for k in range(1, groups):
+            side_copy(i, k).wait_send()
+    for k in range(1, n):
+        swap(k).wait_send()
+
+
+def reduce_sides(part, head, wide, narrow_a, narrow_b, n, groups, pieces, collective_id):
+    _, rows, width = part.shape
+    _, blocks, outs = head.shape
+    count = blocks // n
+    experts, shard, hidden = narrow_a.shape
+    block = min(64, shard)
+    lines = n // 2
+    slots = lines + lines - 1
+    hbm = pl.BlockSpec(memory_space=ANY)
+    vmem = pl.BlockSpec(memory_space=pltpu.VMEM)
+    f32, bf = jnp.float32, jnp.bfloat16
+    grad = jax.ShapeDtypeStruct((count, n * outs // 3), f32)
+    widened = jax.ShapeDtypeStruct((shard, experts, hidden), f32)
+    return pl.pallas_call(
+        functools.partial(reduce_sides_kernel, n, groups, pieces, block),
+        out_shape=(
+            jax.ShapeDtypeStruct((rows, width), f32),
+            grad, grad, grad,
+            jax.ShapeDtypeStruct((count, wide.shape[2]), f32),
+            widened, widened,
+        ),
+        in_specs=[hbm] * 5,
+        out_specs=[vmem] * 5 + [hbm] * 2,
+        scratch_shapes=[
+            pltpu.VMEM((lines, rows, width), bf),
+            pltpu.VMEM((lines, rows, width), bf),
+            pltpu.VMEM((lines - 1, rows, width), bf),
+            pltpu.VMEM((lines - 1, rows, width), bf),
+            pltpu.VMEM((blocks, outs), bf),
+            pltpu.VMEM((groups - 1, blocks, outs), bf),
+            pltpu.VMEM((count, wide.shape[2]), bf),
+            pltpu.VMEM((groups - 1, count, wide.shape[2]), bf),
+            pltpu.VMEM((blocks, outs), bf),
+            pltpu.VMEM((n, count, outs), bf),
+            pltpu.VMEM((2, 2, experts, block, hidden), bf),
+            pltpu.VMEM((2, 2, block, experts, hidden), f32),
+            pltpu.SemaphoreType.DMA((slots, pieces)),
+            pltpu.SemaphoreType.DMA((slots, pieces)),
+            pltpu.SemaphoreType.DMA((lines, pieces)),
+            pltpu.SemaphoreType.DMA((2, groups - 1)),
+            pltpu.SemaphoreType.DMA((2, groups - 1)),
+            pltpu.SemaphoreType.DMA((2,)),
+            pltpu.SemaphoreType.DMA((n - 1,)),
+            pltpu.SemaphoreType.DMA((n - 1,)),
+            pltpu.SemaphoreType.DMA((2, 2)),
+            pltpu.SemaphoreType.DMA((2, 2)),
+        ],
+        compiler_params=pltpu.CompilerParams(
+            collective_id=collective_id, has_side_effects=True, vmem_limit_bytes=50 << 20
+        ),
+        cost_estimate=work(105),
+        name="reduce_sides",
+    )(part, head, wide, narrow_a, narrow_b)
+
+
 def gains_kernel(n, groups, sent, own, out, taken, summed, landed, send_sem, recv_sem, side_send, side_recv):
     me, group = lax.axis_index("seq"), lax.axis_index("fsdp")
     barrier = pltpu.get_barrier_semaphore()
@@ -588,16 +726,35 @@
     ]
     blocks.append((gain_own, gains.at[:, shard_rows]))
     locals_, sides = [], []
+
+    def side_copy(i, src, dst, slot, mate):
+        return pltpu.make_async_remote_copy(
+            src_ref=src, dst_ref=dst, send_sem=side_send.at[i, slot], recv_sem=side_recv.at[i, slot],
+            device_id={"fsdp": mate}, device_id_type=MESH)
+
+    def side_block(i, g):
+        place = pl.ds(pl.multiple_of(g * shard, shard), shard)
+        return gains.at[:, place] if i == 3 else w_ref.at[place, i * span : (i + 1) * span]
+
+    chips = groups // 2
+    partner = group // 2 * 2 + 1 - group % 2
+    alike = [(group + 2 * k) % groups for k in range(1, chips)]
+    behind = [(group + groups - 2 * k) % groups for k in range(1, chips)]
     for i, (src, dst) in enumerate(blocks):
-        for k in range(1, groups):
-            side = pltpu.make_async_remote_copy(
-                src_ref=src, dst_ref=dst, send_sem=side_send.at[i, k - 1], recv_sem=side_recv.at[i, k - 1],
-                device_id={"fsdp": mates[k - 1]}, device_id_type=MESH)
+        for k in range(chips):
+            side = side_copy(i, src, dst, k, partner if k == 0 else alike[k - 1])
             side.start()
             sides.append(side)
         local = pltpu.make_async_copy(src, dst, copy_sem.at[i])
         local.start()
         locals_.append(local)
+    for k in range(1, chips):
+        for i in range(4):
+            block = side_block(i, behind[k - 1])
+            side_copy(i, block, block, k, partner).wait_recv()
+            side = side_copy(i, block, block, chips + k - 1, partner)
+            side.start()
+            sides.append(side)
 
     def project(src, chunk):
         x = chunk[...].astype(jnp.float32)
@@ -626,8 +783,9 @@
             relays.append(copy)
     for copy in locals_:
         copy.wait()
-    for side in sides:
-        side.wait_recv()
+    for i in range(4):
+        for k in [0] + list(range(chips, 2 * chips - 1)):
+            side_copy(i, blocks[i][0], blocks[i][1], k, partner).wait_recv()
     project(me, own)
     for p in range(pieces):
         push(own.at[piece(p)], held.at[across, piece(p)], send_sem.at[0, p], recv_sem.at[0, p], across).wait_recv()
@@ -972,7 +1130,8 @@
     cot_own, ffn_all = barrier((cotangent.reshape(rows, width), ffn_all))
     half = rows // 2
     cot_halves = [cot_own[:half], cot_own[half:]]
-    cot_columns = [gather_column(v, n) for v in cot_halves]
+    cot_columns = [gather_column(cot_halves[0], n)]
+    cot_columns.append(gather_column(cot_halves[1], n))
     cot_others = [gather_across([v], n) for v in cot_halves]
     weights = by_place(weights, n)
     taken = weights > 0
@@ -987,16 +1146,14 @@
     unplace = lambda v: jnp.einsum("cert,ecrd->ctd", place, v, preferred_element_type=f32).astype(bf)
     received = place_rows(ffn_all).astype(bf)
     gate = jnp.einsum("ecrd,edf->ecrf", received, full_gate, preferred_element_type=f32)
-    received, gate, cot_columns[0] = barrier((received, gate, cot_columns[0]))
     cot_others[0] += gather_across(cot_columns[0], n)
+    cot_others[1] += gather_across(cot_columns[1], n)
     up_part = jnp.einsum("ecrd,edf->ecrf", received, full_up, preferred_element_type=f32)
     sigmoid_gate = jax.nn.sigmoid(gate)
     activated = gate * sigmoid_gate
     hidden = (activated * up_part).astype(bf)
     expert_out = jnp.einsum("ecrf,edf->ecrd", hidden, full_down, preferred_element_type=f32)
     expert_out = (expert_out * slot_weight).astype(bf)
-    expert_out, cot_columns[1], cot_others[0] = barrier((expert_out, cot_columns[1], cot_others[0]))
-    cot_others[1] += gather_across(cot_columns[1], n)
     ffn_part = unplace(expert_out)
     ffn_part, cot_others = barrier((ffn_part, cot_others))
     cot_all = jnp.stack(
@@ -1004,7 +1161,8 @@
     )
     lines = n // 2
     ffn_got = {k: gather_across([ffn_part[lines + k]], n)[0] for k in list(range(1, lines)) + [0]}
-    ffn_sum = lambda k: (ffn_part[k].astype(f32) + ffn_got[k].astype(f32)).astype(bf)
+    ffn_keep = [barrier(ffn_part[k]) for k in range(lines)]
+    ffn_sum = lambda k: (ffn_keep[k].astype(f32) + ffn_got[k].astype(f32)).astype(bf)
 
     out_grad = cotangent.reshape(rows, width).astype(f32)
     down_received = (place_rows(cot_all) * slot_weight).astype(bf)
@@ -1021,7 +1179,6 @@
     ffn_pieces.append(reduce_column(ffn_sum(lines - 1), lines - 1, n))
     rows_up = jnp.einsum("ecrf,edf->ecrd", up_grad, full_up, preferred_element_type=f32)
     rows_part = unplace((rows_gate + rows_up).astype(bf))
-    rows_part, down_received, hidden = barrier((rows_part, down_received, hidden))
     down_term = jnp.einsum("ecrd,ecrf->edf", down_received, hidden, preferred_element_type=f32)
     scatter = lambda v: lax.psum_scatter(v, "fsdp", scatter_dimension=1, tiled=True)
     rows_part, ffn_pieces, ffn_got[0], down_term = barrier(
@@ -1050,22 +1207,18 @@
     normed_part = jnp.einsum("te,de->td", proj_grad, w_heads, preferred_element_type=f32).astype(bf)
     head_term = jnp.einsum("td,te->de", normed, proj_grad, preferred_element_type=f32).astype(bf)
     head_term = head_term.reshape(n, groups, part, 3 * span).swapaxes(0, 1)
-    normed_part, out_term, head_term = barrier((normed_part, out_term, head_term))
-    block_out = mid + sum(piece.astype(f32) for piece in [ffn_part[0], ffn_got[0]] + ffn_pieces)
-    normed_grad = reduce_rows(normed_part.reshape(n, rows, width), n, 8, True, 7)
-    out_term, head_term, (down_sum, gate_sum, up_sum), normed_grad = barrier(
-        (out_term, head_term, scattered, normed_grad)
+    block_out = mid + sum(piece.astype(f32) for piece in [ffn_keep[0], ffn_got[0]] + ffn_pieces)
+    down_sum, gate_sum, up_sum = scattered
+    normed_grad, *head_sums, out_sum, down_sum, gate_sum = reduce_sides(
+        normed_part.reshape(n, rows, width),
+        head_term.reshape(groups, n * part, 3 * span),
+        out_term.reshape(groups, part, width),
+        down_sum, gate_sum, n, groups, 8, 7,
     )
-    out_sum = lax.psum_scatter(out_term, "fsdp", scatter_dimension=0, tiled=True).astype(f32)
-    gate_sum, up_sum, down_sum = widen(gate_sum), widen(up_sum), widen(down_sum)
+    up_sum, normed_grad = barrier((up_sum, normed_grad))
+    up_sum = widen(up_sum)
     input_back, attn_gain_term = norm_backward(inputs, inverse_norm(inputs), gain_attn, normed_grad)
     tokens_grad = mid_grad + input_back
-    head_term = lax.psum_scatter(head_term, "fsdp", scatter_dimension=0, tiled=True)
-    head_term = head_term.reshape(n, part, 3, span)
-    head_term = lax.all_to_all(head_term, "seq", split_axis=0, concat_axis=0, tiled=True)
-    head_sums = [
-        head_term[:, :, i].swapaxes(0, 1).reshape(part, width).astype(f32) for i in range(3)
-    ]
     by_span = lambda v: v.reshape(n, 1, span)
     sent_gains = jnp.concatenate([by_span(attn_gain_term), by_span(ffn_gain_term)], axis=1)
     sent_gains = jnp.pad(sent_gains, ((0, 0), (0, 6), (0, 0)))

time: 1310 us -> 1290 us (0.985)
  waiting for transfers between devices: 243 us -> 191 us
  Pallas kernels: 632 us -> 656 us
  local copies, waits for them, and re-layouts: 61.9 us -> 80.9 us
    ppermute x3, waiting for transfers between devices: 65.1 us -> 10.5 us  [reduce_column(): return lax.ppermute(v, 'seq', along_lines(n // 2, 2, n // 2 - k))]
    ppermute x6, waiting for transfers between devices: 0.02 us -> 44.5 us  [gather_column(): lax.ppermute(x, 'seq', along_lines(lines, 2, k))]
    unnamed x106 -> x146, local copies, waits for them, and re-layouts: 23.3 us -> 47.6 us
    pallas_call x1, Pallas kernels: 98.2 us -> 118 us  [reduce_terms(): pl.pallas_call(functools.partial(reduce_terms_kernel, n, pieces, tile), o...]
    pallas_call x1, Pallas kernels: 99.3 us -> 116 us  [reduce_sides(): pl.pallas_call(functools.partial(reduce_sides_kernel, n, groups, pieces,...]
    reduce_scatter x2 -> x0, waiting for transfers between devices: 16.5 us -> none  [the longest x1 11.5 us: local(): lax.psum_scatter(head_term, 'fsdp', scatter_dimension=0, tiled=True)]
    ppermute x3, starting transfers between devices: 4.43 us -> 18.6 us  [reduce_column(): return lax.ppermute(v, 'seq', along_lines(n // 2, 2, n // 2 - k))]
    pallas_call x3 -> x1, Pallas kernels: 19.9 us -> 6.69 us  [widen(): pl.pallas_call(widen_kernel, grid=(rows // step,), out_shape=jax.ShapeDty...]
  transfers between devices with their start and end apart: 32 -> 29, of which waited for: 13 -> 12; matrix products, arithmetic and copies ran while one was open for 25% -> 22% of each run, Pallas kernels for 41% -> 41%
where the time goes in v1:
time: 1290 us; the launch traced here: 1280 us
  Pallas kernels  656 us (51%)
  matrix products  253 us (20%)
  waiting for transfers between devices  191 us (15%)
  local copies, waits for them, and re-layouts  80.9 us (6%)
  starting transfers between devices  49.2 us (4%)
  other arithmetic  34.3 us (3%)
  between operations  15.6 us (1%)
    pallas_call x2, Pallas kernels, gather_rows(): pl.pallas_call(functools.partial(gather_kernel, n, pieces, by_index), out...  217 us
    pallas_call x1, Pallas kernels, project_rows(): pl.pallas_call(functools.partial(project_kernel, n, groups, pieces), out_...  120 us
    pallas_call x1, Pallas kernels, reduce_terms(): pl.pallas_call(functools.partial(reduce_terms_kernel, n, pieces, tile), o...  118 us
    pallas_call x1, Pallas kernels, reduce_sides(): pl.pallas_call(functools.partial(reduce_sides_kernel, n, groups, pieces,...  116 us
    reduce_scatter x3, waiting for transfers between devices, local(): lax.psum_scatter(v, 'fsdp', scatter_dimension=1, tiled=True)  80.1 us
    unnamed x146, local copies, waits for them, and re-layouts  47.6 us
    ppermute x6, waiting for transfers between devices, gather_column(): lax.ppermute(x, 'seq', along_lines(lines, 2, k))  44.5 us
    dot_general x2, matrix products, local(): jnp.einsum('cert,ecrd->ctd', place, v, preferred_element_type=f32)  34.1 us
  transfers between devices with their start and end apart: 29, of which 12 were waited for; matrix products, arithmetic and copies ran while one was open for 22% of the time, Pallas kernels for 41%

profile of v1, /device:TPU:0, one launch (start us, length us, event | category | flops | bytes accessed | tf_op | source)
XLA Modules:
  0.0 1279.4 jit_solution(8815926383978531678)
XLA Ops:
  8.0 5.7 copy.103
  14.0 120.1 %project_rows.1 = (bf16[2048,2048]{1,0:T(8,128)(2,1)}, f32[2048,768]{1,0:T(8,128)}, f32[16,256]{1,0:T(8,128)S(1)}, bf16[2048,768]{1,0:T(8,128)(2,1)}, f32[8,2048]{1,0:T(8,128)S(1)}) custom-call(bf16[256,2048]{1,0:T(8,128)(2,1)S(1)} %bitcast.176, bf16[512,2048]{1,0:T(8,128)(2,1)S(1)} %copy-done.23, bf16[512,2048]{1,0:T(8,128)(2,1)} %w_key.1, ...), custom_call_target="tpu_custom_call" | custom-call | flops 65999998976 | tf_op jit(solution)/shard_map/project_rows/pallas_call | solution.py:810
  134.1 3.4 copy.102
  137.6 5.5 copy.101
  144.1 3.0 copy-done.24
  147.1 11.4 rotate_rows.1
  161.6 15.9 %attend.1 = (bf16[2048,256]{1,0:T(8,128)(2,1)}, f32[2,1,2048]{2,1,0:T(1,128)}) custom-call(bf16[2048,256]{1,0:T(8,128)(2,1)} %copy-done.26, bf16[2048,256]{1,0:T(8,128)(2,1)} %copy-done.27, bf16[2048,256]{1,0:T(8,128)(2,1)} %copy-done.28), custom_call_target="tpu_custom_call" | custom-call | flops 15000000512 | tf_op jit(solution)/shard_map/attend/pallas_call | solution.py:604
  177.5 2.3 copy.57
  179.8 4.7 all-to-all-start
  187.5 20.8 %all-to-all-done = bf16[8,256,256]{1,2,0:T(8,128)(2,1)S(1)} async-done(((bf16[8,256,256]{1,2,0:T(8,128)(2,1)}), bf16[8,256,256]{1,2,0:T(8,128)(2,1)S(1)}, u32[]{:S(2)}, u32[]{:S(2)}) %all-to-all-start) | async-done | bytes 1048608 | tf_op jit(solution)/shard_map/all_to_all | solution.py:1123
  208.4 7.4 multiply_reduce_fusion.2
  218.3 107.9 %gather_rows.2 = bf16[8,256,2048]{2,1,0:T(8,128)(2,1)} custom-call(bf16[256,2048]{1,0:T(8,128)(2,1)} %multiply_convert_fusion.7.own), custom_call_target="tpu_custom_call" | custom-call | flops 62999998464 | tf_op jit(solution)/shard_map/gather_rows/pallas_call | solution.py:86
  327.3 3.0 collective-permute-start.10
  330.3 3.7 collective-permute-start.12
  336.0 2.4 collective-permute-start.8
  338.4 9.9 convert_bitcast_fusion
  348.2 21.3 %collective-permute-done.1 = bf16[128,2048]{1,0:T(8,128)(2,1)S(1)} collective-permute-done((bf16[128,2048]{1,0:T(8,128)(2,1)}, bf16[128,2048]{1,0:T(8,128)(2,1)S(1)}, u32[]{:S(2)}, u32[]{:S(2)}) %collective-permute-start.1) | collective-permute-done | bytes 524320 | tf_op jit(solution)/shard_map/ppermute | solution.py:1066
  369.5 3.0 collective-permute-start.5
  373.5 10.9 copy.61
  384.5 4.4 collective-permute-done.8
  389.9 2.0 collective-permute-start.7
  391.9 18.8 %collective-permute-done.3 = bf16[128,2048]{1,0:T(8,128)(2,1)S(1)} collective-permute-done((bf16[128,2048]{1,0:T(8,128)(2,1)}, bf16[128,2048]{1,0:T(8,128)(2,1)S(1)}, u32[]{:S(2)}, u32[]{:S(2)}) %collective-permute-start.3) | collective-permute-done | bytes 524320 | tf_op jit(solution)/shard_map/ppermute | solution.py:1066
  410.7 2.1 fusion.53
  412.9 2.0 collective-permute-start.2
  416.7 22.5 %fusion.9 = f32[4,8,96,1024]{3,2,1,0:T(8,128)} fusion(bf16[4,2048,1024]{2,1,0:T(8,128)(2,1)} %all-gather.7.cloned.1.call-done, bf16[4,8,96,2048]{3,2,0,1:T(8,128)(2,1)} %convert_bitcast_fusion), kind=kOutput, calls=%fused_computation.15 | convolution fusion | flops 12884901888 | bytes 41943040 | tf_op jit(solution)/shard_map/ecrd,edf->ecrf/dot_general | solution.py:1148
  439.3 26.6 %multiply_convert_fusion.4 = (bf16[4,8,96,1024]{3,2,1,0:T(8,128)(2,1)}, f32[4,8,96,1024]{3,2,1,0:T(8,128)}) fusion(f32[4,8,96,1024]{3,2,1,0:T(8,128)} %fusion.9, bf16[4,2048,1024]{2,1,0:T(8,128)(2,1)} %all-gather.9.cloned.1.call-done, bf16[4,8,96,2048]{3,2,0,1:T(8,128)(2,1)} %convert_bitcast_fusion), kind=kOutput, calls=%fused_computation.27 | convolution fusion | flops 12903776256 | bytes 60817408 | tf_op jit(solution)/shard_map/ecrd,edf->ecrf/dot_general | solution.py:1151
  465.8 22.0 %fusion.11 = f32[4,8,96,2048]{3,2,0,1:T(8,128)} fusion(bf16[4,2048,1024]{2,1,0:T(8,128)(2,1)} %all-gather.11.cloned.1.call-done, bf16[4,8,96,1024]{3,2,1,0:T(8,128)(2,1)} %get-tuple-element.153), kind=kOutput, calls=%fused_computation.18 | convolution fusion | flops 12884901888 | bytes 48234496 | tf_op jit(solution)/shard_map/ecrf,edf->ecrd/dot_general | solution.py:1155
  491.2 12.9 %bitcast_convert_fusion.2 = bf16[8,256,2048]{2,1,0:T(8,128)(2,1)} fusion(f32[4,8,96,2048]{3,2,0,1:T(8,128)} %fusion.11, f32[4,8,96]{2,0,1:T(4,128)S(1)} %bitcast.198, f32[8,4,256]{2,1,0:T(4,128)S(1)} %copy.59, pred[8,4,256]{2,1,0:T(4,128)(4,1)S(1)} %broadcast_compare_fusion), kind=kOutput, calls=%fused_computation.17 | convolution fusion | flops 3239575552 | bytes 33607680 | tf_op jit(solution)/shard_map/cert,ecrd->ctd/dot_general | solution.py:1146
  504.1 9.9 collective-permute-done.6
  513.9 6.7 collective-permute-done.9
  521.7 2.3 fusion.56
  523.9 2.1 fusion.57
  526.1 2.1 fusion.58
  528.2 9.8 fusion
  538.0 19.5 %bitcast_convert_fusion = bf16[4,2048,1024]{2,1,0:T(8,128)(2,1)} fusion(bf16[4,8,96,2048]{3,2,0,1:T(8,128)(2,1)} %fusion, bf16[4,8,96,1024]{3,2,1,0:T(8,128)(2,1)} %get-tuple-element.153), kind=kOutput, calls=%fused_computation.1 | convolution fusion | flops 12893290496 | bytes 35651584 | tf_op jit(solution)/shard_map/ecrd,ecrf->edf/dot_general | solution.py:1182
  557.5 5.6 slice_bitcast_fusion.7
  567.2 29.2 %multiply_convert_fusion.2 = (bf16[4,8,96,1024]{3,2,1,0:T(8,128)(2,1)}, bf16[4,8,96,1024]{3,2,1,0:T(8,128)(2,1)}) fusion(f32[4,8,96,1024]{3,2,1,0:T(8,128)} %fusion.9, f32[4,8,96,1024]{3,2,1,0:T(8,128)} %get-tuple-element.154, bf16[4,2048,1024]{2,1,0:T(8,128)(2,1)} %all-gather.11.cloned.1.call-done, bf16[4,8,96,2048]{3,2,0,1:T(8,128)(2,1)} %fusion), kind=kOutput, calls=%fused_computation.24 | convolution fusion | flops 12925796352 | bytes 67108864 | tf_op jit(solution)/shard_map/ecrd,edf->ecrf/dot_general | solution.py:1169
  596.4 15.5 %collective-permute-done.15 = bf16[256,2048]{1,0:T(8,128)(2,1)} collective-permute-done((bf16[256,2048]{1,0:T(8,128)(2,1)}, bf16[256,2048]{1,0:T(8,128)(2,1)}, u32[]{:S(2)}, u32[]{:S(2)}) %collective-permute-start.15) | collective-permute-done | bytes 1048608 | tf_op jit(solution)/shard_map/ppermute | solution.py:1070
  611.9 21.8 %fusion.7 = f32[4,8,96,2048]{3,2,1,0:T(8,128)} fusion(bf16[4,8,96,1024]{3,2,1,0:T(8,128)(2,1)} %get-tuple-element.90, bf16[4,2048,1024]{2,1,0:T(8,128)(2,1)} %all-gather.7.cloned.1.call-done), kind=kOutput, calls=%fused_computation.13 | convolution fusion | flops 12884901888 | bytes 48234496 | tf_op jit(solution)/shard_map/ecrf,edf->ecrd/dot_general | solution.py:1177
  636.0 13.8 %collective-permute-start.19 = (bf16[256,2048]{1,0:T(8,128)(2,1)S(1)}, bf16[256,2048]{1,0:T(8,128)(2,1)S(1)}, u32[]{:S(2)}, u32[]{:S(2)}) collective-permute-start(bf16[256,2048]{1,0:T(8,128)(2,1)S(1)} %add_convert_fusion.2), channel_id=1, source_target_pairs={{0,8},{4,12},{8,16},{12,20},{16,24},{20,28},{24,0},{28,4},{1,9},{5... | collective-permute-start | bytes 3145736 | tf_op jit(solution)/shard_map/ppermute | solution.py:1074
  651.4 1.9 collective-permute-start.18
  654.9 3.0 collective-permute-start.17
  657.9 21.9 %fusion.3 = f32[4,8,96,2048]{3,2,1,0:T(8,128)} fusion(bf16[4,8,96,1024]{3,2,1,0:T(8,128)(2,1)} %get-tuple-element.92, bf16[4,2048,1024]{2,1,0:T(8,128)(2,1)} %all-gather.9.cloned.1.call-done), kind=kOutput, calls=%fused_computation.9 | convolution fusion | flops 12884901888 | bytes 48234496 | tf_op jit(solution)/shard_map/ecrf,edf->ecrd/dot_general | solution.py:1180
  679.8 21.3 %bitcast_convert_fusion.1.part = bf16[8,256,2048]{2,1,0:T(8,128)(2,1)} fusion(f32[8,4,256]{2,1,0:T(4,128)S(1)} %copy-done.43, pred[8,4,256]{2,1,0:T(4,128)(4,1)S(1)} %copy-done.47, f32[4,8,96,2048]{3,2,1,0:T(8,128)} %fusion.7, f32[4,8,96,2048]{3,2,1,0:T(8,128)} %fusion.3), kind=kOutput, calls=%fused_computation.8 | convolution fusion | flops 3239575552 | bytes 58761216 | tf_op jit(solution)/shard_map/cert,ecrd->ctd/dot_general | solution.py:1146
  702.3 9.3 collective-permute-done.17
  711.6 117.7 %reduce_terms.1 = (f32[256,2048]{1,0:T(8,128)S(1)}, bf16[4,2048,1024]{2,1,0:T(8,128)(2,1)}, bf16[4,2048,1024]{2,1,0:T(8,128)(2,1)}) custom-call(bf16[8,256,2048]{2,1,0:T(8,128)(2,1)} %bitcast_convert_fusion.1.part, bf16[4,768,2048]{2,1,0:T(8,128)(2,1)} %bitcast.187, bf16[4,768,1024]{2,1,0:T(8,128)(2,1)} %bitcast.206, bf16[4,768,1024]{2,1,0:T(8,128)(2,1)} %bitcast.205), custom_call_target="tpu_custom_call" | custom-call | flops 62999998464 | tf_op jit(solution)/shard_map/reduce_terms/pallas_call | solution.py:232
  832.2 2.8 multiply_reduce_fusion
  835.0 3.0 fusion.75.own
  837.9 109.3 %gather_rows.3 = bf16[8,256,2048]{2,1,0:T(8,128)(2,1)} custom-call(bf16[256,2048]{1,0:T(8,128)(2,1)} %fusion.75.own), custom_call_target="tpu_custom_call" | custom-call | flops 62999998464 | tf_op jit(solution)/shard_map/gather_rows/pallas_call | solution.py:86
  947.2 7.1 convolution_convert_fusion.3.g_ref
  954.3 22.1 %attend_back.1 = (bf16[2048,256]{1,0:T(8,128)(2,1)}, bf16[2048,256]{1,0:T(8,128)(2,1)}, bf16[2048,256]{1,0:T(8,128)(2,1)}) custom-call(bf16[2048,256]{1,0:T(8,128)(2,1)} %copy-done.26, bf16[2048,256]{1,0:T(8,128)(2,1)} %copy-done.27, bf16[2048,256]{1,0:T(8,128)(2,1)} %copy-done.28, bf16[2048,256]{1,0:T(8,128)(2,1)} %convolution_convert_fusion.3.g_ref, ...), custom_call_target="tpu_custom_call" | custom-call | flops 35999997952 | tf_op jit(solution)/shard_map/attend_back/pallas_call | solution.py:671
  976.5 4.3 copy-done.25
  984.5 17.5 %heads_back.1 = (bf16[2048,768]{1,0:T(8,128)(2,1)S(1)}, f32[8,256]{1,0:T(8,128)S(1)}) custom-call(bf16[2048,256]{1,0:T(8,128)(2,1)S(1)} %copy-done.29, bf16[2048,256]{1,0:T(8,128)(2,1)S(1)} %copy-done.30, bf16[2048,256]{1,0:T(8,128)(2,1)S(1)} %copy-done.31, f32[2048,768]{1,0:T(8,128)S(1)} %copy-done.25, f32[16,256]{1,0:T(8,128)S(1)} %get-tuple-element.107.factors, ...), custom_call_target="tpu_custom_call" | custom-call | flops 12000000000 | tf_op jit(solution)/shard_map/heads_back/pallas_call | solution.py:1004
  1002.1 9.5 convolution_convert_fusion.1
  1013.6 2.3 convolution_convert_fusion.2
  1015.9 9.2 convolution_convert_fusion
  1025.2 57.3 %reduce-scatter.6.cloned.1.call-done.narrow_a = bf16[4,512,1024]{2,1,0:T(8,128)(2,1)} async-done(((bf16[4,2048,1024]{2,1,0:T(8,128)(2,1)}), bf16[4,512,1024]{2,1,0:T(8,128)(2,1)}) %reduce-scatter.6.cloned.1.call-update) | async-done | bytes 4194320 | tf_op jit(solution)/shard_map/reduce_scatter | solution.py:1183
  1082.5 115.9 %reduce_sides.1 = (f32[256,2048]{1,0:T(8,128)}, f32[64,2048]{1,0:T(8,128)S(1)}, f32[64,2048]{1,0:T(8,128)S(1)}, f32[64,2048]{1,0:T(8,128)S(1)}, f32[64,2048]{1,0...) custom-call(bf16[8,256,2048]{2,1,0:T(8,128)(2,1)} %bitcast.204, bf16[4,512,768]{2,1,0:T(8,128)(2,1)} %bitcast.190, ...), custom_call_target="tpu_custom_call" | custom-call | flops 62999998464 | tf_op jit(solution)/shard_map/reduce_sides/pallas_call | solution.py:431
  1201.6 22.8 %reduce-scatter.4.cloned.1.call-done.x_ref = bf16[4,512,1024]{2,1,0:T(8,128)(2,1)} async-done(((bf16[4,2048,1024]{2,1,0:T(8,128)(2,1)}), bf16[4,512,1024]{2,1,0:T(8,128)(2,1)}) %reduce-scatter.4.cloned.1.call-update) | async-done | bytes 4194320 | tf_op jit(solution)/shard_map/reduce_scatter | solution.py:1183
  1224.4 6.7 widen.1
  1232.4 11.1 sum_gains.1
  1244.9 6.4 fusion.40
  1254.5 8.8 copy.121
  1263.3 8.8 copy.122
  (227 shorter events, 49.9 us)
Async XLA Ops:
  7.2 201.2 %all-gather.5.cloned.1.call-start = ((), (), s32[]{:S(2)}) async-start(), calls=%async_computation.4 | async-start | bytes 10485760 | tf_op jit(solution)/shard_map/all_gather | solution.py:1102
  8.0 408.7 %all-gather.7.cloned.1.call-start = ((), (), s32[]{:S(2)}) async-start(), calls=%async_computation.5 | async-start | bytes 20971520 | tf_op jit(solution)/shard_map/all_gather | solution.py:1103
  13.8 425.5 %all-gather.9.cloned.1.call-start = ((), (), s32[]{:S(2)}) async-start(), calls=%async_computation.6 | async-start | bytes 20971520 | tf_op jit(solution)/shard_map/all_gather | solution.py:1103
  14.0 120.1 %copy-start.38 = (bf16[512,4,1024]{2,1,0:T(4,128)(2,1)S(1)}, bf16[512,4,1024]{2,1,0:T(4,128)(2,1)}, u32[]{:S(2)}) copy-start(bf16[512,4,1024]{2,1,0:T(4,128)(2,1)} %param.28) | copy-start | bytes 12582916
  137.5 328.3 %all-gather.11.cloned.1.call-start = ((), (), s32[]{:S(2)}) async-start(), calls=%async_computation.7 | async-start | bytes 20971520 | tf_op jit(solution)/shard_map/all_gather | solution.py:1103
  143.4 15.1 %copy-start.21 = (f32[2,256]{1,0:T(2,128)}, f32[2,256]{1,0:T(2,128)S(1)}, u32[]{:S(2)}) copy-start(f32[2,256]{1,0:T(2,128)S(1)} %constant_dynamic-slice_fusion.1.gains) | copy-start | bytes 6148
  143.5 15.0 %copy-start.17 = (f32[8,128]{1,0:T(8,128)}, f32[8,128]{1,0:T(8,128)S(1)}, u32[]{:S(2)}) copy-start(f32[8,128]{1,0:T(8,128)S(1)} %get-tuple-element.147.far_sin) | copy-start | bytes 12292
  143.5 15.0 %copy-start.19 = (f32[8,128]{1,0:T(8,128)}, f32[8,128]{1,0:T(8,128)S(1)}, u32[]{:S(2)}) copy-start(f32[8,128]{1,0:T(8,128)S(1)} %get-tuple-element.148.far_cos) | copy-start | bytes 12292
  144.1 14.5 %copy-start.13 = (f32[256,128]{1,0:T(8,128)}, f32[256,128]{1,0:T(8,128)S(1)}, u32[]{:S(2)}) copy-start(f32[256,128]{1,0:T(8,128)S(1)} %get-tuple-element.149.near_sin) | copy-start | bytes 393220
  144.1 14.5 %copy-start.15 = (f32[256,128]{1,0:T(8,128)}, f32[256,128]{1,0:T(8,128)S(1)}, u32[]{:S(2)}) copy-start(f32[256,128]{1,0:T(8,128)S(1)} %get-tuple-element.150.near_cos) | copy-start | bytes 393220
  179.8 28.6 %all-to-all-start = ((bf16[8,256,256]{1,2,0:T(8,128)(2,1)}), bf16[8,256,256]{1,2,0:T(8,128)(2,1)S(1)}, u32[]{:S(2)}, u32[]{:S(2)}) async-start(bf16[8,256,256]{1,2,0:T(8,128)(2,1)} %copy.57), calls=%async_computation | async-start | bytes 2097152 | tf_op jit(solution)/shard_map/all_to_all | solution.py:1123
  184.5 840.7 %reduce-scatter.8.cloned.1.call-start = ((), (), s32[]{:S(2)}) async-start(), calls=%async_computation.10 | async-start | bytes 20971520 | tf_op jit(solution)/shard_map/reduce_scatter | solution.py:1183
  185.3 342.9 %copy-start.46 = (pred[8,4,256]{2,1,0:T(4,128)(4,1)}, pred[8,4,256]{2,1,0:T(4,128)(4,1)S(1)}, u32[]{:S(2)}) copy-start(pred[8,4,256]{2,1,0:T(4,128)(4,1)S(1)} %broadcast_compare_fusion) | copy-start | bytes 24580
  185.5 342.7 %copy-start.42 = (f32[8,4,256]{2,1,0:T(4,128)}, f32[8,4,256]{2,1,0:T(4,128)S(1)}, u32[]{:S(2)}) copy-start(f32[8,4,256]{2,1,0:T(4,128)S(1)} %copy.59) | copy-start | bytes 98308
  187.5 28.2 %copy-start.48 = (f32[1,2048]{1,0:T(1,128)}, f32[1,2048]{1,0:T(1,128)S(1)}, u32[]{:S(2)}) copy-start(f32[1,2048]{1,0:T(1,128)S(1)} %get-tuple-element.142) | copy-start | bytes 24580
  215.7 110.5 %copy-start.54 = (f32[256]{0:T(256)}, f32[256]{0:T(256)S(1)}, u32[]{:S(2)}) copy-start(f32[256]{0:T(256)S(1)} %add_rsqrt_fusion.1) | copy-start | bytes 3076
  218.3 108.0 %copy-start.35 = (bf16[1,256,2048]{2,1,0:T(8,128)(2,1)S(1)}, bf16[1,256,2048]{2,1,0:T(8,128)(2,1)}, u32[]{:S(2)}) copy-start(bf16[1,256,2048]{2,1,0:T(8,128)(2,1)} %param.18) | copy-start | bytes 3145732
  327.3 62.6 %collective-permute-start.10 = (bf16[128,2048]{1,0:T(8,128)(2,1)}, bf16[128,2048]{1,0:T(8,128)(2,1)}, u32[]{:S(2)}, u32[]{:S(2)}) collective-permute-start(bf16[128,2048]{1,0:T(8,128)(2,1)} %get-tuple-element.140), channel_id=1, source_target_pairs={{0,16},{4,20},{8,24},{12,28},{16,0},{20,4},{24,8},{28,12},{1,17},{... | collective-permute-start | bytes 1572872 | tf_op jit(solution)/shard_map/ppermute | solution.py:1066
  330.3 82.6 %collective-permute-start.12 = (bf16[128,2048]{1,0:T(8,128)(2,1)}, bf16[128,2048]{1,0:T(8,128)(2,1)S(1)}, u32[]{:S(2)}, u32[]{:S(2)}) collective-permute-start(bf16[128,2048]{1,0:T(8,128)(2,1)} %get-tuple-element.140), channel_id=1, source_target_pairs={{0,24},{4,28},{8,0},{12,4},{16,8},{20,12},{24,16},{28,20},{1,25},{... | collective-permute-start | bytes 1572872 | tf_op jit(solution)/shard_map/ppermute | solution.py:1066
  334.0 35.6 %collective-permute-start.1 = (bf16[128,2048]{1,0:T(8,128)(2,1)}, bf16[128,2048]{1,0:T(8,128)(2,1)S(1)}, u32[]{:S(2)}, u32[]{:S(2)}) collective-permute-start(bf16[128,2048]{1,0:T(8,128)(2,1)} %get-tuple-element.139), channel_id=1, source_target_pairs={{0,8},{4,12},{8,16},{12,20},{16,24},{20,28},{24,0},{28,4},{1,9},{5... | collective-permute-start | bytes 1572872 | tf_op jit(solution)/shard_map/ppermute | solution.py:1066
  334.6 76.2 %collective-permute-start.3 = (bf16[128,2048]{1,0:T(8,128)(2,1)}, bf16[128,2048]{1,0:T(8,128)(2,1)S(1)}, u32[]{:S(2)}, u32[]{:S(2)}) collective-permute-start(bf16[128,2048]{1,0:T(8,128)(2,1)} %get-tuple-element.139), channel_id=1, source_target_pairs={{0,16},{4,20},{8,24},{12,28},{16,0},{20,4},{24,8},{28,12},{1,17},{... | collective-permute-start | bytes 1572872 | tf_op jit(solution)/shard_map/ppermute | solution.py:1066
  336.0 52.9 %collective-permute-start.8 = (bf16[128,2048]{1,0:T(8,128)(2,1)}, bf16[128,2048]{1,0:T(8,128)(2,1)S(1)}, u32[]{:S(2)}, u32[]{:S(2)}) collective-permute-start(bf16[128,2048]{1,0:T(8,128)(2,1)} %get-tuple-element.140), channel_id=1, source_target_pairs={{0,8},{4,12},{8,16},{12,20},{16,24},{20,28},{24,0},{28,4},{1,9},{5... | collective-permute-start | bytes 1572872 | tf_op jit(solution)/shard_map/ppermute | solution.py:1066
  369.5 45.4 %collective-permute-start.5 = (bf16[128,2048]{1,0:T(8,128)(2,1)}, bf16[128,2048]{1,0:T(8,128)(2,1)S(1)}, u32[]{:S(2)}, u32[]{:S(2)}) collective-permute-start(bf16[128,2048]{1,0:T(8,128)(2,1)} %get-tuple-element.139), channel_id=1, source_target_pairs={{0,24},{4,28},{8,0},{12,4},{16,8},{20,12},{24,16},{28,20},{1,25},{... | collective-permute-start | bytes 1572872 | tf_op jit(solution)/shard_map/ppermute | solution.py:1066
  388.9 99.0 %collective-permute-start = (bf16[128,2048]{1,0:T(8,128)(2,1)}, bf16[128,2048]{1,0:T(8,128)(2,1)S(1)}, u32[]{:S(2)}, u32[]{:S(2)}) collective-permute-start(bf16[128,2048]{1,0:T(8,128)(2,1)} %get-tuple-element.139), channel_id=1, source_target_pairs={{0,4},{4,0},{8,12},{12,8},{16,20},{20,16},{24,28},{28,24},{1,5},{5... | collective-permute-start | bytes 1572872 | tf_op jit(solution)/shard_map/ppermute | solution.py:1070
  389.9 99.2 %collective-permute-start.7 = (bf16[128,2048]{1,0:T(8,128)(2,1)}, bf16[128,2048]{1,0:T(8,128)(2,1)S(1)}, u32[]{:S(2)}, u32[]{:S(2)}) collective-permute-start(bf16[128,2048]{1,0:T(8,128)(2,1)} %get-tuple-element.140), channel_id=1, source_target_pairs={{0,4},{4,0},{8,12},{12,8},{16,20},{20,16},{24,28},{28,24},{1,5},{5... | collective-permute-start | bytes 1572872 | tf_op jit(solution)/shard_map/ppermute | solution.py:1070
  410.7 79.2 %collective-permute-start.11 = (bf16[128,2048]{1,0:T(8,128)(2,1)}, bf16[128,2048]{1,0:T(8,128)(2,1)}, u32[]{:S(2)}, u32[]{:S(2)}) collective-permute-start(bf16[128,2048]{1,0:T(8,128)(2,1)} %collective-permute-done.10), channel_id=1, source_target_pairs={{0,4},{4,0},{8,12},{12,8},{16,20},{20,16},{24,28},{28,24},{1,5},{5... | collective-permute-start | bytes 1572872 | tf_op jit(solution)/shard_map/ppermute | solution.py:1070
  412.9 91.2 %collective-permute-start.2 = (bf16[128,2048]{1,0:T(8,128)(2,1)S(1)}, bf16[128,2048]{1,0:T(8,128)(2,1)}, u32[]{:S(2)}, u32[]{:S(2)}) collective-permute-start(bf16[128,2048]{1,0:T(8,128)(2,1)S(1)} %collective-permute-done.1), channel_id=1, source_target_pairs={{0,4},{4,0},{8,12},{12,8},{16,20},{20,16},{24,28},{28,24},{1,5},{5... | collective-permute-start | bytes 1572872 | tf_op jit(solution)/shard_map/ppermute | solution.py:1070
  414.9 89.2 %collective-permute-start.13 = (bf16[128,2048]{1,0:T(8,128)(2,1)S(1)}, bf16[128,2048]{1,0:T(8,128)(2,1)}, u32[]{:S(2)}, u32[]{:S(2)}) collective-permute-start(bf16[128,2048]{1,0:T(8,128)(2,1)S(1)} %collective-permute-done.12), channel_id=1, source_target_pairs={{0,4},{4,0},{8,12},{12,8},{16,20},{20,16},{24,28},{28,24},{1,5},{5... | collective-permute-start | bytes 1572872 | tf_op jit(solution)/shard_map/ppermute | solution.py:1070
  465.8 23.3 %copy-start.45 = (bf16[128,2048]{1,0:T(8,128)(2,1)S(1)}, bf16[128,2048]{1,0:T(8,128)(2,1)}, u32[]{:S(2)}) copy-start(bf16[128,2048]{1,0:T(8,128)(2,1)} %copy-done.44) | copy-start | bytes 1572868
  465.8 25.4 %copy-start.52 = (f32[8,4,96]{2,1,0:T(4,128)S(1)}, f32[8,4,96]{2,1,0:T(4,128)}, u32[]{:S(2)}) copy-start(f32[8,4,96]{2,1,0:T(4,128)} %select_reduce_fusion) | copy-start | bytes 36868
  487.9 16.2 %collective-permute-start.4 = (bf16[128,2048]{1,0:T(8,128)(2,1)S(1)}, bf16[128,2048]{1,0:T(8,128)(2,1)S(1)}, u32[]{:S(2)}, u32[]{:S(2)}) collective-permute-start(bf16[128,2048]{1,0:T(8,128)(2,1)S(1)} %collective-permute-done.3), channel_id=1, source_target_pairs={{0,4},{4,0},{8,12},{12,8},{16,20},{20,16},{24,28},{28,24},{1,5},{5... | collective-permute-start | bytes 1572872 | tf_op jit(solution)/shard_map/ppermute | solution.py:1070
  489.2 24.8 %collective-permute-start.6 = (bf16[128,2048]{1,0:T(8,128)(2,1)S(1)}, bf16[128,2048]{1,0:T(8,128)(2,1)S(1)}, u32[]{:S(2)}, u32[]{:S(2)}) collective-permute-start(bf16[128,2048]{1,0:T(8,128)(2,1)S(1)} %copy-done.45), channel_id=1, source_target_pairs={{0,4},{4,0},{8,12},{12,8},{16,20},{20,16},{24,28},{28,24},{1,5},{5... | collective-permute-start | bytes 1572872 | tf_op jit(solution)/shard_map/ppermute | solution.py:1070
  490.0 30.7 %collective-permute-start.9 = (bf16[128,2048]{1,0:T(8,128)(2,1)S(1)}, bf16[128,2048]{1,0:T(8,128)(2,1)}, u32[]{:S(2)}, u32[]{:S(2)}) collective-permute-start(bf16[128,2048]{1,0:T(8,128)(2,1)S(1)} %collective-permute-done.8), channel_id=1, source_target_pairs={{0,4},{4,0},{8,12},{12,8},{16,20},{20,16},{24,28},{28,24},{1,5},{5... | collective-permute-start | bytes 1572872 | tf_op jit(solution)/shard_map/ppermute | solution.py:1070
  563.1 33.3 %collective-permute-start.14 = (bf16[256,2048]{1,0:T(8,128)(2,1)}, bf16[256,2048]{1,0:T(8,128)(2,1)}, u32[]{:S(2)}, u32[]{:S(2)}) collective-permute-start(bf16[256,2048]{1,0:T(8,128)(2,1)} %get-tuple-element.136), channel_id=1, source_target_pairs={{0,4},{4,0},{8,12},{12,8},{16,20},{20,16},{24,28},{28,24},{1,5},{5... | collective-permute-start | bytes 3145736 | tf_op jit(solution)/shard_map/ppermute | solution.py:1070
  564.1 47.9 %collective-permute-start.15 = (bf16[256,2048]{1,0:T(8,128)(2,1)}, bf16[256,2048]{1,0:T(8,128)(2,1)}, u32[]{:S(2)}, u32[]{:S(2)}) collective-permute-start(bf16[256,2048]{1,0:T(8,128)(2,1)} %get-tuple-element.135), channel_id=1, source_target_pairs={{0,4},{4,0},{8,12},{12,8},{16,20},{20,16},{24,28},{28,24},{1,5},{5... | collective-permute-start | bytes 3145736 | tf_op jit(solution)/shard_map/ppermute | solution.py:1070
  565.1 69.3 %collective-permute-start.16 = (bf16[256,2048]{1,0:T(8,128)(2,1)}, bf16[256,2048]{1,0:T(8,128)(2,1)}, u32[]{:S(2)}, u32[]{:S(2)}) collective-permute-start(bf16[256,2048]{1,0:T(8,128)(2,1)} %get-tuple-element.134), channel_id=1, source_target_pairs={{0,4},{4,0},{8,12},{12,8},{16,20},{20,16},{24,28},{28,24},{1,5},{5... | collective-permute-start | bytes 3145736 | tf_op jit(solution)/shard_map/ppermute | solution.py:1070
  566.1 135.0 %collective-permute-start.20 = (bf16[256,2048]{1,0:T(8,128)(2,1)}, bf16[256,2048]{1,0:T(8,128)(2,1)}, u32[]{:S(2)}, u32[]{:S(2)}) collective-permute-start(bf16[256,2048]{1,0:T(8,128)(2,1)} %get-tuple-element.130), channel_id=1, source_target_pairs={{0,4},{4,0},{8,12},{12,8},{16,20},{20,16},{24,28},{28,24},{1,5},{5... | collective-permute-start | bytes 3145736 | tf_op jit(solution)/shard_map/ppermute | solution.py:1070
  636.0 65.1 %collective-permute-start.19 = (bf16[256,2048]{1,0:T(8,128)(2,1)S(1)}, bf16[256,2048]{1,0:T(8,128)(2,1)S(1)}, u32[]{:S(2)}, u32[]{:S(2)}) collective-permute-start(bf16[256,2048]{1,0:T(8,128)(2,1)S(1)} %add_convert_fusion.2), channel_id=1, source_target_pairs={{0,8},{4,12},{8,16},{12,20},{16,24},{20,28},{24,0},{28,4},{1,9},{5... | collective-permute-start | bytes 3145736 | tf_op jit(solution)/shard_map/ppermute | solution.py:1074
  651.4 50.9 %collective-permute-start.18 = (bf16[256,2048]{1,0:T(8,128)(2,1)S(1)}, bf16[256,2048]{1,0:T(8,128)(2,1)S(1)}, u32[]{:S(2)}, u32[]{:S(2)}) collective-permute-start(bf16[256,2048]{1,0:T(8,128)(2,1)S(1)} %add_convert_fusion.3), channel_id=1, source_target_pairs={{0,16},{4,20},{8,24},{12,28},{16,0},{20,4},{24,8},{28,12},{1,17},{... | collective-permute-start | bytes 3145736 | tf_op jit(solution)/shard_map/ppermute | solution.py:1074
  654.9 24.9 %copy-start.43 = (f32[8,4,256]{2,1,0:T(4,128)S(1)}, f32[8,4,256]{2,1,0:T(4,128)}, u32[]{:S(2)}) copy-start(f32[8,4,256]{2,1,0:T(4,128)} %copy-done.42) | copy-start | bytes 98308
  654.9 24.9 %copy-start.47 = (pred[8,4,256]{2,1,0:T(4,128)(4,1)S(1)}, pred[8,4,256]{2,1,0:T(4,128)(4,1)}, u32[]{:S(2)}) copy-start(pred[8,4,256]{2,1,0:T(4,128)(4,1)} %copy-done.46) | copy-start | bytes 24580
  654.9 56.7 %collective-permute-start.17 = (bf16[256,2048]{1,0:T(8,128)(2,1)S(1)}, bf16[256,2048]{1,0:T(8,128)(2,1)S(1)}, u32[]{:S(2)}, u32[]{:S(2)}) collective-permute-start(bf16[256,2048]{1,0:T(8,128)(2,1)S(1)} %add_convert_fusion.4), channel_id=1, source_target_pairs={{0,24},{4,28},{8,0},{12,4},{16,8},{20,12},{24,16},{28,20},{1,25},{... | collective-permute-start | bytes 3145736 | tf_op jit(solution)/shard_map/ppermute | solution.py:1074
  701.1 128.3 %copy-start.39 = (bf16[256,2048]{1,0:T(8,128)(2,1)}, bf16[256,2048]{1,0:T(8,128)(2,1)S(1)}, u32[]{:S(2)}) copy-start(bf16[256,2048]{1,0:T(8,128)(2,1)S(1)} %collective-permute-done.19) | copy-start | bytes 3145732
  702.3 127.1 %copy-start.40 = (bf16[256,2048]{1,0:T(8,128)(2,1)}, bf16[256,2048]{1,0:T(8,128)(2,1)S(1)}, u32[]{:S(2)}) copy-start(bf16[256,2048]{1,0:T(8,128)(2,1)S(1)} %collective-permute-done.18) | copy-start | bytes 3145732
  711.6 117.8 %copy-start.41 = (bf16[256,2048]{1,0:T(8,128)(2,1)}, bf16[256,2048]{1,0:T(8,128)(2,1)S(1)}, u32[]{:S(2)}) copy-start(bf16[256,2048]{1,0:T(8,128)(2,1)S(1)} %collective-permute-done.17) | copy-start | bytes 3145732
  829.4 253.0 %reduce-scatter.6.cloned.1.call-start = ((), (), s32[]{:S(2)}) async-start(), calls=%async_computation.9 | async-start | bytes 20971520 | tf_op jit(solution)/shard_map/reduce_scatter | solution.py:1183
  830.0 394.3 %reduce-scatter.4.cloned.1.call-start = ((), (), s32[]{:S(2)}) async-start(), calls=%async_computation.8 | async-start | bytes 20971520 | tf_op jit(solution)/shard_map/reduce_scatter | solution.py:1183
  835.0 112.3 %copy-start.58 = (f32[256]{0:T(256)}, f32[256]{0:T(256)S(1)}, u32[]{:S(2)}) copy-start(f32[256]{0:T(256)S(1)} %broadcast_multiply_fusion.1) | copy-start | bytes 3076
  954.3 22.1 %copy-start.14 = (f32[256,128]{1,0:T(8,128)S(1)}, f32[256,128]{1,0:T(8,128)}, u32[]{:S(2)}) copy-start(f32[256,128]{1,0:T(8,128)} %copy-done.13) | copy-start | bytes 393220
  954.3 22.1 %copy-start.16 = (f32[256,128]{1,0:T(8,128)S(1)}, f32[256,128]{1,0:T(8,128)}, u32[]{:S(2)}) copy-start(f32[256,128]{1,0:T(8,128)} %copy-done.15) | copy-start | bytes 393220
  954.3 22.1 %copy-start.18 = (f32[8,128]{1,0:T(8,128)S(1)}, f32[8,128]{1,0:T(8,128)}, u32[]{:S(2)}) copy-start(f32[8,128]{1,0:T(8,128)} %copy-done.17) | copy-start | bytes 12292
  954.3 22.1 %copy-start.20 = (f32[8,128]{1,0:T(8,128)S(1)}, f32[8,128]{1,0:T(8,128)}, u32[]{:S(2)}) copy-start(f32[8,128]{1,0:T(8,128)} %copy-done.19) | copy-start | bytes 12292
  954.3 22.1 %copy-start.22 = (f32[2,256]{1,0:T(2,128)S(1)}, f32[2,256]{1,0:T(2,128)}, u32[]{:S(2)}) copy-start(f32[2,256]{1,0:T(2,128)} %copy-done.21) | copy-start | bytes 6148
  984.5 29.0 %slice-start = ((s8[8388608]{0:T(1024)(128)(4,1)}), s8[4194304]{0:T(1024)(128)(4,1)S(1)}, s32[]{:S(2)}) async-start(s8[8388608]{0:T(1024)(128)(4,1)} %bitcast.179), calls=%async_computation.11 | async-start | bytes 8388608
  1002.1 9.6 copy-start.32
  1002.1 11.4 slice-start.1
  1224.4 7.4 copy-start.53
  1232.4 12.4 copy-start.1
  1232.4 12.4 copy-start.50
  1232.4 12.4 copy-start.56
  1232.4 12.4 copy-start.59
  1244.9 7.2 copy-start.10
  1244.9 8.0 copy-start.8
  1244.9 8.8 copy-start.6
  (34 other events, 118.4 us)
Sparse Core Ops, SparseCore 0:
  9.5 75.4 all-gather.4
  87.2 104.6 all-gather.6
  194.0 105.8 all-gather.8
  301.4 105.8 all-gather.10
  829.6 125.3 reduce-scatter.7
  957.4 125.0 reduce-scatter.5
  1085.1 139.2 reduce-scatter.3

commit v2 on v1

--- a/solution.py
+++ b/solution.py
@@ -258,10 +258,9 @@
 
 
 def reduce_sides_kernel(
-    n, groups, pieces, block, part, head, wide, narrow_a, narrow_b,
-    out, q_out, k_out, v_out, o_out, wide_a, wide_b,
-    mine, got, sums, landed, head_own, head_land, wide_own, wide_land, head_sum, head_got, x_buf, o_buf,
-    send_sem, recv_sem, load_sem, side_send, side_recv, side_load, swap_send, swap_recv, x_sem, o_sem
+    n, groups, pieces, part, head, wide, out, q_out, k_out, v_out, o_out,
+    mine, got, sums, landed, head_own, head_land, wide_own, wide_land, head_sum, head_got,
+    send_sem, recv_sem, load_sem, side_send, side_recv, side_load, swap_send, swap_recv
 ):
     pair = 2
     lines = n // pair
@@ -277,8 +276,6 @@
         pl.semaphore_signal(barrier, inc=1, device_id={"fsdp": mate}, device_id_type=MESH)
     pl.semaphore_wait(barrier, n - 1 + groups - 1)
     rows = out.shape[0] // pieces
-    experts, shard, _ = narrow_a.shape
-    blocks = shard // block
 
     def piece(p):
         return pl.ds(pl.multiple_of(p * rows, rows), rows)
@@ -302,16 +299,6 @@
             src_ref=src.at[mates[k - 1]], dst_ref=dst.at[k - 1],
             send_sem=side_send.at[i, k - 1], recv_sem=side_recv.at[i, k - 1],
             device_id={"fsdp": mates[k - 1]}, device_id_type=MESH)
-
-    def job_refs(j, i):
-        place = pl.ds(pl.multiple_of(j * block, block), block)
-        return (narrow_a, narrow_b)[i].at[:, place, :], (wide_a, wide_b)[i].at[place]
-
-    def x_copy(j, i):
-        return pltpu.make_async_copy(job_refs(j, i)[0], x_buf.at[j % 2, i], x_sem.at[j % 2, i])
-
-    def o_copy(j, i):
-        return pltpu.make_async_copy(o_buf.at[j % 2, i], job_refs(j, i)[1], o_sem.at[j % 2, i])
 
     for k in list(range(1, lines)) + [0]:
         for p in range(pieces):
@@ -326,47 +313,19 @@
     for i in range(2):
         for k in range(1, groups):
             side_copy(i, k).start()
-        x_copy(0, i).start()
 
     def add(k, p):
         first_copy(k, p).wait_recv()
         load(k, p).wait()
         return mine[k, piece(p)].astype(jnp.float32) + got[k, piece(p)].astype(jnp.float32)
 
-    def step(s):
+    def step(s, _):
         k, p = 1 + s // pieces, s % pieces
         sums[k - 1, piece(p)] = add(k, p).astype(jnp.bfloat16)
         second_copy(k, p).start()
-
-    def job(j, i):
-        @pl.when(j + 1 < blocks)
-        def _():
-            x_copy(j + 1, i).start()
-
-        @pl.when(j >= 2)
-        def _():
-            o_copy(j - 2, i).wait()
-
-        x_copy(j, i).wait()
-        for e in range(experts):
-            o_buf[j % 2, i, :, e, :] = x_buf[j % 2, i, e].astype(jnp.float32)
-        o_copy(j, i).start()
-
-    per = (lines - 1) * pieces // blocks
-
-    def both(t, _):
-        for i in range(per):
-            step(t * per + i)
-            if i == 0:
-                job(t, 0)
-            if i == per - 1:
-                job(t, 1)
         return 0
 
-    lax.fori_loop(0, blocks, both, 0)
-    for i in range(2):
-        for j in range(max(0, blocks - 2), blocks):
-            o_copy(j, i).wait()
+    lax.fori_loop(0, (lines - 1) * pieces, step, 0)
 
     for copy in own_copies:
         copy.wait()
@@ -415,29 +374,25 @@
         swap(k).wait_send()
 
 
-def reduce_sides(part, head, wide, narrow_a, narrow_b, n, groups, pieces, collective_id):
+def reduce_sides(part, head, wide, n, groups, pieces, collective_id):
     _, rows, width = part.shape
     _, blocks, outs = head.shape
     count = blocks // n
-    experts, shard, hidden = narrow_a.shape
-    block = min(64, shard)
     lines = n // 2
     slots = lines + lines - 1
     hbm = pl.BlockSpec(memory_space=ANY)
     vmem = pl.BlockSpec(memory_space=pltpu.VMEM)
     f32, bf = jnp.float32, jnp.bfloat16
     grad = jax.ShapeDtypeStruct((count, n * outs // 3), f32)
-    widened = jax.ShapeDtypeStruct((shard, experts, hidden), f32)
     return pl.pallas_call(
-        functools.partial(reduce_sides_kernel, n, groups, pieces, block),
+        functools.partial(reduce_sides_kernel, n, groups, pieces),
         out_shape=(
             jax.ShapeDtypeStruct((rows, width), f32),
             grad, grad, grad,
             jax.ShapeDtypeStruct((count, wide.shape[2]), f32),
-            widened, widened,
         ),
-        in_specs=[hbm] * 5,
-        out_specs=[vmem] * 5 + [hbm] * 2,
+        in_specs=[hbm] * 3,
+        out_specs=[vmem] * 5,
         scratch_shapes=[
             pltpu.VMEM((lines, rows, width), bf),
             pltpu.VMEM((lines, rows, width), bf),
@@ -449,8 +404,6 @@
             pltpu.VMEM((groups - 1, count, wide.shape[2]), bf),
             pltpu.VMEM((blocks, outs), bf),
             pltpu.VMEM((n, count, outs), bf),
-            pltpu.VMEM((2, 2, experts, block, hidden), bf),
-            pltpu.VMEM((2, 2, block, experts, hidden), f32),
             pltpu.SemaphoreType.DMA((slots, pieces)),
             pltpu.SemaphoreType.DMA((slots, pieces)),
             pltpu.SemaphoreType.DMA((lines, pieces)),
@@ -459,15 +412,13 @@
             pltpu.SemaphoreType.DMA((2,)),
             pltpu.SemaphoreType.DMA((n - 1,)),
             pltpu.SemaphoreType.DMA((n - 1,)),
-            pltpu.SemaphoreType.DMA((2, 2)),
-            pltpu.SemaphoreType.DMA((2, 2)),
         ],
         compiler_params=pltpu.CompilerParams(
             collective_id=collective_id, has_side_effects=True, vmem_limit_bytes=50 << 20
         ),
         cost_estimate=work(105),
         name="reduce_sides",
-    )(part, head, wide, narrow_a, narrow_b)
+    )(part, head, wide)
 
 
 def gains_kernel(n, groups, sent, own, out, taken, summed, landed, send_sem, recv_sem, side_send, side_recv):
@@ -527,6 +478,111 @@
     )(sent, own)
 
 
+def slots_of(w, experts, capacity):
+    tokens = w.shape[1]
+    taken = w > 0
+    before = lax.broadcasted_iota(jnp.int32, (tokens, tokens), 0) <= lax.broadcasted_iota(jnp.int32, (tokens, tokens), 1)
+    rank = jnp.dot(
+        taken.astype(jnp.float32).astype(jnp.bfloat16), before.astype(jnp.float32).astype(jnp.bfloat16),
+        preferred_element_type=jnp.float32,
+    )
+    rank = jnp.where(taken, rank - 1.0, -1.0)
+    slot = lax.broadcasted_iota(jnp.int32, (capacity, tokens), 0).astype(jnp.float32)
+    hits, weights = [], []
+    for e in range(experts):
+        hit = slot == rank[e : e + 1, :]
+        hits.append(hit.astype(jnp.float32).astype(jnp.bfloat16))
+        weights.append(jnp.sum(jnp.where(hit, w[e : e + 1, :], 0.0), axis=1, keepdims=True))
+    return jnp.concatenate(hits, axis=0), weights
+
+
+def place_kernel(experts, w_ref, x_ref, o_ref, s_ref):
+    capacity = o_ref.shape[1]
+    hits, weights = slots_of(w_ref[0], experts, capacity)
+    out = jnp.dot(hits, x_ref[0], preferred_element_type=jnp.float32)
+    for e in range(experts):
+        o_ref[e] = out[e * capacity : (e + 1) * capacity].astype(jnp.bfloat16)
+        s_ref[e] = weights[e]
+
+
+def place(weights, x, experts, capacity):
+    n, tokens, width = x.shape
+    return pl.pallas_call(
+        functools.partial(place_kernel, experts),
+        grid=(n,),
+        out_shape=(
+            jax.ShapeDtypeStruct((experts, n * capacity, width), x.dtype),
+            jax.ShapeDtypeStruct((experts, n * capacity, 1), jnp.float32),
+        ),
+        in_specs=[
+            pl.BlockSpec((1, 8, tokens), lambda c: (c, 0, 0)),
+            pl.BlockSpec((1, tokens, width), lambda c: (c, 0, 0)),
+        ],
+        out_specs=[
+            pl.BlockSpec((experts, capacity, width), lambda c: (0, c, 0)),
+            pl.BlockSpec((experts, capacity, 1), lambda c: (0, c, 0)),
+        ],
+        cost_estimate=work(10),
+        name="place",
+    )(weights, x)
+
+
+def place_weighted_kernel(experts, w_ref, *refs):
+    pieces, o_ref, x_buf = refs[:-2], refs[-2], refs[-1]
+    capacity = o_ref.shape[1]
+    half = pieces[0].shape[0]
+    for k in range(len(pieces) // 2):
+
+        @pl.when(pl.program_id(0) == k)
+        def _():
+            x_buf[:half] = pieces[2 * k][...]
+            x_buf[half:] = pieces[2 * k + 1][...]
+
+    hits, weights = slots_of(w_ref[0], experts, capacity)
+    out = jnp.dot(hits, x_buf[...], preferred_element_type=jnp.float32)
+    for e in range(experts):
+        o_ref[e] = (out[e * capacity : (e + 1) * capacity] * weights[e]).astype(jnp.bfloat16)
+
+
+def place_weighted(weights, pieces, experts, capacity):
+    n, _, tokens = weights.shape
+    half, width = pieces[0].shape
+    return pl.pallas_call(
+        functools.partial(place_weighted_kernel, experts),
+        grid=(n,),
+        out_shape=jax.ShapeDtypeStruct((experts, n * capacity, width), pieces[0].dtype),
+        in_specs=[pl.BlockSpec((1, 8, tokens), lambda c: (c, 0, 0))]
+        + [pl.BlockSpec((half, width), lambda c: (0, 0), pipeline_mode=pl.Buffered(1))] * len(pieces),
+        out_specs=pl.BlockSpec((experts, capacity, width), lambda c: (0, c, 0)),
+        scratch_shapes=[pltpu.VMEM((2 * half, width), pieces[0].dtype)],
+        cost_estimate=work(12),
+        name="place_weighted",
+    )(weights, *pieces)
+
+
+def unplace_kernel(experts, w_ref, y_ref, o_ref):
+    capacity, width = y_ref.shape[1:]
+    hits, _ = slots_of(w_ref[0], experts, capacity)
+    o_ref[0] = down_rows(hits, y_ref[...].reshape(experts * capacity, width)).astype(o_ref.dtype)
+
+
+def unplace(weights, y, capacity):
+    n, _, tokens = weights.shape
+    experts, _, width = y.shape
+    return pl.pallas_call(
+        functools.partial(unplace_kernel, experts),
+        grid=(n,),
+        out_shape=jax.ShapeDtypeStruct((n, tokens, width), y.dtype),
+        in_specs=[
+            pl.BlockSpec((1, 8, tokens), lambda c: (c, 0, 0)),
+            pl.BlockSpec((experts, capacity, width), lambda c: (0, c, 0)),
+        ],
+        out_specs=pl.BlockSpec((1, tokens, width), lambda c: (c, 0, 0)),
+        cost_estimate=work(10),
+        name="unplace",
+    )(weights, y)
+
+
 def widen_kernel(x_ref, o_ref):
     for e in range(x_ref.shape[0]):
         o_ref[:, e, :] = x_ref[e].astype(jnp.float32)
@@ -1133,40 +1189,30 @@
     cot_columns = [gather_column(cot_halves[0], n)]
     cot_columns.append(gather_column(cot_halves[1], n))
     cot_others = [gather_across([v], n) for v in cot_halves]
-    weights = by_place(weights, n)
-    taken = weights > 0
-    tri = (jnp.arange(rows)[:, None] <= jnp.arange(rows)[None, :]).astype(bf)
-    rank = jnp.einsum("cet,tu->ceu", taken.astype(bf), tri, preferred_element_type=f32) - 1.0
-    slot_ids = jnp.arange(capacity, dtype=f32)
-    hit = (rank[:, :, None, :] == slot_ids[None, None, :, None]) & taken[:, :, None, :]
-    place = hit.astype(bf)
-    slot_weight = jnp.sum(jnp.where(hit, weights[:, :, None, :], 0.0), axis=-1)
-    slot_weight = jnp.swapaxes(slot_weight, 0, 1)[..., None]
-    place_rows = lambda v: jnp.einsum("cert,ctd->ecrd", place, v, preferred_element_type=f32)
-    unplace = lambda v: jnp.einsum("cert,ecrd->ctd", place, v, preferred_element_type=f32).astype(bf)
-    received = place_rows(ffn_all).astype(bf)
-    gate = jnp.einsum("ecrd,edf->ecrf", received, full_gate, preferred_element_type=f32)
+    weights = jnp.pad(by_place(weights, n), ((0, 0), (0, 8 - local_experts), (0, 0)))
+    received, slot_weight = place(weights, ffn_all, local_experts, capacity)
+    gate = jnp.einsum("erd,edf->erf", received, full_gate, preferred_element_type=f32)
     cot_others[0] += gather_across(cot_columns[0], n)
     cot_others[1] += gather_across(cot_columns[1], n)
-    up_part = jnp.einsum("ecrd,edf->ecrf", received, full_up, preferred_element_type=f32)
+    up_part = jnp.einsum("erd,edf->erf", received, full_up, preferred_element_type=f32)
     sigmoid_gate = jax.nn.sigmoid(gate)
     activated = gate * sigmoid_gate
     hidden = (activated * up_part).astype(bf)
-    expert_out = jnp.einsum("ecrf,edf->ecrd", hidden, full_down, preferred_element_type=f32)
+    expert_out = jnp.einsum("erf,edf->erd", hidden, full_down, preferred_element_type=f32)
     expert_out = (expert_out * slot_weight).astype(bf)
-    ffn_part = unplace(expert_out)
+    ffn_part = unplace(weights, expert_out, capacity)
     ffn_part, cot_others = barrier((ffn_part, cot_others))
-    cot_all = jnp.stack(
-        [jnp.concatenate(v) for v in zip(*(([h] + c + o) for h, c, o in zip(cot_halves, cot_columns, cot_others)))]
-    )
+    cot_pieces = [
+        v for pair in zip(*(([h] + c + o) for h, c, o in zip(cot_halves, cot_columns, cot_others))) for v in pair
+    ]
     lines = n // 2
     ffn_got = {k: gather_across([ffn_part[lines + k]], n)[0] for k in list(range(1, lines)) + [0]}
     ffn_keep = [barrier(ffn_part[k]) for k in range(lines)]
     ffn_sum = lambda k: (ffn_keep[k].astype(f32) + ffn_got[k].astype(f32)).astype(bf)
 
     out_grad = cotangent.reshape(rows, width).astype(f32)
-    down_received = (place_rows(cot_all) * slot_weight).astype(bf)
-    hidden_grad = jnp.einsum("ecrd,edf->ecrf", down_received, full_down, preferred_element_type=f32)
+    down_received = place_weighted(weights, cot_pieces, local_experts, capacity)
+    hidden_grad = jnp.einsum("erd,edf->erf", down_received, full_down, preferred_element_type=f32)
     slope = sigmoid_gate * (1.0 + gate * (1.0 - sigmoid_gate))
     gate_grad = (hidden_grad * up_part * slope).astype(bf)
     up_grad = (hidden_grad * activated).astype(bf)
@@ -1174,21 +1220,19 @@
     gate_grad, up_grad, got = barrier((gate_grad, up_grad, [ffn_got[k] for k in early]))
     ffn_got.update(zip(early, got))
     ffn_pieces = [reduce_column(ffn_sum(k), k, n) for k in early]
-    rows_gate = jnp.einsum("ecrf,edf->ecrd", gate_grad, full_gate, preferred_element_type=f32)
+    rows_gate = jnp.einsum("erf,edf->erd", gate_grad, full_gate, preferred_element_type=f32)
     rows_gate, ffn_got[lines - 1] = barrier((rows_gate, ffn_got[lines - 1]))
     ffn_pieces.append(reduce_column(ffn_sum(lines - 1), lines - 1, n))
-    rows_up = jnp.einsum("ecrf,edf->ecrd", up_grad, full_up, preferred_element_type=f32)
-    rows_part = unplace((rows_gate + rows_up).astype(bf))
-    down_term = jnp.einsum("ecrd,ecrf->edf", down_received, hidden, preferred_element_type=f32)
+    rows_up = jnp.einsum("erf,edf->erd", up_grad, full_up, preferred_element_type=f32)
+    rows_grad = (rows_gate + rows_up).astype(bf)
+    rows_part = unplace(weights, rows_grad, capacity)
+    down_term = jnp.einsum("erd,erf->edf", down_received, hidden, preferred_element_type=f32)
     scatter = lambda v: lax.psum_scatter(v, "fsdp", scatter_dimension=1, tiled=True)
-    rows_part, ffn_pieces, ffn_got[0], down_term = barrier(
-        (rows_part, ffn_pieces, ffn_got[0], down_term.astype(bf))
+    rows_part, ffn_pieces, ffn_got[0] = barrier((rows_part, ffn_pieces, ffn_got[0]))
+    ffn_in_grad, gate_term, up_term = reduce_terms(
+        rows_part, received, gate_grad, up_grad, n, 8, 512, 4
     )
-    by_slot = lambda v: v.reshape(local_experts, n * capacity, v.shape[-1])
-    ffn_in_grad, gate_term, up_term = reduce_terms(
-        rows_part, by_slot(received), by_slot(gate_grad), by_slot(up_grad), n, 8, 512, 4
-    )
-    scattered = [scatter(down_term)]
+    scattered = [scatter(down_term.astype(bf))]
     scattered += [scatter(gate_term), scatter(up_term)]
     mid_back, ffn_gain_term = norm_backward(mid, norm_two, gain_ffn, ffn_in_grad)
     mid_grad = out_grad + mid_back
@@ -1208,15 +1252,14 @@
     head_term = jnp.einsum("td,te->de", normed, proj_grad, preferred_element_type=f32).astype(bf)
     head_term = head_term.reshape(n, groups, part, 3 * span).swapaxes(0, 1)
     block_out = mid + sum(piece.astype(f32) for piece in [ffn_keep[0], ffn_got[0]] + ffn_pieces)
-    down_sum, gate_sum, up_sum = scattered
-    normed_grad, *head_sums, out_sum, down_sum, gate_sum = reduce_sides(
+    normed_grad, *head_sums, out_sum = reduce_sides(
         normed_part.reshape(n, rows, width),
         head_term.reshape(groups, n * part, 3 * span),
         out_term.reshape(groups, part, width),
-        down_sum, gate_sum, n, groups, 8, 7,
+        n, groups, 8, 7,
     )
-    up_sum, normed_grad = barrier((up_sum, normed_grad))
-    up_sum = widen(up_sum)
+    scattered, normed_grad = barrier((scattered, normed_grad))
+    down_sum, gate_sum, up_sum = [widen(v) for v in scattered]
     input_back, attn_gain_term = norm_backward(inputs, inverse_norm(inputs), gain_attn, normed_grad)
     tokens_grad = mid_grad + input_back
     by_span = lambda v: v.reshape(n, 1, span)

time: 1290 us -> 1170 us (0.907)
  waiting for transfers between devices: 191 us -> 82.8 us
  Pallas kernels: 656 us -> 721 us
  matrix products: 253 us -> 206 us
  local copies, waits for them, and re-layouts: 80.9 us -> 51.1 us
  starting transfers between devices: 49.2 us -> 31.9 us
    reduce_scatter x3, waiting for transfers between devices: 80.1 us -> 0.01 us  [local(): lax.psum_scatter(v, 'fsdp', scatter_dimension=1, tiled=True)]
    pallas_call x1 -> x5, Pallas kernels: 116 us -> 167 us  [the longest x1 116 us: reduce_sides(): pl.pallas_call(functools.partial(reduce_sides_kernel, n, groups, pieces),...]
    dot_general x12 -> x7, matrix products: 217 us -> 171 us  [the longest x1 35 us: local(): jnp.einsum('erd,edf->erf', down_received, full_down, preferred_element_ty...]
    ppermute x6, waiting for transfers between devices: 44.5 us -> 0.02 us  [gather_column(): lax.ppermute(x, 'seq', along_lines(lines, 2, k))]
    ppermute x12, waiting for transfers between devices: 32.8 us -> 56.1 us  [gather_across(): return [lax.ppermute(c, 'seq', across_pairs(n // 2, 2)) for c in column]]
    convert_element_type x0 -> x1, other arithmetic: none -> 21.5 us  [local(): rows_grad = (rows_gate + rows_up).astype(bf)]
    unnamed x146 -> x145, local copies, waits for them, and re-layouts: 47.6 us -> 28.6 us
    ppermute x3, starting transfers between devices: 18.6 us -> 4.54 us  [reduce_column(): return lax.ppermute(v, 'seq', along_lines(n // 2, 2, n // 2 - k))]
  transfers between devices with their start and end apart: 29 -> 29, of which waited for: 12 -> 9; matrix products, arithmetic and copies ran while one was open for 22% -> 22% of each run, Pallas kernels for 41% -> 58%
where the time goes in v2:
time: 1170 us; the launch traced here: 1160 us
  Pallas kernels  721 us (62%)
  matrix products  206 us (18%)
  waiting for transfers between devices  82.8 us (7%)
  local copies, waits for them, and re-layouts  51.1 us (4%)
  other arithmetic  46.5 us (4%)
  starting transfers between devices  31.9 us (3%)
  between operations  15.3 us (1%)
    pallas_call x2, Pallas kernels, gather_rows(): pl.pallas_call(functools.partial(gather_kernel, n, pieces, by_index), out...  216 us
    pallas_call x1, Pallas kernels, project_rows(): pl.pallas_call(functools.partial(project_kernel, n, groups, pieces), out_...  120 us
    pallas_call x1, Pallas kernels, reduce_terms(): pl.pallas_call(functools.partial(reduce_terms_kernel, n, pieces, tile), o...  119 us
    pallas_call x1, Pallas kernels, reduce_sides(): pl.pallas_call(functools.partial(reduce_sides_kernel, n, groups, pieces),...  116 us
    ppermute x12, waiting for transfers between devices, gather_across(): return [lax.ppermute(c, 'seq', across_pairs(n // 2, 2)) for c in column]  56.1 us
    dot_general x1, matrix products, local(): jnp.einsum('erd,edf->erf', down_received, full_down, preferred_element_ty...  35 us
    unnamed x145, local copies, waits for them, and re-layouts  28.6 us
    dot_general x1, matrix products, local(): jnp.einsum('erd,edf->erf', received, full_up, preferred_element_type=f32)  26.6 us
  transfers between devices with their start and end apart: 29, of which 9 were waited for; matrix products, arithmetic and copies ran while one was open for 22% of the time, Pallas kernels for 58%

profile of v2, /device:TPU:0, one launch (start us, length us, event | category | flops | bytes accessed | tf_op | source)
XLA Modules:
  0.0 1155.0 jit_solution(15430585704461224531)
XLA Ops:
  8.0 5.7 copy.55
  14.0 120.0 %project_rows.1 = (bf16[2048,2048]{1,0:T(8,128)(2,1)}, f32[2048,768]{1,0:T(8,128)}, f32[16,256]{1,0:T(8,128)S(1)}, bf16[2048,768]{1,0:T(8,128)(2,1)}, f32[8,2048]{1,0:T(8,128)S(1)}) custom-call(bf16[256,2048]{1,0:T(8,128)(2,1)S(1)} %bitcast.99, bf16[512,2048]{1,0:T(8,128)(2,1)S(1)} %copy-done.23, bf16[512,2048]{1,0:T(8,128)(2,1)} %w_key.1, ...), custom_call_target="tpu_custom_call" | custom-call | flops 65999998976 | tf_op jit(solution)/shard_map/project_rows/pallas_call | solution.py:866
  133.9 3.4 copy.54
  137.4 5.6 copy.53
  144.0 3.0 copy-done.24
  147.0 11.5 rotate_rows.1
  161.5 15.8 %attend.1 = (bf16[2048,256]{1,0:T(8,128)(2,1)}, f32[2,1,2048]{2,1,0:T(1,128)}) custom-call(bf16[2048,256]{1,0:T(8,128)(2,1)} %copy-done.26, bf16[2048,256]{1,0:T(8,128)(2,1)} %copy-done.27, bf16[2048,256]{1,0:T(8,128)(2,1)} %copy-done.28), custom_call_target="tpu_custom_call" | custom-call | flops 15000000512 | tf_op jit(solution)/shard_map/attend/pallas_call | solution.py:660
  177.3 2.3 copy.43
  179.6 4.7 all-to-all-start
  186.4 21.8 %all-to-all-done = bf16[8,256,256]{1,2,0:T(8,128)(2,1)S(1)} async-done(((bf16[8,256,256]{1,2,0:T(8,128)(2,1)}), bf16[8,256,256]{1,2,0:T(8,128)(2,1)S(1)}, u32[]{:S(2)}, u32[]{:S(2)}) %all-to-all-start) | async-done | bytes 1048608 | tf_op jit(solution)/shard_map/all_to_all | solution.py:1179
  208.2 7.5 multiply_reduce_fusion.2
  218.4 107.9 %gather_rows.2.x_ref = bf16[8,256,2048]{2,1,0:T(8,128)(2,1)} custom-call(bf16[256,2048]{1,0:T(8,128)(2,1)} %multiply_convert_fusion.4.own), custom_call_target="tpu_custom_call" | custom-call | flops 62999998464 | tf_op jit(solution)/shard_map/gather_rows/pallas_call | solution.py:86
  326.4 3.2 collective-permute-start.10
  329.5 3.8 collective-permute-start.12
  335.3 2.9 collective-permute-start.5
  338.2 12.8 %place.1 = (bf16[4,768,2048]{2,1,0:T(8,128)(2,1)}, f32[4,768,1]{2,1,0:T(8,128)}) custom-call(f32[8,8,256]{2,1,0:T(8,128)} %pad.16.w_ref, bf16[8,256,2048]{2,1,0:T(8,128)(2,1)} %gather_rows.2.x_ref), custom_call_target="tpu_custom_call" | custom-call | flops 6000000000 | tf_op jit(solution)/shard_map/place/pallas_call | solution.py:510
  351.0 1.9 reduce
  352.9 22.6 %fusion.28 = f32[4,768,1024]{2,1,0:T(8,128)} fusion(bf16[4,768,2048]{2,1,0:T(8,128)(2,1)} %get-tuple-element.79.x, bf16[4,2048,1024]{2,1,0:T(8,128)(2,1)} %all-gather.7.cloned.1.call-done), kind=kOutput, calls=%fused_computation.86 | convolution fusion | flops 12884901888 | bytes 41943040 | tf_op jit(solution)/shard_map/erd,edf->erf/dot_general | solution.py:1194
  375.5 26.6 %multiply_convert_fusion.3 = (bf16[4,768,1024]{2,1,0:T(8,128)(2,1)}, f32[4,768,1024]{2,1,0:T(8,128)}) fusion(f32[4,768,1024]{2,1,0:T(8,128)} %fusion.28, bf16[4,768,2048]{2,1,0:T(8,128)(2,1)} %get-tuple-element.79.x, bf16[4,2048,1024]{2,1,0:T(8,128)(2,1)} %all-gather.9.cloned.1.call-done), kind=kOutput, calls=%fused_computation.6 | convolution fusion | flops 12903776256 | bytes 60817408 | tf_op jit(solution)/shard_map/erd,edf->erf/dot_general | solution.py:1197
  402.3 2.0 collective-permute-start.7
  404.5 3.4 all-gather.11.cloned.1.call-done
  407.9 20.0 %multiply_convert_fusion.y_ref = bf16[4,768,2048]{2,1,0:T(8,128)(2,1)} fusion(f32[4,768]{1,0:T(4,128)S(1)} %reduce, bf16[4,768,1024]{2,1,0:T(8,128)(2,1)} %get-tuple-element.155, bf16[4,2048,1024]{2,1,0:T(8,128)(2,1)} %all-gather.11.cloned.1.call-done), kind=kOutput, calls=%fused_computation.2 | convolution fusion | flops 12897484800 | bytes 35663872 | tf_op jit(solution)/shard_map/erf,edf->erd/dot_general | solution.py:1201
  427.9 1.5 collective-permute-start.13
  430.0 1.5 collective-permute-start.4
  432.0 6.6 collective-permute-done.11.refs_13_
  438.6 12.7 %unplace.2 = bf16[8,256,2048]{2,1,0:T(8,128)(2,1)} custom-call(f32[8,8,256]{2,1,0:T(8,128)} %pad.16.w_ref, bf16[4,768,2048]{2,1,0:T(8,128)(2,1)} %multiply_convert_fusion.y_ref), custom_call_target="tpu_custom_call" | custom-call | flops 6000000000 | tf_op jit(solution)/shard_map/unplace/pallas_call | solution.py:572
  451.3 9.7 collective-permute-done.2.refs_10_
  461.1 11.1 collective-permute-done.4.refs_12_
  472.2 11.2 collective-permute-done.6.refs_14_
  483.4 7.4 collective-permute-done.9.refs_11_
  491.6 12.3 %place_weighted.1 = bf16[4,768,2048]{2,1,0:T(8,128)(2,1)} custom-call(f32[8,8,256]{2,1,0:T(8,128)} %pad.16.w_ref, bf16[128,2048]{1,0:T(8,128)(2,1)} %copy-done.41, bf16[128,2048]{1,0:T(8,128)(2,1)} %copy-done.40, bf16[128,2048]{1,0:T(8,128)(2,1)} %copy-done.61, bf16[128,2048]{1,0:T(8,128)(2,1)} %collective-permute-done.8.refs_3_, ...), custom_call_target="tpu_custom_call" | custom-call | flops 7200000000 | tf_op jit(solution)/shard_map/place_weighted/pallas_call | solution.py:550
  503.9 19.6 %convolution_convert_fusion = bf16[4,2048,1024]{2,1,0:T(8,128)(2,1)} fusion(bf16[4,768,2048]{2,1,0:T(8,128)(2,1)} %place_weighted.1, bf16[4,768,1024]{2,1,0:T(8,128)(2,1)} %get-tuple-element.155), kind=kOutput, calls=%fused_computation.3 | convolution fusion | flops 12893290496 | bytes 35651584 | tf_op jit(solution)/shard_map/erd,erf->edf/dot_general | solution.py:1229
  523.7 5.9 slice_bitcast_fusion.7
  529.9 1.7 collective-permute-start.15
  531.9 1.7 collective-permute-start.20
  533.6 35.0 %multiply_convert_fusion.1 = (bf16[4,768,1024]{2,1,0:T(8,128)(2,1)}, bf16[4,768,1024]{2,1,0:T(8,128)(2,1)}) fusion(f32[4,768,1024]{2,1,0:T(8,128)} %fusion.28, f32[4,768,1024]{2,1,0:T(8,128)} %get-tuple-element.156, bf16[4,768,2048]{2,1,0:T(8,128)(2,1)} %place_weighted.1, bf16[4,2048,1024]{2,1,0:T(8,128)(2,1)} %all-gather.11.cloned.1.call-done), kind=kOutput, calls=%fused_computation.4 | convolution fusion | flops 12925796352 | bytes 67108864 | tf_op jit(solution)/shard_map/erd,edf->erf/dot_general | solution.py:1215
  568.6 9.8 collective-permute-done.15
  578.4 22.2 %fusion.29 = f32[4,768,2048]{2,1,0:T(8,128)} fusion(bf16[4,768,1024]{2,1,0:T(8,128)(2,1)} %get-tuple-element.93.first, bf16[4,2048,1024]{2,1,0:T(8,128)(2,1)} %all-gather.7.cloned.1.call-done), kind=kOutput, calls=%fused_computation.87 | convolution fusion | flops 12884901888 | bytes 48234496 | tf_op jit(solution)/shard_map/erf,edf->erd/dot_general | solution.py:1223
  600.9 2.8 add_convert_fusion.2
  603.7 1.7 collective-permute-start.19
  605.4 1.6 add_convert_fusion.3
  607.0 2.2 collective-permute-start.18
  609.2 1.7 add_convert_fusion.4
  611.5 24.5 %fusion.30 = f32[4,768,2048]{2,1,0:T(8,128)} fusion(bf16[4,768,1024]{2,1,0:T(8,128)(2,1)S(1)} %copy-done.67, bf16[4,2048,1024]{2,1,0:T(8,128)(2,1)} %all-gather.9.cloned.1.call-done), kind=kOutput, calls=%fused_computation.88 | convolution fusion | flops 12884901888 | bytes 48234496 | tf_op jit(solution)/shard_map/erf,edf->erd/dot_general | solution.py:1226
  636.0 21.5 %add_convert_fusion.y_ref = bf16[4,768,2048]{2,1,0:T(8,128)(2,1)} fusion(f32[4,768,2048]{2,1,0:T(8,128)} %fusion.29, f32[4,768,2048]{2,1,0:T(8,128)} %fusion.30), kind=kLoop, calls=%fused_computation.1 | loop fusion | flops 12582912 | bytes 62914560 | tf_op jit(solution)/shard_map/convert_element_type | solution.py:1227
  657.6 12.7 %unplace.3.part = bf16[8,256,2048]{2,1,0:T(8,128)(2,1)} custom-call(f32[8,8,256]{2,1,0:T(8,128)} %pad.16.w_ref, bf16[4,768,2048]{2,1,0:T(8,128)(2,1)} %add_convert_fusion.y_ref), custom_call_target="tpu_custom_call" | custom-call | flops 6000000000 | tf_op jit(solution)/shard_map/unplace/pallas_call | solution.py:572
  670.3 119.0 %reduce_terms.1 = (f32[256,2048]{1,0:T(8,128)S(1)}, bf16[4,2048,1024]{2,1,0:T(8,128)(2,1)}, bf16[4,2048,1024]{2,1,0:T(8,128)(2,1)}) custom-call(bf16[8,256,2048]{2,1,0:T(8,128)(2,1)} %unplace.3.part, bf16[4,768,2048]{2,1,0:T(8,128)(2,1)} %get-tuple-element.79.x, bf16[4,768,1024]{2,1,0:T(8,128)(2,1)} %get-tuple-element.93.first, ...), custom_call_target="tpu_custom_call" | custom-call | flops 62999998464 | tf_op jit(solution)/shard_map/reduce_terms/pallas_call | solution.py:232
  792.2 3.2 multiply_reduce_fusion
  795.4 3.2 fusion.25.own
  798.6 108.1 %gather_rows.3 = bf16[8,256,2048]{2,1,0:T(8,128)(2,1)} custom-call(bf16[256,2048]{1,0:T(8,128)(2,1)} %fusion.25.own), custom_call_target="tpu_custom_call" | custom-call | flops 62999998464 | tf_op jit(solution)/shard_map/gather_rows/pallas_call | solution.py:86
  906.7 7.0 convolution_convert_fusion.4.g_ref
  913.7 22.4 %attend_back.1 = (bf16[2048,256]{1,0:T(8,128)(2,1)}, bf16[2048,256]{1,0:T(8,128)(2,1)}, bf16[2048,256]{1,0:T(8,128)(2,1)}) custom-call(bf16[2048,256]{1,0:T(8,128)(2,1)} %copy-done.26, bf16[2048,256]{1,0:T(8,128)(2,1)} %copy-done.27, bf16[2048,256]{1,0:T(8,128)(2,1)} %copy-done.28, bf16[2048,256]{1,0:T(8,128)(2,1)} %convolution_convert_fusion.4.g_ref, ...), custom_call_target="tpu_custom_call" | custom-call | flops 35999997952 | tf_op jit(solution)/shard_map/attend_back/pallas_call | solution.py:727
  936.1 3.4 copy-done.25
  943.2 16.8 %heads_back.1 = (bf16[2048,768]{1,0:T(8,128)(2,1)S(1)}, f32[8,256]{1,0:T(8,128)S(1)}) custom-call(bf16[2048,256]{1,0:T(8,128)(2,1)S(1)} %copy-done.29, bf16[2048,256]{1,0:T(8,128)(2,1)S(1)} %copy-done.30, bf16[2048,256]{1,0:T(8,128)(2,1)S(1)} %copy-done.31, f32[2048,768]{1,0:T(8,128)S(1)} %copy-done.25, f32[16,256]{1,0:T(8,128)S(1)} %get-tuple-element.111.factors, ...), custom_call_target="tpu_custom_call" | custom-call | flops 12000000000 | tf_op jit(solution)/shard_map/heads_back/pallas_call | solution.py:1060
  960.1 9.7 convolution_convert_fusion.2
  969.8 2.0 copy.48
  971.8 2.3 convolution_convert_fusion.3
  974.2 9.1 convolution_convert_fusion.1
  983.3 115.9 %reduce_sides.1 = (f32[256,2048]{1,0:T(8,128)}, f32[64,2048]{1,0:T(8,128)S(1)}, f32[64,2048]{1,0:T(8,128)S(1)}, f32[64,2048]{1,0:T(8,128)S(1)}, f32[64,2048]{1,0:T(8,128)S(1)}) custom-call(bf16[8,256,2048]{2,1,0:T(8,128)(2,1)} %bitcast.123, bf16[4,512,768]{2,1,0:T(8,128)(2,1)} %bitcast.111, bf16[4,64,2048]{2,1,0:T(8,128)(2,1)S(1)} %bitcast.100), custom_call_target="tpu_custom_call" | custom-call | flops 62999998464 | tf_op jit(solution)/shard_map/reduce_sides/pallas_call | solution.py:387
  1102.4 6.5 widen.3
  1109.0 6.5 widen.4
  1115.5 6.7 widen.5
  1123.6 13.5 %sum_gains.1 = f32[8,256]{1,0:T(8,128)} custom-call(f32[8,8,256]{2,1,0:T(8,128)} %select_maximum_fusion.sent, f32[8,256]{1,0:T(8,128)} %copy-done.32), custom_call_target="tpu_custom_call" | custom-call | flops 6000000000 | tf_op jit(solution)/shard_map/sum_gains/pallas_call | solution.py:461
  1138.4 6.4 fusion.8
  (219 shorter events, 30.8 us)
Async XLA Ops:
  7.2 201.1 %all-gather.5.cloned.1.call-start = ((), (), s32[]{:S(2)}) async-start(), calls=%async_computation.4 | async-start | bytes 10485760 | tf_op jit(solution)/shard_map/all_gather | solution.py:1158
  8.0 344.9 %all-gather.7.cloned.1.call-start = ((), (), s32[]{:S(2)}) async-start(), calls=%async_computation.5 | async-start | bytes 20971520 | tf_op jit(solution)/shard_map/all_gather | solution.py:1159
  13.8 361.8 %all-gather.9.cloned.1.call-start = ((), (), s32[]{:S(2)}) async-start(), calls=%async_computation.6 | async-start | bytes 20971520 | tf_op jit(solution)/shard_map/all_gather | solution.py:1159
  14.0 120.0 %copy-start.38 = (bf16[512,4,1024]{2,1,0:T(4,128)(2,1)S(1)}, bf16[512,4,1024]{2,1,0:T(4,128)(2,1)}, u32[]{:S(2)}) copy-start(bf16[512,4,1024]{2,1,0:T(4,128)(2,1)} %param.28) | copy-start | bytes 12582916
  137.4 270.5 %all-gather.11.cloned.1.call-start = ((), (), s32[]{:S(2)}) async-start(), calls=%async_computation.7 | async-start | bytes 20971520 | tf_op jit(solution)/shard_map/all_gather | solution.py:1159
  143.3 15.1 %copy-start.21 = (f32[2,256]{1,0:T(2,128)}, f32[2,256]{1,0:T(2,128)S(1)}, u32[]{:S(2)}) copy-start(f32[2,256]{1,0:T(2,128)S(1)} %constant_dynamic-slice_fusion.1.gains) | copy-start | bytes 6148
  143.4 15.0 %copy-start.17 = (f32[8,128]{1,0:T(8,128)}, f32[8,128]{1,0:T(8,128)S(1)}, u32[]{:S(2)}) copy-start(f32[8,128]{1,0:T(8,128)S(1)} %get-tuple-element.149.far_sin) | copy-start | bytes 12292
  143.5 15.0 %copy-start.19 = (f32[8,128]{1,0:T(8,128)}, f32[8,128]{1,0:T(8,128)S(1)}, u32[]{:S(2)}) copy-start(f32[8,128]{1,0:T(8,128)S(1)} %get-tuple-element.150.far_cos) | copy-start | bytes 12292
  144.0 14.5 %copy-start.13 = (f32[256,128]{1,0:T(8,128)}, f32[256,128]{1,0:T(8,128)S(1)}, u32[]{:S(2)}) copy-start(f32[256,128]{1,0:T(8,128)S(1)} %get-tuple-element.151.near_sin) | copy-start | bytes 393220
  144.0 14.5 %copy-start.15 = (f32[256,128]{1,0:T(8,128)}, f32[256,128]{1,0:T(8,128)S(1)}, u32[]{:S(2)}) copy-start(f32[256,128]{1,0:T(8,128)S(1)} %get-tuple-element.152.near_cos) | copy-start | bytes 393220
  179.6 28.6 %all-to-all-start = ((bf16[8,256,256]{1,2,0:T(8,128)(2,1)}), bf16[8,256,256]{1,2,0:T(8,128)(2,1)S(1)}, u32[]{:S(2)}, u32[]{:S(2)}) async-start(bf16[8,256,256]{1,2,0:T(8,128)(2,1)} %copy.43), calls=%async_computation | async-start | bytes 2097152 | tf_op jit(solution)/shard_map/all_to_all | solution.py:1179
  184.3 918.1 %reduce-scatter.4.cloned.1.call-start = ((), (), s32[]{:S(2)}) async-start(), calls=%async_computation.8 | async-start | bytes 20971520 | tf_op jit(solution)/shard_map/reduce_scatter | solution.py:1230
  186.4 29.4 %copy-start.42 = (f32[1,2048]{1,0:T(1,128)}, f32[1,2048]{1,0:T(1,128)S(1)}, u32[]{:S(2)}) copy-start(f32[1,2048]{1,0:T(1,128)S(1)} %get-tuple-element.144) | copy-start | bytes 24580
  215.7 110.5 %copy-start.47 = (f32[256]{0:T(256)}, f32[256]{0:T(256)S(1)}, u32[]{:S(2)}) copy-start(f32[256]{0:T(256)S(1)} %add_rsqrt_fusion.1) | copy-start | bytes 3076
  218.4 107.9 %copy-start.35 = (bf16[1,256,2048]{2,1,0:T(8,128)(2,1)S(1)}, bf16[1,256,2048]{2,1,0:T(8,128)(2,1)}, u32[]{:S(2)}) copy-start(bf16[1,256,2048]{2,1,0:T(8,128)(2,1)} %param.18) | copy-start | bytes 3145732
  326.3 75.9 %copy-start.41 = (bf16[128,2048]{1,0:T(8,128)(2,1)}, bf16[128,2048]{1,0:T(8,128)(2,1)S(1)}, u32[]{:S(2)}) copy-start(bf16[128,2048]{1,0:T(8,128)(2,1)S(1)} %get-tuple-element.142.refs_0_) | copy-start | bytes 1572868
  326.3 76.0 %copy-start.40 = (bf16[128,2048]{1,0:T(8,128)(2,1)}, bf16[128,2048]{1,0:T(8,128)(2,1)S(1)}, u32[]{:S(2)}) copy-start(bf16[128,2048]{1,0:T(8,128)(2,1)S(1)} %get-tuple-element.141.refs_1_) | copy-start | bytes 1572868
  326.4 75.7 %collective-permute-start.10 = (bf16[128,2048]{1,0:T(8,128)(2,1)S(1)}, bf16[128,2048]{1,0:T(8,128)(2,1)S(1)}, u32[]{:S(2)}, u32[]{:S(2)}) collective-permute-start(bf16[128,2048]{1,0:T(8,128)(2,1)S(1)} %get-tuple-element.141.refs_1_), channel_id=1, source_target_pairs={{0,16},{4,20},{8,24},{12,28},{16,0},{20,4},{24,8},{28,12},{1,17},{... | collective-permute-start | bytes 1572872 | tf_op jit(solution)/shard_map/ppermute | solution.py:1122
  329.5 72.7 %collective-permute-start.12 = (bf16[128,2048]{1,0:T(8,128)(2,1)S(1)}, bf16[128,2048]{1,0:T(8,128)(2,1)S(1)}, u32[]{:S(2)}, u32[]{:S(2)}) collective-permute-start(bf16[128,2048]{1,0:T(8,128)(2,1)S(1)} %get-tuple-element.141.refs_1_), channel_id=1, source_target_pairs={{0,24},{4,28},{8,0},{12,4},{16,8},{20,12},{24,16},{28,20},{1,25},{... | collective-permute-start | bytes 1572872 | tf_op jit(solution)/shard_map/ppermute | solution.py:1122
  333.3 69.0 %collective-permute-start.1 = (bf16[128,2048]{1,0:T(8,128)(2,1)S(1)}, bf16[128,2048]{1,0:T(8,128)(2,1)S(1)}, u32[]{:S(2)}, u32[]{:S(2)}) collective-permute-start(bf16[128,2048]{1,0:T(8,128)(2,1)S(1)} %get-tuple-element.142.refs_0_), channel_id=1, source_target_pairs={{0,8},{4,12},{8,16},{12,20},{16,24},{20,28},{24,0},{28,4},{1,9},{5... | collective-permute-start | bytes 1572872 | tf_op jit(solution)/shard_map/ppermute | solution.py:1122
  333.8 70.6 %collective-permute-start.3 = (bf16[128,2048]{1,0:T(8,128)(2,1)S(1)}, bf16[128,2048]{1,0:T(8,128)(2,1)S(1)}, u32[]{:S(2)}, u32[]{:S(2)}) collective-permute-start(bf16[128,2048]{1,0:T(8,128)(2,1)S(1)} %get-tuple-element.142.refs_0_), channel_id=1, source_target_pairs={{0,16},{4,20},{8,24},{12,28},{16,0},{20,4},{24,8},{28,12},{1,17},{... | collective-permute-start | bytes 1572872 | tf_op jit(solution)/shard_map/ppermute | solution.py:1122
  335.3 92.6 %collective-permute-start.5 = (bf16[128,2048]{1,0:T(8,128)(2,1)S(1)}, bf16[128,2048]{1,0:T(8,128)(2,1)}, u32[]{:S(2)}, u32[]{:S(2)}) collective-permute-start(bf16[128,2048]{1,0:T(8,128)(2,1)S(1)} %get-tuple-element.142.refs_0_), channel_id=1, source_target_pairs={{0,24},{4,28},{8,0},{12,4},{16,8},{20,12},{24,16},{28,20},{1,25},{... | collective-permute-start | bytes 1572872 | tf_op jit(solution)/shard_map/ppermute | solution.py:1122
  402.1 25.7 %copy-start.59 = (bf16[128,2048]{1,0:T(8,128)(2,1)}, bf16[128,2048]{1,0:T(8,128)(2,1)S(1)}, u32[]{:S(2)}) copy-start(bf16[128,2048]{1,0:T(8,128)(2,1)S(1)} %collective-permute-done.10.refs_5_) | copy-start | bytes 1572868
  402.1 27.3 %collective-permute-start.8 = (bf16[128,2048]{1,0:T(8,128)(2,1)S(1)}, bf16[128,2048]{1,0:T(8,128)(2,1)}, u32[]{:S(2)}, u32[]{:S(2)}) collective-permute-start(bf16[128,2048]{1,0:T(8,128)(2,1)S(1)} %get-tuple-element.141.refs_1_), channel_id=1, source_target_pairs={{0,8},{4,12},{8,16},{12,20},{16,24},{20,28},{24,0},{28,4},{1,9},{5... | collective-permute-start | bytes 1572872 | tf_op jit(solution)/shard_map/ppermute | solution.py:1122
  402.2 25.7 %copy-start.60 = (bf16[128,2048]{1,0:T(8,128)(2,1)}, bf16[128,2048]{1,0:T(8,128)(2,1)S(1)}, u32[]{:S(2)}) copy-start(bf16[128,2048]{1,0:T(8,128)(2,1)S(1)} %collective-permute-done.12.refs_7_) | copy-start | bytes 1572868
  402.2 27.8 %collective-permute-start = (bf16[128,2048]{1,0:T(8,128)(2,1)S(1)}, bf16[128,2048]{1,0:T(8,128)(2,1)}, u32[]{:S(2)}, u32[]{:S(2)}) collective-permute-start(bf16[128,2048]{1,0:T(8,128)(2,1)S(1)} %get-tuple-element.142.refs_0_), channel_id=1, source_target_pairs={{0,4},{4,0},{8,12},{12,8},{16,20},{20,16},{24,28},{28,24},{1,5},{5... | collective-permute-start | bytes 1572872 | tf_op jit(solution)/shard_map/ppermute | solution.py:1126
  402.3 27.1 %copy-start.61 = (bf16[128,2048]{1,0:T(8,128)(2,1)}, bf16[128,2048]{1,0:T(8,128)(2,1)S(1)}, u32[]{:S(2)}) copy-start(bf16[128,2048]{1,0:T(8,128)(2,1)S(1)} %collective-permute-done.1.refs_2_) | copy-start | bytes 1572868
  402.3 29.1 %collective-permute-start.7 = (bf16[128,2048]{1,0:T(8,128)(2,1)S(1)}, bf16[128,2048]{1,0:T(8,128)(2,1)}, u32[]{:S(2)}, u32[]{:S(2)}) collective-permute-start(bf16[128,2048]{1,0:T(8,128)(2,1)S(1)} %get-tuple-element.141.refs_1_), channel_id=1, source_target_pairs={{0,4},{4,0},{8,12},{12,8},{16,20},{20,16},{24,28},{28,24},{1,5},{5... | collective-permute-start | bytes 1572872 | tf_op jit(solution)/shard_map/ppermute | solution.py:1126
  404.4 25.6 %copy-start.62 = (bf16[128,2048]{1,0:T(8,128)(2,1)}, bf16[128,2048]{1,0:T(8,128)(2,1)S(1)}, u32[]{:S(2)}) copy-start(bf16[128,2048]{1,0:T(8,128)(2,1)S(1)} %collective-permute-done.3.refs_4_) | copy-start | bytes 1572868
  404.4 34.2 %collective-permute-start.11 = (bf16[128,2048]{1,0:T(8,128)(2,1)S(1)}, bf16[128,2048]{1,0:T(8,128)(2,1)}, u32[]{:S(2)}, u32[]{:S(2)}) collective-permute-start(bf16[128,2048]{1,0:T(8,128)(2,1)S(1)} %collective-permute-done.10.refs_5_), channel_id=1, source_target_pairs={{0,4},{4,0},{8,12},{12,8},{16,20},{20,16},{24,28},{28,24},{1,5},{5... | collective-permute-start | bytes 1572872 | tf_op jit(solution)/shard_map/ppermute | solution.py:1126
  427.9 23.5 %collective-permute-start.13 = (bf16[128,2048]{1,0:T(8,128)(2,1)S(1)}, bf16[128,2048]{1,0:T(8,128)(2,1)}, u32[]{:S(2)}, u32[]{:S(2)}) collective-permute-start(bf16[128,2048]{1,0:T(8,128)(2,1)S(1)} %collective-permute-done.12.refs_7_), channel_id=1, source_target_pairs={{0,4},{4,0},{8,12},{12,8},{16,20},{20,16},{24,28},{28,24},{1,5},{5... | collective-permute-start | bytes 1572872 | tf_op jit(solution)/shard_map/ppermute | solution.py:1126
  429.4 31.7 %collective-permute-start.2 = (bf16[128,2048]{1,0:T(8,128)(2,1)S(1)}, bf16[128,2048]{1,0:T(8,128)(2,1)}, u32[]{:S(2)}, u32[]{:S(2)}) collective-permute-start(bf16[128,2048]{1,0:T(8,128)(2,1)S(1)} %collective-permute-done.1.refs_2_), channel_id=1, source_target_pairs={{0,4},{4,0},{8,12},{12,8},{16,20},{20,16},{24,28},{28,24},{1,5},{5... | collective-permute-start | bytes 1572872 | tf_op jit(solution)/shard_map/ppermute | solution.py:1126
  430.0 42.2 %collective-permute-start.4 = (bf16[128,2048]{1,0:T(8,128)(2,1)S(1)}, bf16[128,2048]{1,0:T(8,128)(2,1)S(1)}, u32[]{:S(2)}, u32[]{:S(2)}) collective-permute-start(bf16[128,2048]{1,0:T(8,128)(2,1)S(1)} %collective-permute-done.3.refs_4_), channel_id=1, source_target_pairs={{0,4},{4,0},{8,12},{12,8},{16,20},{20,16},{24,28},{28,24},{1,5},{5... | collective-permute-start | bytes 1572872 | tf_op jit(solution)/shard_map/ppermute | solution.py:1126
  431.4 52.0 %collective-permute-start.6 = (bf16[128,2048]{1,0:T(8,128)(2,1)}, bf16[128,2048]{1,0:T(8,128)(2,1)S(1)}, u32[]{:S(2)}, u32[]{:S(2)}) collective-permute-start(bf16[128,2048]{1,0:T(8,128)(2,1)} %collective-permute-done.5.refs_6_), channel_id=1, source_target_pairs={{0,4},{4,0},{8,12},{12,8},{16,20},{20,16},{24,28},{28,24},{1,5},{5... | collective-permute-start | bytes 1572872 | tf_op jit(solution)/shard_map/ppermute | solution.py:1126
  438.6 52.2 %collective-permute-start.9 = (bf16[128,2048]{1,0:T(8,128)(2,1)}, bf16[128,2048]{1,0:T(8,128)(2,1)S(1)}, u32[]{:S(2)}, u32[]{:S(2)}) collective-permute-start(bf16[128,2048]{1,0:T(8,128)(2,1)} %collective-permute-done.8.refs_3_), channel_id=1, source_target_pairs={{0,4},{4,0},{8,12},{12,8},{16,20},{20,16},{24,28},{28,24},{1,5},{5... | collective-permute-start | bytes 1572872 | tf_op jit(solution)/shard_map/ppermute | solution.py:1126
  472.2 18.6 %copy-start.63 = (bf16[128,2048]{1,0:T(8,128)(2,1)}, bf16[128,2048]{1,0:T(8,128)(2,1)S(1)}, u32[]{:S(2)}) copy-start(bf16[128,2048]{1,0:T(8,128)(2,1)S(1)} %collective-permute-done.4.refs_12_) | copy-start | bytes 1572868
  483.4 7.4 copy-start.64
  523.6 578.8 %reduce-scatter.6.cloned.1.call-start = ((), (), s32[]{:S(2)}) async-start(), calls=%async_computation.9 | async-start | bytes 20971520 | tf_op jit(solution)/shard_map/reduce_scatter | solution.py:1230
  529.5 39.1 %collective-permute-start.14 = (bf16[256,2048]{1,0:T(8,128)(2,1)}, bf16[256,2048]{1,0:T(8,128)(2,1)}, u32[]{:S(2)}, u32[]{:S(2)}) collective-permute-start(bf16[256,2048]{1,0:T(8,128)(2,1)} %get-tuple-element.138), channel_id=1, source_target_pairs={{0,4},{4,0},{8,12},{12,8},{16,20},{20,16},{24,28},{28,24},{1,5},{5... | collective-permute-start | bytes 3145736 | tf_op jit(solution)/shard_map/ppermute | solution.py:1126
  529.9 48.5 %collective-permute-start.15 = (bf16[256,2048]{1,0:T(8,128)(2,1)}, bf16[256,2048]{1,0:T(8,128)(2,1)}, u32[]{:S(2)}, u32[]{:S(2)}) collective-permute-start(bf16[256,2048]{1,0:T(8,128)(2,1)} %get-tuple-element.137), channel_id=1, source_target_pairs={{0,4},{4,0},{8,12},{12,8},{16,20},{20,16},{24,28},{28,24},{1,5},{5... | collective-permute-start | bytes 3145736 | tf_op jit(solution)/shard_map/ppermute | solution.py:1126
  531.6 69.3 %collective-permute-start.16 = (bf16[256,2048]{1,0:T(8,128)(2,1)}, bf16[256,2048]{1,0:T(8,128)(2,1)}, u32[]{:S(2)}, u32[]{:S(2)}) collective-permute-start(bf16[256,2048]{1,0:T(8,128)(2,1)} %get-tuple-element.136), channel_id=1, source_target_pairs={{0,4},{4,0},{8,12},{12,8},{16,20},{20,16},{24,28},{28,24},{1,5},{5... | collective-permute-start | bytes 3145736 | tf_op jit(solution)/shard_map/ppermute | solution.py:1126
  531.9 138.4 %collective-permute-start.20 = (bf16[256,2048]{1,0:T(8,128)(2,1)}, bf16[256,2048]{1,0:T(8,128)(2,1)}, u32[]{:S(2)}, u32[]{:S(2)}) collective-permute-start(bf16[256,2048]{1,0:T(8,128)(2,1)} %get-tuple-element.132), channel_id=1, source_target_pairs={{0,4},{4,0},{8,12},{12,8},{16,20},{20,16},{24,28},{28,24},{1,5},{5... | collective-permute-start | bytes 3145736 | tf_op jit(solution)/shard_map/ppermute | solution.py:1126
  600.6 10.9 copy-start.67
  603.7 66.7 %collective-permute-start.19 = (bf16[256,2048]{1,0:T(8,128)(2,1)}, bf16[256,2048]{1,0:T(8,128)(2,1)}, u32[]{:S(2)}, u32[]{:S(2)}) collective-permute-start(bf16[256,2048]{1,0:T(8,128)(2,1)} %add_convert_fusion.2), channel_id=1, source_target_pairs={{0,8},{4,12},{8,16},{12,20},{16,24},{20,28},{24,0},{28,4},{1,9},{5... | collective-permute-start | bytes 3145736 | tf_op jit(solution)/shard_map/ppermute | solution.py:1130
  607.0 63.3 %collective-permute-start.18 = (bf16[256,2048]{1,0:T(8,128)(2,1)S(1)}, bf16[256,2048]{1,0:T(8,128)(2,1)}, u32[]{:S(2)}, u32[]{:S(2)}) collective-permute-start(bf16[256,2048]{1,0:T(8,128)(2,1)S(1)} %add_convert_fusion.3), channel_id=1, source_target_pairs={{0,16},{4,20},{8,24},{12,28},{16,0},{20,4},{24,8},{28,12},{1,17},{... | collective-permute-start | bytes 3145736 | tf_op jit(solution)/shard_map/ppermute | solution.py:1130
  610.9 59.5 %collective-permute-start.17 = (bf16[256,2048]{1,0:T(8,128)(2,1)S(1)}, bf16[256,2048]{1,0:T(8,128)(2,1)S(1)}, u32[]{:S(2)}, u32[]{:S(2)}) collective-permute-start(bf16[256,2048]{1,0:T(8,128)(2,1)S(1)} %add_convert_fusion.4), channel_id=1, source_target_pairs={{0,24},{4,28},{8,0},{12,4},{16,8},{20,12},{24,16},{28,20},{1,25},{... | collective-permute-start | bytes 3145736 | tf_op jit(solution)/shard_map/ppermute | solution.py:1130
  670.3 119.0 %copy-start.39 = (bf16[256,2048]{1,0:T(8,128)(2,1)}, bf16[256,2048]{1,0:T(8,128)(2,1)S(1)}, u32[]{:S(2)}) copy-start(bf16[256,2048]{1,0:T(8,128)(2,1)S(1)} %collective-permute-done.17) | copy-start | bytes 3145732
  789.4 313.0 %reduce-scatter.8.cloned.1.call-start = ((), (), s32[]{:S(2)}) async-start(), calls=%async_computation.10 | async-start | bytes 20971520 | tf_op jit(solution)/shard_map/reduce_scatter | solution.py:1230
  795.4 111.3 %copy-start.51 = (f32[256]{0:T(256)}, f32[256]{0:T(256)S(1)}, u32[]{:S(2)}) copy-start(f32[256]{0:T(256)S(1)} %broadcast_multiply_fusion.1) | copy-start | bytes 3076
  913.7 22.4 %copy-start.14 = (f32[256,128]{1,0:T(8,128)S(1)}, f32[256,128]{1,0:T(8,128)}, u32[]{:S(2)}) copy-start(f32[256,128]{1,0:T(8,128)} %copy-done.13) | copy-start | bytes 393220
  913.7 22.4 %copy-start.16 = (f32[256,128]{1,0:T(8,128)S(1)}, f32[256,128]{1,0:T(8,128)}, u32[]{:S(2)}) copy-start(f32[256,128]{1,0:T(8,128)} %copy-done.15) | copy-start | bytes 393220
  913.7 22.4 %copy-start.18 = (f32[8,128]{1,0:T(8,128)S(1)}, f32[8,128]{1,0:T(8,128)}, u32[]{:S(2)}) copy-start(f32[8,128]{1,0:T(8,128)} %copy-done.17) | copy-start | bytes 12292
  913.7 22.4 %copy-start.20 = (f32[8,128]{1,0:T(8,128)S(1)}, f32[8,128]{1,0:T(8,128)}, u32[]{:S(2)}) copy-start(f32[8,128]{1,0:T(8,128)} %copy-done.19) | copy-start | bytes 12292
  913.7 22.4 %copy-start.22 = (f32[2,256]{1,0:T(2,128)S(1)}, f32[2,256]{1,0:T(2,128)}, u32[]{:S(2)}) copy-start(f32[2,256]{1,0:T(2,128)} %copy-done.21) | copy-start | bytes 6148
  943.2 28.6 %slice-start = ((s8[8388608]{0:T(1024)(128)(4,1)}), s8[4194304]{0:T(1024)(128)(4,1)S(1)}, s32[]{:S(2)}) async-start(s8[8388608]{0:T(1024)(128)(4,1)} %bitcast.102), calls=%async_computation.11 | async-start | bytes 8388608
  960.1 9.7 copy-start.32
  960.1 11.7 %slice-start.1 = ((s8[8388608]{0:T(1024)(128)(4,1)}), s8[4194304]{0:T(1024)(128)(4,1)S(1)}, s32[]{:S(2)}) async-start(s8[8388608]{0:T(1024)(128)(4,1)} %bitcast.102), calls=%async_computation.12 | async-start | bytes 8388608
  1115.5 7.4 copy-start.46
  1123.5 14.8 %copy-start.1 = (f32[256,2048]{1,0:T(8,128)S(1)}, f32[256,2048]{1,0:T(8,128)}, u32[]{:S(2)}) copy-start(f32[256,2048]{1,0:T(8,128)} %copy-done) | copy-start | bytes 6291460
  1123.5 14.8 %copy-start.44 = (f32[1,2048]{1,0:T(1,128)S(1)}, f32[1,2048]{1,0:T(1,128)}, u32[]{:S(2)}) copy-start(f32[1,2048]{1,0:T(1,128)} %copy-done.42) | copy-start | bytes 24580
  1123.5 14.8 %copy-start.49 = (f32[256]{0:T(256)S(1)}, f32[256]{0:T(256)}, u32[]{:S(2)}) copy-start(f32[256]{0:T(256)} %copy-done.47) | copy-start | bytes 3076
  1123.5 14.8 %copy-start.52 = (f32[256]{0:T(256)S(1)}, f32[256]{0:T(256)}, u32[]{:S(2)}) copy-start(f32[256]{0:T(256)} %copy-done.51) | copy-start | bytes 3076
  1138.4 8.0 copy-start.8
  1138.4 8.8 copy-start.6
  (35 other events, 127.7 us)
Sparse Core Ops, SparseCore 0:
  9.5 75.4 all-gather.4
  87.2 104.6 all-gather.6
  194.0 105.8 all-gather.8
  302.0 105.8 all-gather.10
  523.7 124.8 reduce-scatter.3
  789.5 122.4 reduce-scatter.5
  914.6 169.9 reduce-scatter.7

commit v3 on v2

--- a/solution.py
+++ b/solution.py
@@ -257,15 +257,20 @@
     )(part, x, first, second)
 
 
-def reduce_sides_kernel(
-    n, groups, pieces, part, head, wide, out, q_out, k_out, v_out, o_out,
-    mine, got, sums, landed, head_own, head_land, wide_own, wide_land, head_sum, head_got,
-    send_sem, recv_sem, load_sem, side_send, side_recv, side_load, swap_send, swap_recv
+def finish_kernel(
+    n, groups, pieces, part, head, wide, tokens, mid_grad, gains, gain_term, own_gains,
+    tokens_grad, q_out, k_out, v_out, o_out, gain_out,
+    mine, got, sums, landed, head_own, head_land, head_pair, head_far, wide_own, wide_land, wide_pair, wide_far,
+    head_sum, head_got, gain_acc, gain_send, gain_got, gain_sum, gain_far,
+    send_sem, recv_sem, load_sem, near_send, near_recv, near_load, far_send, far_recv,
+    swap_send, swap_recv, gain_sends, gain_recvs, side_sends, side_recvs
 ):
     pair = 2
     lines = n // pair
+    chips = groups // 2
     me, group = lax.axis_index("seq"), lax.axis_index("fsdp")
     a, b = me // pair, me % pair
+    chip, parity = group // 2, group % 2
     across = a * pair + (1 - b)
     peers = [(me + k) % n for k in range(1, n)]
     mates = [(group + k) % groups for k in range(1, groups)]
@@ -275,7 +280,8 @@
     for mate in mates:
         pl.semaphore_signal(barrier, inc=1, device_id={"fsdp": mate}, device_id_type=MESH)
     pl.semaphore_wait(barrier, n - 1 + groups - 1)
-    rows = out.shape[0] // pieces
+    rows = tokens_grad.shape[0] // pieces
+    bf, f32 = jnp.bfloat16, jnp.float32
 
     def piece(p):
         return pl.ds(pl.multiple_of(p * rows, rows), rows)
@@ -293,50 +299,65 @@
         slot = lines + k - 1
         return push(sums.at[k - 1, piece(p)], landed.at[k - 1, piece(p)], send_sem.at[slot, p], recv_sem.at[slot, p], peer)
 
-    def side_copy(i, k):
-        src, dst = ((head, head_land), (wide, wide_land))[i]
+    def to_group(src, dst, send, recv, mate):
         return pltpu.make_async_remote_copy(
-            src_ref=src.at[mates[k - 1]], dst_ref=dst.at[k - 1],
-            send_sem=side_send.at[i, k - 1], recv_sem=side_recv.at[i, k - 1],
-            device_id={"fsdp": mates[k - 1]}, device_id_type=MESH)
-
+            src_ref=src, dst_ref=dst, send_sem=send, recv_sem=recv, device_id={"fsdp": mate}, device_id_type=MESH)
+
+    both = ((head, head_own, head_land, head_pair, head_far), (wide, wide_own, wide_land, wide_pair, wide_far))
+
+    def near_copy(i, c):
+        src, _, dst, _, _ = both[i]
+        return to_group(
+            src.at[2 * c + 1 - parity], dst.at[c], near_send.at[i, c], near_recv.at[i, c], 2 * chip + 1 - parity)
+
+    def near_own(i, c):
+        return pltpu.make_async_copy(both[i][0].at[2 * c + parity], both[i][1].at[c], near_load.at[i, c])
+
+    def far_copy(i, k):
+        dest = (chip + k) % chips
+        return to_group(
+            both[i][3].at[dest], both[i][4].at[k - 1], far_send.at[i, k - 1], far_recv.at[i, k - 1], 2 * dest + parity)
+
+    for i in range(2):
+        for c in range(chips):
+            near_copy(i, c).start()
+            near_own(i, c).start()
     for k in list(range(1, lines)) + [0]:
         for p in range(pieces):
             first_copy(k, p).start()
             load(k, p).start()
-    own_copies = [
-        pltpu.make_async_copy(head.at[group], head_own, side_load.at[0]),
-        pltpu.make_async_copy(wide.at[group], wide_own, side_load.at[1]),
-    ]
-    for copy in own_copies:
-        copy.start()
     for i in range(2):
-        for k in range(1, groups):
-            side_copy(i, k).start()
+        _, own, land, pairs, _ = both[i]
+        for c in range(chips):
+            near_own(i, c).wait()
+            near_copy(i, c).wait_recv()
+            pairs[c] = (own[c].astype(f32) + land[c].astype(f32)).astype(bf)
+        for k in range(1, chips):
+            far_copy(i, k).start()
 
     def add(k, p):
         first_copy(k, p).wait_recv()
         load(k, p).wait()
-        return mine[k, piece(p)].astype(jnp.float32) + got[k, piece(p)].astype(jnp.float32)
+        return mine[k, piece(p)].astype(f32) + got[k, piece(p)].astype(f32)
 
     def step(s, _):
         k, p = 1 + s // pieces, s % pieces
-        sums[k - 1, piece(p)] = add(k, p).astype(jnp.bfloat16)
+        sums[k - 1, piece(p)] = add(k, p).astype(bf)
         second_copy(k, p).start()
         return 0
 
     lax.fori_loop(0, (lines - 1) * pieces, step, 0)
 
-    for copy in own_copies:
-        copy.wait()
-    total, side = head_own[...].astype(jnp.float32), wide_own[...].astype(jnp.float32)
-    for k in range(1, groups):
-        side_copy(0, k).wait_recv()
-        side_copy(1, k).wait_recv()
-        total = total + head_land[k - 1].astype(jnp.float32)
-        side = side + wide_land[k - 1].astype(jnp.float32)
-    o_out[...] = side
-    head_sum[...] = total.astype(jnp.bfloat16)
+    def joined(i):
+        _, own, land, _, far = both[i]
+        total = own[chip].astype(f32) + land[chip].astype(f32)
+        for k in range(1, chips):
+            far_copy(i, k).wait_recv()
+            total = total + far[k - 1].astype(f32)
+        return total
+
+    head_sum[...] = joined(0).astype(bf)
+    o_out[...] = joined(1)
     count = o_out.shape[0]
 
     def swap(k):
@@ -346,136 +367,124 @@
     for k in range(1, n):
         swap(k).start()
     head_got[me] = head_sum[pl.ds(pl.multiple_of(me * count, count), count), :]
+    gain_acc[...] = jnp.zeros_like(gain_acc)
 
     def finish(p, _):
         total = add(0, p)
         for k in range(1, lines):
             second_copy(k, p).wait_recv()
-            total += landed[k - 1, piece(p)].astype(jnp.float32)
-        out[piece(p), :] = total
+            total += landed[k - 1, piece(p)].astype(f32)
+        x = tokens[piece(p), :].astype(f32)
+        factor = lax.rsqrt(jnp.mean(x * x, axis=-1, keepdims=True) + epsilon)
+        normal = x * factor
+        gain_acc[...] += jnp.sum(total * normal, axis=0, keepdims=True)
+        weighted = total * gains[0:1, :]
+        back = factor * (weighted - normal * jnp.mean(weighted * normal, axis=-1, keepdims=True))
+        tokens_grad[piece(p), :] = mid_grad[piece(p), :] + back
         return 0
 
     lax.fori_loop(0, pieces, finish, 0)
+    span = own_gains.shape[1]
+    gain_send[...] = jnp.zeros_like(gain_send)
+    for s in range(n):
+        gain_send[s, 0:1, :] = gain_acc[:, s * span : (s + 1) * span]
+        gain_send[s, 1:2, :] = gain_term[:, s * span : (s + 1) * span]
+
+    def gain_copy(k):
+        return push(
+            gain_send.at[peers[k - 1]], gain_got.at[k - 1], gain_sends.at[k - 1], gain_recvs.at[k - 1], peers[k - 1])
+
+    def gain_side(k):
+        return to_group(gain_sum, gain_far.at[k - 1], side_sends.at[k - 1], side_recvs.at[k - 1], mates[k - 1])
+
+    for k in range(1, n):
+        gain_copy(k).start()
     for k in range(1, n):
         swap(k).wait_recv()
-    span = head.shape[2] // 3
     for s in range(n):
         for i, o in enumerate((q_out, k_out, v_out)):
-            o[:, s * span : (s + 1) * span] = head_got[s, :, i * span : (i + 1) * span].astype(jnp.float32)
+            o[:, s * span : (s + 1) * span] = head_got[s, :, i * span : (i + 1) * span].astype(f32)
+    total = gain_send[me] + own_gains[...]
+    for k in range(1, n):
+        gain_copy(k).wait_recv()
+        total = total + gain_got[k - 1]
+    gain_sum[...] = total
+    for k in range(1, groups):
+        gain_side(k).start()
+    for k in range(1, groups):
+        gain_side(k).wait_recv()
+        total = total + gain_far[k - 1]
+    gain_out[...] = total
     for p in range(pieces):
         for k in range(lines):
             first_copy(k, p).wait_send()
         for k in range(1, lines):
             second_copy(k, p).wait_send()
     for i in range(2):
-        for k in range(1, groups):
-            side_copy(i, k).wait_send()
+        for c in range(chips):
+            near_copy(i, c).wait_send()
+        for k in range(1, chips):
+            far_copy(i, k).wait_send()
     for k in range(1, n):
         swap(k).wait_send()
-
-
-def reduce_sides(part, head, wide, n, groups, pieces, collective_id):
+        gain_copy(k).wait_send()
+    for k in range(1, groups):
+        gain_side(k).wait_send()
+
+
+def finish_rows(part, head, wide, tokens, mid_grad, gains, gain_term, own_gains, n, groups, pieces, collective_id):
     _, rows, width = part.shape
     _, blocks, outs = head.shape
     count = blocks // n
-    lines = n // 2
+    lines, chips = n // 2, groups // 2
     slots = lines + lines - 1
     hbm = pl.BlockSpec(memory_space=ANY)
     vmem = pl.BlockSpec(memory_space=pltpu.VMEM)
     f32, bf = jnp.float32, jnp.bfloat16
     grad = jax.ShapeDtypeStruct((count, n * outs // 3), f32)
-    return pl.pallas_call(
-        functools.partial(reduce_sides_kernel, n, groups, pieces),
+    cell = own_gains.shape
+    far = max(1, chips - 1)
+    dma = pltpu.SemaphoreType.DMA
+    return pl.pallas_call(
+        functools.partial(finish_kernel, n, groups, pieces),
         out_shape=(
             jax.ShapeDtypeStruct((rows, width), f32),
             grad, grad, grad,
             jax.ShapeDtypeStruct((count, wide.shape[2]), f32),
+            jax.ShapeDtypeStruct(cell, f32),
         ),
-        in_specs=[hbm] * 3,
-        out_specs=[vmem] * 5,
+        in_specs=[hbm] * 3 + [vmem] * 5,
+        out_specs=[vmem] * 6,
         scratch_shapes=[
             pltpu.VMEM((lines, rows, width), bf),
             pltpu.VMEM((lines, rows, width), bf),
             pltpu.VMEM((lines - 1, rows, width), bf),
             pltpu.VMEM((lines - 1, rows, width), bf),
-            pltpu.VMEM((blocks, outs), bf),
-            pltpu.VMEM((groups - 1, blocks, outs), bf),
-            pltpu.VMEM((count, wide.shape[2]), bf),
-            pltpu.VMEM((groups - 1, count, wide.shape[2]), bf),
+            pltpu.VMEM((chips, blocks, outs), bf),
+            pltpu.VMEM((chips, blocks, outs), bf),
+            pltpu.VMEM((chips, blocks, outs), bf),
+            pltpu.VMEM((far, blocks, outs), bf),
+            pltpu.VMEM((chips, count, wide.shape[2]), bf),
+            pltpu.VMEM((chips, count, wide.shape[2]), bf),
+            pltpu.VMEM((chips, count, wide.shape[2]), bf),
+            pltpu.VMEM((far, count, wide.shape[2]), bf),
             pltpu.VMEM((blocks, outs), bf),
             pltpu.VMEM((n, count, outs), bf),
-            pltpu.SemaphoreType.DMA((slots, pieces)),
-            pltpu.SemaphoreType.DMA((slots, pieces)),
-            pltpu.SemaphoreType.DMA((lines, pieces)),
-            pltpu.SemaphoreType.DMA((2, groups - 1)),
-            pltpu.SemaphoreType.DMA((2, groups - 1)),
-            pltpu.SemaphoreType.DMA((2,)),
-            pltpu.SemaphoreType.DMA((n - 1,)),
-            pltpu.SemaphoreType.DMA((n - 1,)),
+            pltpu.VMEM((1, width), f32),
+            pltpu.VMEM((n,) + cell, f32),
+            pltpu.VMEM((n - 1,) + cell, f32),
+            pltpu.VMEM(cell, f32),
+            pltpu.VMEM((groups - 1,) + cell, f32),
+            dma((slots, pieces)), dma((slots, pieces)), dma((lines, pieces)),
+            dma((2, chips)), dma((2, chips)), dma((2, chips)), dma((2, far)), dma((2, far)),
+            dma((n - 1,)), dma((n - 1,)), dma((n - 1,)), dma((n - 1,)), dma((groups - 1,)), dma((groups - 1,)),
         ],
         compiler_params=pltpu.CompilerParams(
             collective_id=collective_id, has_side_effects=True, vmem_limit_bytes=50 << 20
         ),
-        cost_estimate=work(105),
-        name="reduce_sides",
-    )(part, head, wide)
-
-
-def gains_kernel(n, groups, sent, own, out, taken, summed, landed, send_sem, recv_sem, side_send, side_recv):
-    me, group = lax.axis_index("seq"), lax.axis_index("fsdp")
-    barrier = pltpu.get_barrier_semaphore()
-    peers = [(me + k) % n for k in range(1, n)]
-    mates = [(group + k) % groups for k in range(1, groups)]
-    for peer in peers:
-        pl.semaphore_signal(barrier, inc=1, device_id={"seq": peer}, device_id_type=MESH)
-    for mate in mates:
-        pl.semaphore_signal(barrier, inc=1, device_id={"fsdp": mate}, device_id_type=MESH)
-    pl.semaphore_wait(barrier, n - 1 + groups - 1)
-    copies = []
-    for k in range(1, n):
-        copy = push(sent.at[peers[k - 1]], taken.at[k - 1], send_sem.at[k - 1], recv_sem.at[k - 1], peers[k - 1])
-        copy.start()
-        copies.append(copy)
-    total = sent[me] + own[...]
-    for k in range(1, n):
-        copies[k - 1].wait_recv()
-        total = total + taken[k - 1]
-    summed[...] = total
-    sides = []
-    for k in range(1, groups):
-        side = pltpu.make_async_remote_copy(
-            src_ref=summed, dst_ref=landed.at[k - 1], send_sem=side_send.at[k - 1], recv_sem=side_recv.at[k - 1],
-            device_id={"fsdp": mates[k - 1]}, device_id_type=MESH)
-        side.start()
-        sides.append(side)
-    for k in range(1, groups):
-        sides[k - 1].wait_recv()
-        total = total + landed[k - 1]
-    out[...] = total
-    for copy in copies + sides:
-        copy.wait_send()
-
-
-def sum_gains(sent, own, n, groups, collective_id):
-    shape = own.shape
-    return pl.pallas_call(
-        functools.partial(gains_kernel, n, groups),
-        out_shape=jax.ShapeDtypeStruct(shape, own.dtype),
-        in_specs=[pl.BlockSpec(memory_space=pltpu.VMEM)] * 2,
-        out_specs=pl.BlockSpec(memory_space=pltpu.VMEM),
-        scratch_shapes=[
-            pltpu.VMEM((n - 1,) + shape, own.dtype),
-            pltpu.VMEM(shape, own.dtype),
-            pltpu.VMEM((groups - 1,) + shape, own.dtype),
-            pltpu.SemaphoreType.DMA((n - 1,)),
-            pltpu.SemaphoreType.DMA((n - 1,)),
-            pltpu.SemaphoreType.DMA((groups - 1,)),
-            pltpu.SemaphoreType.DMA((groups - 1,)),
-        ],
-        compiler_params=pltpu.CompilerParams(collective_id=collective_id, has_side_effects=True),
-        cost_estimate=work(10),
-        name="sum_gains",
-    )(sent, own)
+        cost_estimate=work(110),
+        name="finish_rows",
+    )(part, head, wide, tokens, mid_grad, gains, gain_term, own_gains)
 
 
 def slots_of(w, experts, capacity):
@@ -583,6 +592,35 @@
     )(weights, y)
 
 
+def unplace_split_kernel(experts, w_ref, y_ref, *outs):
+    capacity, width = y_ref.shape[1:]
+    hits, _ = slots_of(w_ref[0], experts, capacity)
+    out = down_rows(hits, y_ref[...].reshape(experts * capacity, width)).astype(y_ref.dtype)
+    for k, o_ref in enumerate(outs):
+
+        @pl.when(pl.program_id(0) == k)
+        def _():
+            o_ref[...] = out
+
+
+def unplace_split(weights, y, capacity):
+    n, _, tokens = weights.shape
+    experts, _, width = y.shape
+    return pl.pallas_call(
+        functools.partial(unplace_split_kernel, experts),
+        grid=(n,),
+        out_shape=[jax.ShapeDtypeStruct((tokens, width), y.dtype)] * n,
+        in_specs=[
+            pl.BlockSpec((1, 8, tokens), lambda c: (c, 0, 0)),
+            pl.BlockSpec((experts, capacity, width), lambda c: (0, c, 0)),
+        ],
+        out_specs=[pl.BlockSpec((tokens, width), lambda c: (0, 0))] * n,
+        compiler_params=pltpu.CompilerParams(vmem_limit_bytes=40 << 20),
+        cost_estimate=work(12),
+        name="unplace_split",
+    )(weights, y)
+
+
 def widen_kernel(x_ref, o_ref):
     for e in range(x_ref.shape[0]):
         o_ref[:, e, :] = x_ref[e].astype(jnp.float32)
@@ -590,7 +628,7 @@
 
 def widen(x):
     experts, rows, columns = x.shape
-    step = min(128, rows)
+    step = min(256, rows)
     return pl.pallas_call(
         widen_kernel,
         grid=(rows // step,),
@@ -738,6 +776,53 @@
         cost_estimate=work(60),
         name="attend_back",
     )(q, k, v, g, o, lse)
+
+
+def rows_kernel(a_ref, b_ref, wa_ref, wb_ref, o_ref):
+    o_ref[0] = (across_lanes(a_ref[0], wa_ref[0]) + across_lanes(b_ref[0], wb_ref[0])).astype(o_ref.dtype)
+
+
+def rows_sum(a, b, wa, wb, tile):
+    experts, rows, hidden = a.shape
+    width = wa.shape[1]
+    rows_spec = pl.BlockSpec((1, tile, hidden), lambda e, i: (e, i, 0))
+    weights = pl.BlockSpec((1, width, hidden), lambda e, i: (e, 0, 0))
+    return pl.pallas_call(
+        rows_kernel,
+        grid=(experts, rows // tile),
+        out_shape=jax.ShapeDtypeStruct((experts, rows, width), jnp.bfloat16),
+        in_specs=[rows_spec] * 2 + [weights] * 2,
+        out_specs=pl.BlockSpec((1, tile, width), lambda e, i: (e, i, 0)),
+        compiler_params=pltpu.CompilerParams(vmem_limit_bytes=50 << 20),
+        cost_estimate=work(36),
+        name="rows_sum",
+    )(a, b, wa, wb)
+
+
+def slopes_kernel(g_ref, w_ref, gate_ref, up_ref, dg_ref, du_ref):
+    back = jnp.dot(g_ref[0], w_ref[0], preferred_element_type=jnp.float32)
+    gate, up = gate_ref[0].astype(jnp.float32), up_ref[0].astype(jnp.float32)
+    s = jax.nn.sigmoid(gate)
+    dg_ref[0] = (back * up * (s * (1.0 + gate * (1.0 - s)))).astype(dg_ref.dtype)
+    du_ref[0] = (back * (gate * s)).astype(du_ref.dtype)
+
+
+def slopes(g, w, gate, up, tile):
+    experts, rows, width = g.shape
+    hidden = w.shape[2]
+    wide = pl.BlockSpec((1, tile, width), lambda e, i: (e, i, 0))
+    narrow = pl.BlockSpec((1, tile, hidden), lambda e, i: (e, i, 0))
+    out = jax.ShapeDtypeStruct((experts, rows, hidden), jnp.bfloat16)
+    return pl.pallas_call(
+        slopes_kernel,
+        grid=(experts, rows // tile),
+        out_shape=(out, out),
+        in_specs=[wide, pl.BlockSpec((1, width, hidden), lambda e, i: (e, 0, 0)), narrow, narrow],
+        out_specs=[narrow] * 2,
+        compiler_params=pltpu.CompilerParams(vmem_limit_bytes=50 << 20),
+        cost_estimate=work(20),
+        name="slopes",
+    )(g, w, gate, up)
 
 
 def project_kernel(
@@ -1163,7 +1248,7 @@
     )
     w_up, w_down, squares = barrier((w_up, w_down, squares))
     full_up, full_down = by_expert(w_up), by_expert(w_down)
-    gain_attn, gain_ffn = gains[0], gains[3]
+    gain_ffn = gains[3]
     head_gains = lax.dynamic_slice(gains, (1, me * span), (2, span))
 
     expert_ids = jnp.arange(experts, dtype=jnp.int32)
@@ -1191,48 +1276,37 @@
     cot_others = [gather_across([v], n) for v in cot_halves]
     weights = jnp.pad(by_place(weights, n), ((0, 0), (0, 8 - local_experts), (0, 0)))
     received, slot_weight = place(weights, ffn_all, local_experts, capacity)
-    gate = jnp.einsum("erd,edf->erf", received, full_gate, preferred_element_type=f32)
+    gate_low = jnp.einsum("erd,edf->erf", received, full_gate, preferred_element_type=f32).astype(bf)
     cot_others[0] += gather_across(cot_columns[0], n)
     cot_others[1] += gather_across(cot_columns[1], n)
     up_part = jnp.einsum("erd,edf->erf", received, full_up, preferred_element_type=f32)
-    sigmoid_gate = jax.nn.sigmoid(gate)
-    activated = gate * sigmoid_gate
-    hidden = (activated * up_part).astype(bf)
+    gate = gate_low.astype(f32)
+    hidden = (gate * jax.nn.sigmoid(gate) * up_part).astype(bf)
+    up_low = up_part.astype(bf)
     expert_out = jnp.einsum("erf,edf->erd", hidden, full_down, preferred_element_type=f32)
     expert_out = (expert_out * slot_weight).astype(bf)
-    ffn_part = unplace(weights, expert_out, capacity)
+    ffn_part = unplace_split(weights, expert_out, capacity)
     ffn_part, cot_others = barrier((ffn_part, cot_others))
     cot_pieces = [
         v for pair in zip(*(([h] + c + o) for h, c, o in zip(cot_halves, cot_columns, cot_others))) for v in pair
     ]
     lines = n // 2
     ffn_got = {k: gather_across([ffn_part[lines + k]], n)[0] for k in list(range(1, lines)) + [0]}
-    ffn_keep = [barrier(ffn_part[k]) for k in range(lines)]
-    ffn_sum = lambda k: (ffn_keep[k].astype(f32) + ffn_got[k].astype(f32)).astype(bf)
+    ffn_sum = lambda k: (ffn_part[k].astype(f32) + ffn_got[k].astype(f32)).astype(bf)
 
     out_grad = cotangent.reshape(rows, width).astype(f32)
     down_received = place_weighted(weights, cot_pieces, local_experts, capacity)
-    hidden_grad = jnp.einsum("erd,edf->erf", down_received, full_down, preferred_element_type=f32)
-    slope = sigmoid_gate * (1.0 + gate * (1.0 - sigmoid_gate))
-    gate_grad = (hidden_grad * up_part * slope).astype(bf)
-    up_grad = (hidden_grad * activated).astype(bf)
-    early = list(range(1, lines - 1))
-    gate_grad, up_grad, got = barrier((gate_grad, up_grad, [ffn_got[k] for k in early]))
-    ffn_got.update(zip(early, got))
-    ffn_pieces = [reduce_column(ffn_sum(k), k, n) for k in early]
-    rows_gate = jnp.einsum("erf,edf->erd", gate_grad, full_gate, preferred_element_type=f32)
-    rows_gate, ffn_got[lines - 1] = barrier((rows_gate, ffn_got[lines - 1]))
-    ffn_pieces.append(reduce_column(ffn_sum(lines - 1), lines - 1, n))
-    rows_up = jnp.einsum("erf,edf->erd", up_grad, full_up, preferred_element_type=f32)
-    rows_grad = (rows_gate + rows_up).astype(bf)
-    rows_part = unplace(weights, rows_grad, capacity)
-    down_term = jnp.einsum("erd,erf->edf", down_received, hidden, preferred_element_type=f32)
+    down_term = jnp.einsum("erd,erf->edf", down_received, hidden, preferred_element_type=f32).astype(bf)
+    gate_grad, up_grad = slopes(down_received, full_down, gate_low, up_low, 256)
+    gate_grad, up_grad, got = barrier((gate_grad, up_grad, [ffn_got[k] for k in range(1, lines)]))
+    ffn_got.update(zip(range(1, lines), got))
+    ffn_pieces = [reduce_column(ffn_sum(k), k, n) for k in range(1, lines)]
+    rows_part = unplace(weights, rows_sum(gate_grad, up_grad, full_gate, full_up, n * capacity), capacity)
     scatter = lambda v: lax.psum_scatter(v, "fsdp", scatter_dimension=1, tiled=True)
-    rows_part, ffn_pieces, ffn_got[0] = barrier((rows_part, ffn_pieces, ffn_got[0]))
     ffn_in_grad, gate_term, up_term = reduce_terms(
         rows_part, received, gate_grad, up_grad, n, 8, 512, 4
     )
-    scattered = [scatter(down_term.astype(bf))]
+    scattered = [scatter(down_term)]
     scattered += [scatter(gate_term), scatter(up_term)]
     mid_back, ffn_gain_term = norm_backward(mid, norm_two, gain_ffn, ffn_in_grad)
     mid_grad = out_grad + mid_back
@@ -1251,21 +1325,15 @@
     normed_part = jnp.einsum("te,de->td", proj_grad, w_heads, preferred_element_type=f32).astype(bf)
     head_term = jnp.einsum("td,te->de", normed, proj_grad, preferred_element_type=f32).astype(bf)
     head_term = head_term.reshape(n, groups, part, 3 * span).swapaxes(0, 1)
-    block_out = mid + sum(piece.astype(f32) for piece in [ffn_keep[0], ffn_got[0]] + ffn_pieces)
-    normed_grad, *head_sums, out_sum = reduce_sides(
+    block_out = mid + sum(piece.astype(f32) for piece in [ffn_part[0], ffn_got[0]] + ffn_pieces)
+    tokens_grad, *head_sums, out_sum, gain_sums = finish_rows(
         normed_part.reshape(n, rows, width),
         head_term.reshape(groups, n * part, 3 * span),
         out_term.reshape(groups, part, width),
-        n, groups, 8, 7,
+        own_tokens, mid_grad, gains, ffn_gain_term[None], gain_terms, n, groups, 8, 7,
     )
-    scattered, normed_grad = barrier((scattered, normed_grad))
+    scattered, tokens_grad = barrier((scattered, tokens_grad))
     down_sum, gate_sum, up_sum = [widen(v) for v in scattered]
-    input_back, attn_gain_term = norm_backward(inputs, inverse_norm(inputs), gain_attn, normed_grad)
-    tokens_grad = mid_grad + input_back
-    by_span = lambda v: v.reshape(n, 1, span)
-    sent_gains = jnp.concatenate([by_span(attn_gain_term), by_span(ffn_gain_term)], axis=1)
-    sent_gains = jnp.pad(sent_gains, ((0, 0), (0, 6), (0, 0)))
-    gain_sums = sum_gains(sent_gains, gain_terms, n, groups, 8)
     gain_sums = lax.dynamic_slice_in_dim(gain_sums, lax.axis_index("fsdp") * part, part, 1)
     return (
         block_out.astype(bf).reshape(tokens.shape),

time: 1170 us -> 1200 us (1.026)
  waiting for transfers between devices: 82.8 us -> 165 us
  matrix products: 206 us -> 131 us
  Pallas kernels: 721 us -> 779 us
  other arithmetic: 46.5 us -> 20.6 us
    dot_general x3 -> x0, matrix products: 81.7 us -> none  [the longest x1 35 us: local(): jnp.einsum('erd,edf->erf', down_received, full_down, preferred_element_ty...]
    pallas_call x2 -> x4, Pallas kernels: 129 us -> 202 us  [the longest x1 126 us: finish_rows(): pl.pallas_call(functools.partial(finish_kernel, n, groups, pieces), out_s...]
    ppermute x3, waiting for transfers between devices: 0.01 us -> 56 us  [reduce_column(): return lax.ppermute(v, 'seq', along_lines(n // 2, 2, n // 2 - k))]
    ppermute x12, waiting for transfers between devices: 56.1 us -> 78.3 us  [gather_across(): return [lax.ppermute(c, 'seq', across_pairs(n // 2, 2)) for c in column]]
    convert_element_type x4 -> x3, other arithmetic: 27.6 us -> 7.73 us  [local(): (ffn_part[k].astype(f32) + ffn_got[k].astype(f32)).astype(bf)]
    pallas_call x1, Pallas kernels: 119 us -> 100 us  [reduce_terms(): pl.pallas_call(functools.partial(reduce_terms_kernel, n, pieces, tile), o...]
    pallas_call x2, Pallas kernels: 216 us -> 234 us  [gather_rows(): pl.pallas_call(functools.partial(gather_kernel, n, pieces, by_index), out...]
    pallas_call x2 -> x1, Pallas kernels: 25.5 us -> 12.8 us  [unplace(): pl.pallas_call(functools.partial(unplace_kernel, experts), grid=(n,), out...]
  transfers between devices with their start and end apart: 29 -> 29, of which waited for: 9 -> 11; matrix products, arithmetic and copies ran while one was open for 22% -> 12% of each run, Pallas kernels for 58% -> 63%
where the time goes in v3:
time: 1200 us; the launch traced here: 1190 us
  Pallas kernels  779 us (65%)
  waiting for transfers between devices  165 us (14%)
  matrix products  131 us (11%)
  local copies, waits for them, and re-layouts  47.8 us (4%)
  starting transfers between devices  32.7 us (3%)
  other arithmetic  20.6 us (2%)
  between operations  15.4 us (1%)
    pallas_call x2, Pallas kernels, gather_rows(): pl.pallas_call(functools.partial(gather_kernel, n, pieces, by_index), out...  234 us
    pallas_call x1, Pallas kernels, finish_rows(): pl.pallas_call(functools.partial(finish_kernel, n, groups, pieces), out_s...  126 us
    pallas_call x1, Pallas kernels, project_rows(): pl.pallas_call(functools.partial(project_kernel, n, groups, pieces), out_...  120 us
    pallas_call x1, Pallas kernels, reduce_terms(): pl.pallas_call(functools.partial(reduce_terms_kernel, n, pieces, tile), o...  100 us
    ppermute x12, waiting for transfers between devices, gather_across(): return [lax.ppermute(c, 'seq', across_pairs(n // 2, 2)) for c in column]  78.3 us
    ppermute x3, waiting for transfers between devices, reduce_column(): return lax.ppermute(v, 'seq', along_lines(n // 2, 2, n // 2 - k))  56 us
    pallas_call x1, Pallas kernels, rows_sum(): pl.pallas_call(rows_kernel, grid=(experts, rows // tile), out_shape=jax.S...  33 us
    unnamed x120, local copies, waits for them, and re-layouts  32.5 us
  transfers between devices with their start and end apart: 29, of which 11 were waited for; matrix products, arithmetic and copies ran while one was open for 12% of the time, Pallas kernels for 63%

profile of v3, /device:TPU:0, one launch (start us, length us, event | category | flops | bytes accessed | tf_op | source)
XLA Modules:
  0.0 1191.4 jit_solution(13130922072400623622)
XLA Ops:
  8.0 5.7 copy.55
  14.0 120.1 %project_rows.1 = (bf16[2048,2048]{1,0:T(8,128)(2,1)}, f32[2048,768]{1,0:T(8,128)}, f32[16,256]{1,0:T(8,128)S(1)}, bf16[2048,768]{1,0:T(8,128)(2,1)}, f32[8,2048]{1,0:T(8,128)S(1)}) custom-call(bf16[256,2048]{1,0:T(8,128)(2,1)S(1)} %bitcast.66, bf16[512,2048]{1,0:T(8,128)(2,1)S(1)} %copy-done.18, bf16[512,2048]{1,0:T(8,128)(2,1)} %w_key.1, ...), custom_call_target="tpu_custom_call" | custom-call | flops 65999998976 | tf_op jit(solution)/shard_map/project_rows/pallas_call | solution.py:951
  134.1 3.4 copy.54
  137.6 5.6 copy.53
  144.2 3.0 copy-done.21
  147.2 11.4 rotate_rows.1
  161.6 15.9 %attend.1 = (bf16[2048,256]{1,0:T(8,128)(2,1)}, f32[2,1,2048]{2,1,0:T(1,128)}) custom-call(bf16[2048,256]{1,0:T(8,128)(2,1)} %copy-done.23, bf16[2048,256]{1,0:T(8,128)(2,1)} %copy-done.24, bf16[2048,256]{1,0:T(8,128)(2,1)} %copy-done.25), custom_call_target="tpu_custom_call" | custom-call | flops 15000000512 | tf_op jit(solution)/shard_map/attend/pallas_call | solution.py:698
  177.5 2.3 copy.43
  179.7 4.7 all-to-all-start
  185.9 22.4 %all-to-all-done = bf16[8,256,256]{1,2,0:T(8,128)(2,1)S(1)} async-done(((bf16[8,256,256]{1,2,0:T(8,128)(2,1)}), bf16[8,256,256]{1,2,0:T(8,128)(2,1)S(1)}, u32[]{:S(2)}, u32[]{:S(2)}) %all-to-all-start) | async-done | bytes 1048608 | tf_op jit(solution)/shard_map/all_to_all | solution.py:1264
  209.3 7.3 multiply_reduce_fusion.2
  216.6 1.4 multiply_convert_fusion.1.own
  218.0 108.6 %gather_rows.2.x_ref = bf16[8,256,2048]{2,1,0:T(8,128)(2,1)} custom-call(bf16[256,2048]{1,0:T(8,128)(2,1)} %multiply_convert_fusion.1.own), custom_call_target="tpu_custom_call" | custom-call | flops 62999998464 | tf_op jit(solution)/shard_map/gather_rows/pallas_call | solution.py:86
  326.9 6.6 collective-permute-start.12
  334.1 3.2 collective-permute-start.5
  337.3 12.8 %place.1 = (bf16[4,768,2048]{2,1,0:T(8,128)(2,1)}, f32[4,768,1]{2,1,0:T(8,128)}) custom-call(f32[8,8,256]{2,1,0:T(8,128)} %pad.12.w_ref, bf16[8,256,2048]{2,1,0:T(8,128)(2,1)} %gather_rows.2.x_ref), custom_call_target="tpu_custom_call" | custom-call | flops 6000000000 | tf_op jit(solution)/shard_map/place/pallas_call | solution.py:519
  350.1 2.0 reduce
  352.1 22.1 %convolution_convert_fusion.2.gate_ref = bf16[4,768,1024]{2,1,0:T(8,128)(2,1)} fusion(bf16[4,768,2048]{2,1,0:T(8,128)(2,1)} %get-tuple-element.91.x, bf16[4,2048,1024]{2,1,0:T(8,128)(2,1)} %all-gather.7.cloned.1.call-done.wa_ref), kind=kOutput, calls=%fused_computation.14 | convolution fusion | flops 12888047616 | bytes 35651584 | tf_op jit(solution)/shard_map/erd,edf->erf/dot_general | solution.py:1279
  374.2 23.3 %fusion.23 = (bf16[4,768,1024]{2,1,0:T(8,128)(2,1)}, f32[4,768,1024]{2,1,0:T(8,128)}) fusion(bf16[4,768,2048]{2,1,0:T(8,128)(2,1)} %get-tuple-element.91.x, bf16[4,2048,1024]{2,1,0:T(8,128)(2,1)} %all-gather.9.cloned.1.call-done.wb_ref), kind=kOutput, calls=%fused_computation.63 | convolution fusion | flops 12888047616 | bytes 48234496 | tf_op jit(solution)/shard_map/erd,edf->erf/dot_general | solution.py:1282
  397.5 1.3 collective-permute-start.3
  398.9 2.0 collective-permute-start
  400.9 7.0 all-gather.11.cloned.1.call-done.w_ref
  407.9 24.9 %multiply_convert_fusion.y_ref = bf16[4,768,2048]{2,1,0:T(8,128)(2,1)} fusion(f32[4,768]{1,0:T(4,128)S(1)} %reduce, bf16[4,2048,1024]{2,1,0:T(8,128)(2,1)} %all-gather.11.cloned.1.call-done.w_ref, f32[4,768,1024]{2,1,0:T(8,128)} %get-tuple-element.167, bf16[4,768,1024]{2,1,0:T(8,128)(2,1)} %convolution_convert_fusion.2.gate_ref), kind=kOutput, calls=%fused_computation.1 | convolution fusion | flops 12919504896 | bytes 48246784 | tf_op jit(solution)/shard_map/erf,edf->erd/dot_general | solution.py:1286
  432.8 1.5 collective-permute-start.11
  434.9 1.4 collective-permute-start.6
  439.1 11.1 unplace_split.1
  455.1 4.1 collective-permute-done.9.refs_11_
  459.2 11.2 collective-permute-done.6.refs_14_
  470.4 11.2 collective-permute-done.4.refs_12_
  481.7 10.5 collective-permute-done.2.refs_10_
  492.1 12.2 %place_weighted.1.g_ref = bf16[4,768,2048]{2,1,0:T(8,128)(2,1)} custom-call(f32[8,8,256]{2,1,0:T(8,128)} %pad.12.w_ref, bf16[128,2048]{1,0:T(8,128)(2,1)} %copy-done.39, bf16[128,2048]{1,0:T(8,128)(2,1)} %copy-done.38, bf16[128,2048]{1,0:T(8,128)(2,1)} %collective-permute-done.1.refs_2_, bf16[128,2048]{1,0:T(8,128)(2,1)} %collective-permute-done.8.refs_3_, ...), custom_call_target="tpu_custom_call" | custom-call | flops 7200000000 | tf_op jit(solution)/shard_map/place_weighted/pallas_call | solution.py:559
  504.4 25.1 %convolution_convert_fusion = bf16[4,2048,1024]{2,1,0:T(8,128)(2,1)} fusion(bf16[4,768,2048]{2,1,0:T(8,128)(2,1)} %place_weighted.1.g_ref, f32[4,768,1024]{2,1,0:T(8,128)} %get-tuple-element.167, bf16[4,768,1024]{2,1,0:T(8,128)(2,1)} %convolution_convert_fusion.2.gate_ref), kind=kOutput, calls=%fused_computation.4 | convolution fusion | flops 12915310592 | bytes 48234496 | tf_op jit(solution)/shard_map/erd,erf->edf/dot_general | solution.py:1299
  529.5 1.6 collective-permute-start.15
  531.6 1.5 collective-permute-start.17
  533.1 32.4 %slopes.1 = (bf16[4,768,1024]{2,1,0:T(8,128)(2,1)}, bf16[4,768,1024]{2,1,0:T(8,128)(2,1)}) custom-call(bf16[4,768,2048]{2,1,0:T(8,128)(2,1)} %place_weighted.1.g_ref, bf16[4,2048,1024]{2,1,0:T(8,128)(2,1)} %all-gather.11.cloned.1.call-done.w_ref, bf16[4,768,1024]{2,1,0:T(8,128)(2,1)} %convolution_convert_fusion.2.gate_ref, ...), custom_call_target="tpu_custom_call" | custom-call | flops 12000000000 | tf_op jit(solution)/shard_map/slopes/pallas_call | solution.py:816
  565.5 12.8 %collective-permute-done.16 = bf16[256,2048]{1,0:T(8,128)(2,1)S(1)} collective-permute-done((bf16[256,2048]{1,0:T(8,128)(2,1)S(1)}, bf16[256,2048]{1,0:T(8,128)(2,1)S(1)}, u32[]{:S(2)}, u32[]{:S(2)}) %collective-permute-start.16) | collective-permute-done | bytes 1048608 | tf_op jit(solution)/shard_map/ppermute | solution.py:1211
  578.3 20.9 %collective-permute-done.17 = bf16[256,2048]{1,0:T(8,128)(2,1)S(1)} collective-permute-done((bf16[256,2048]{1,0:T(8,128)(2,1)S(1)}, bf16[256,2048]{1,0:T(8,128)(2,1)S(1)}, u32[]{:S(2)}, u32[]{:S(2)}) %collective-permute-start.17) | collective-permute-done | bytes 1048608 | tf_op jit(solution)/shard_map/ppermute | solution.py:1211
  600.2 33.0 %rows_sum.1.y_ref = bf16[4,768,2048]{2,1,0:T(8,128)(2,1)} custom-call(bf16[4,768,1024]{2,1,0:T(8,128)(2,1)} %get-tuple-element.125.a_ref.first, bf16[4,768,1024]{2,1,0:T(8,128)(2,1)} %get-tuple-element.126.b_ref.second, bf16[4,2048,1024]{2,1,0:T(8,128)(2,1)} %all-gather.7.cloned.1.call-done.wa_ref, bf16[4,2048,1024]{2,1,0:T(8,128)(2,1)} %all-gather.9.cloned.1.call-done.wb_ref), custom_call_target="tpu_custom_call" | custom-call | flops 21600000000 | tf_op jit(solution)/shard_map/rows_sum/pallas_call | solution.py:790
  633.1 12.8 %unplace.1.part = bf16[8,256,2048]{2,1,0:T(8,128)(2,1)} custom-call(f32[8,8,256]{2,1,0:T(8,128)} %pad.12.w_ref, bf16[4,768,2048]{2,1,0:T(8,128)(2,1)} %rows_sum.1.y_ref), custom_call_target="tpu_custom_call" | custom-call | flops 6000000000 | tf_op jit(solution)/shard_map/unplace/pallas_call | solution.py:581
  645.9 100.1 %reduce_terms.1 = (f32[256,2048]{1,0:T(8,128)S(1)}, bf16[4,2048,1024]{2,1,0:T(8,128)(2,1)}, bf16[4,2048,1024]{2,1,0:T(8,128)(2,1)}) custom-call(bf16[8,256,2048]{2,1,0:T(8,128)(2,1)} %unplace.1.part, bf16[4,768,2048]{2,1,0:T(8,128)(2,1)} %get-tuple-element.91.x, bf16[4,768,1024]{2,1,0:T(8,128)(2,1)} %get-tuple-element.125.a_ref.first, ...), custom_call_target="tpu_custom_call" | custom-call | flops 62999998464 | tf_op jit(solution)/shard_map/reduce_terms/pallas_call | solution.py:232
  747.4 2.9 add_convert_fusion.2
  750.3 2.3 collective-permute-start.19
  752.7 3.5 add_convert_fusion.3
  756.1 1.4 add_convert_fusion.1
  757.5 2.0 collective-permute-start.20
  759.5 2.8 multiply_reduce_fusion
  762.3 7.6 collective-permute-done.14
  769.9 30.0 %collective-permute-done.19 = bf16[256,2048]{1,0:T(8,128)(2,1)} collective-permute-done((bf16[256,2048]{1,0:T(8,128)(2,1)}, bf16[256,2048]{1,0:T(8,128)(2,1)}, u32[]{:S(2)}, u32[]{:S(2)}) %collective-permute-start.19) | collective-permute-done | bytes 1048608 | tf_op jit(solution)/shard_map/ppermute | solution.py:1215
  799.9 26.1 %collective-permute-done.18 = bf16[256,2048]{1,0:T(8,128)(2,1)} collective-permute-done((bf16[256,2048]{1,0:T(8,128)(2,1)}, bf16[256,2048]{1,0:T(8,128)(2,1)}, u32[]{:S(2)}, u32[]{:S(2)}) %collective-permute-start.18) | collective-permute-done | bytes 1048608 | tf_op jit(solution)/shard_map/ppermute | solution.py:1215
  826.0 5.9 fusion.21
  831.8 125.5 %gather_rows.3 = bf16[8,256,2048]{2,1,0:T(8,128)(2,1)} custom-call(bf16[256,2048]{1,0:T(8,128)(2,1)} %get-tuple-element.151.own), custom_call_target="tpu_custom_call" | custom-call | flops 62999998464 | tf_op jit(solution)/shard_map/gather_rows/pallas_call | solution.py:86
  957.3 7.2 convolution_convert_fusion.5.g_ref
  964.6 22.1 %attend_back.1 = (bf16[2048,256]{1,0:T(8,128)(2,1)}, bf16[2048,256]{1,0:T(8,128)(2,1)}, bf16[2048,256]{1,0:T(8,128)(2,1)}) custom-call(bf16[2048,256]{1,0:T(8,128)(2,1)} %copy-done.23, bf16[2048,256]{1,0:T(8,128)(2,1)} %copy-done.24, bf16[2048,256]{1,0:T(8,128)(2,1)} %copy-done.25, bf16[2048,256]{1,0:T(8,128)(2,1)} %convolution_convert_fusion.5.g_ref, ...), custom_call_target="tpu_custom_call" | custom-call | flops 35999997952 | tf_op jit(solution)/shard_map/attend_back/pallas_call | solution.py:765
  986.7 2.8 copy-done.22
  993.2 18.1 %heads_back.1 = (bf16[2048,768]{1,0:T(8,128)(2,1)S(1)}, f32[8,256]{1,0:T(8,128)S(1)}) custom-call(bf16[2048,256]{1,0:T(8,128)(2,1)S(1)} %copy-done.26, bf16[2048,256]{1,0:T(8,128)(2,1)S(1)} %copy-done.27, bf16[2048,256]{1,0:T(8,128)(2,1)S(1)} %copy-done.28, f32[2048,768]{1,0:T(8,128)S(1)} %copy-done.22, f32[16,256]{1,0:T(8,128)S(1)} %get-tuple-element.134.factors, ...), custom_call_target="tpu_custom_call" | custom-call | flops 12000000000 | tf_op jit(solution)/shard_map/heads_back/pallas_call | solution.py:1145
  1011.3 9.4 convolution_convert_fusion.3
  1020.7 2.0 copy.48
  1022.8 2.3 convolution_convert_fusion.4
  1025.1 9.0 convolution_convert_fusion.1
  1034.1 125.6 %finish_rows.1 = (f32[256,2048]{1,0:T(8,128)}, f32[64,2048]{1,0:T(8,128)S(1)}, f32[64,2048]{1,0:T(8,128)S(1)}, f32[64,2048]{1,0:T(8,128)S(1)}, f32[64,2048]{1,0:T(8,128)S(1)}, /*index=5*/f32[8,256]{1,0:T(8,128)S(1)}) custom-call(bf16[8,256,2048]{2,1,0:T(8,128)(2,1)} %bitcast.87, bf16[4,512,768]{2,1,0:T(8,128)(2,1)} %bitcast.79, ...), custom_call_target="tpu_custom_call" | custom-call | flops 65999998976 | tf_op jit(solution)/shard_map/finish_rows/pallas_call | solution.py:448
  1160.3 5.8 widen.3
  1166.2 5.8 widen.4
  1172.0 5.8 widen.5
  1177.8 3.1 copy.61
  (184 shorter events, 27.0 us)
Async XLA Ops:
  7.2 201.2 %all-gather.5.cloned.1.call-start = ((), (), s32[]{:S(2)}) async-start(), calls=%async_computation.4 | async-start | bytes 10485760 | tf_op jit(solution)/shard_map/all_gather | solution.py:1243
  7.9 5.9 copy-start.47
  7.9 5.9 copy-start.48
  7.9 5.9 copy-start.49
  8.0 6.0 copy-start
  8.0 6.0 copy-start.18
  8.0 344.1 %all-gather.7.cloned.1.call-start = ((), (), s32[]{:S(2)}) async-start(), calls=%async_computation.5 | async-start | bytes 20971520 | tf_op jit(solution)/shard_map/all_gather | solution.py:1244
  13.8 360.4 %all-gather.9.cloned.1.call-start = ((), (), s32[]{:S(2)}) async-start(), calls=%async_computation.6 | async-start | bytes 20971520 | tf_op jit(solution)/shard_map/all_gather | solution.py:1244
  14.0 120.2 %copy-start.33 = (bf16[512,4,1024]{2,1,0:T(4,128)(2,1)S(1)}, bf16[512,4,1024]{2,1,0:T(4,128)(2,1)}, u32[]{:S(2)}) copy-start(bf16[512,4,1024]{2,1,0:T(4,128)(2,1)} %param.28) | copy-start | bytes 12582916
  134.1 50.4 %copy-start.16 = (f32[8,2048]{1,0:T(8,128)}, f32[8,2048]{1,0:T(8,128)S(1)}, u32[]{:S(2)}) copy-start(f32[8,2048]{1,0:T(8,128)S(1)} %get-tuple-element.84.gains) | copy-start | bytes 196612
  137.6 270.3 %all-gather.11.cloned.1.call-start = ((), (), s32[]{:S(2)}) async-start(), calls=%async_computation.7 | async-start | bytes 20971520 | tf_op jit(solution)/shard_map/all_gather | solution.py:1244
  143.5 15.1 %copy-start.14 = (f32[2,256]{1,0:T(2,128)}, f32[2,256]{1,0:T(2,128)S(1)}, u32[]{:S(2)}) copy-start(f32[2,256]{1,0:T(2,128)S(1)} %constant_dynamic-slice_fusion.1.gains) | copy-start | bytes 6148
  143.6 15.0 %copy-start.10 = (f32[8,128]{1,0:T(8,128)}, f32[8,128]{1,0:T(8,128)S(1)}, u32[]{:S(2)}) copy-start(f32[8,128]{1,0:T(8,128)S(1)} %get-tuple-element.160.far_sin) | copy-start | bytes 12292
  143.6 15.0 %copy-start.12 = (f32[8,128]{1,0:T(8,128)}, f32[8,128]{1,0:T(8,128)S(1)}, u32[]{:S(2)}) copy-start(f32[8,128]{1,0:T(8,128)S(1)} %get-tuple-element.161.far_cos) | copy-start | bytes 12292
  144.2 14.5 %copy-start.5 = (f32[256,128]{1,0:T(8,128)}, f32[256,128]{1,0:T(8,128)S(1)}, u32[]{:S(2)}) copy-start(f32[256,128]{1,0:T(8,128)S(1)} %get-tuple-element.162.near_sin) | copy-start | bytes 393220
  144.2 14.5 %copy-start.7 = (f32[256,128]{1,0:T(8,128)}, f32[256,128]{1,0:T(8,128)S(1)}, u32[]{:S(2)}) copy-start(f32[256,128]{1,0:T(8,128)S(1)} %get-tuple-element.163.near_cos) | copy-start | bytes 393220
  179.7 28.6 %all-to-all-start = ((bf16[8,256,256]{1,2,0:T(8,128)(2,1)}), bf16[8,256,256]{1,2,0:T(8,128)(2,1)S(1)}, u32[]{:S(2)}, u32[]{:S(2)}) async-start(bf16[8,256,256]{1,2,0:T(8,128)(2,1)} %copy.43), calls=%async_computation | async-start | bytes 2097152 | tf_op jit(solution)/shard_map/all_to_all | solution.py:1264
  184.4 975.9 %reduce-scatter.4.cloned.1.call-start = ((), (), s32[]{:S(2)}) async-start(), calls=%async_computation.8 | async-start | bytes 20971520 | tf_op jit(solution)/shard_map/reduce_scatter | solution.py:1305
  184.6 32.0 %copy-start.40 = (f32[1,2048]{1,0:T(1,128)}, f32[1,2048]{1,0:T(1,128)S(1)}, u32[]{:S(2)}) copy-start(f32[1,2048]{1,0:T(1,128)S(1)} %slice.21) | copy-start | bytes 24580
  216.6 110.1 %copy-start.29 = (f32[256,2048]{1,0:T(8,128)}, f32[256,2048]{1,0:T(8,128)S(1)}, u32[]{:S(2)}) copy-start(f32[256,2048]{1,0:T(8,128)S(1)} %get-tuple-element.165) | copy-start | bytes 6291460
  216.6 110.1 %copy-start.42 = (f32[256]{0:T(256)}, f32[256]{0:T(256)S(1)}, u32[]{:S(2)}) copy-start(f32[256]{0:T(256)S(1)} %add_rsqrt_fusion) | copy-start | bytes 3076
  218.0 108.7 %copy-start.32 = (bf16[1,256,2048]{2,1,0:T(8,128)(2,1)S(1)}, bf16[1,256,2048]{2,1,0:T(8,128)(2,1)}, u32[]{:S(2)}) copy-start(bf16[1,256,2048]{2,1,0:T(8,128)(2,1)} %param.18) | copy-start | bytes 3145732
  326.8 23.2 %copy-start.38 = (bf16[128,2048]{1,0:T(8,128)(2,1)}, bf16[128,2048]{1,0:T(8,128)(2,1)S(1)}, u32[]{:S(2)}) copy-start(bf16[128,2048]{1,0:T(8,128)(2,1)S(1)} %get-tuple-element.154.refs_1_) | copy-start | bytes 1572868
  326.8 72.0 %copy-start.39 = (bf16[128,2048]{1,0:T(8,128)(2,1)}, bf16[128,2048]{1,0:T(8,128)(2,1)S(1)}, u32[]{:S(2)}) copy-start(bf16[128,2048]{1,0:T(8,128)(2,1)S(1)} %get-tuple-element.155.refs_0_) | copy-start | bytes 1572868
  326.9 70.7 %collective-permute-start.12 = (bf16[128,2048]{1,0:T(8,128)(2,1)S(1)}, bf16[128,2048]{1,0:T(8,128)(2,1)S(1)}, u32[]{:S(2)}, u32[]{:S(2)}) collective-permute-start(bf16[128,2048]{1,0:T(8,128)(2,1)S(1)} %get-tuple-element.154.refs_1_), channel_id=1, source_target_pairs={{0,24},{4,28},{8,0},{12,4},{16,8},{20,12},{24,16},{28,20},{1,25},{... | collective-permute-start | bytes 1572872 | tf_op jit(solution)/shard_map/ppermute | solution.py:1207
  333.5 65.3 %collective-permute-start.10 = (bf16[128,2048]{1,0:T(8,128)(2,1)S(1)}, bf16[128,2048]{1,0:T(8,128)(2,1)}, u32[]{:S(2)}, u32[]{:S(2)}) collective-permute-start(bf16[128,2048]{1,0:T(8,128)(2,1)S(1)} %get-tuple-element.154.refs_1_), channel_id=1, source_target_pairs={{0,16},{4,20},{8,24},{12,28},{16,0},{20,4},{24,8},{28,12},{1,17},{... | collective-permute-start | bytes 1572872 | tf_op jit(solution)/shard_map/ppermute | solution.py:1207
  333.5 65.4 %collective-permute-start.8 = (bf16[128,2048]{1,0:T(8,128)(2,1)S(1)}, bf16[128,2048]{1,0:T(8,128)(2,1)}, u32[]{:S(2)}, u32[]{:S(2)}) collective-permute-start(bf16[128,2048]{1,0:T(8,128)(2,1)S(1)} %get-tuple-element.154.refs_1_), channel_id=1, source_target_pairs={{0,8},{4,12},{8,16},{12,20},{16,24},{20,28},{24,0},{28,4},{1,9},{5... | collective-permute-start | bytes 1572872 | tf_op jit(solution)/shard_map/ppermute | solution.py:1207
  334.1 66.7 %collective-permute-start.7 = (bf16[128,2048]{1,0:T(8,128)(2,1)S(1)}, bf16[128,2048]{1,0:T(8,128)(2,1)S(1)}, u32[]{:S(2)}, u32[]{:S(2)}) collective-permute-start(bf16[128,2048]{1,0:T(8,128)(2,1)S(1)} %get-tuple-element.154.refs_1_), channel_id=1, source_target_pairs={{0,4},{4,0},{8,12},{12,8},{16,20},{20,16},{24,28},{28,24},{1,5},{5... | collective-permute-start | bytes 1572872 | tf_op jit(solution)/shard_map/ppermute | solution.py:1211
  334.1 98.7 %collective-permute-start.5 = (bf16[128,2048]{1,0:T(8,128)(2,1)S(1)}, bf16[128,2048]{1,0:T(8,128)(2,1)}, u32[]{:S(2)}, u32[]{:S(2)}) collective-permute-start(bf16[128,2048]{1,0:T(8,128)(2,1)S(1)} %get-tuple-element.155.refs_0_), channel_id=1, source_target_pairs={{0,24},{4,28},{8,0},{12,4},{16,8},{20,12},{24,16},{28,20},{1,25},{... | collective-permute-start | bytes 1572872 | tf_op jit(solution)/shard_map/ppermute | solution.py:1207
  397.5 35.2 %copy-start.50 = (bf16[128,2048]{1,0:T(8,128)(2,1)}, bf16[128,2048]{1,0:T(8,128)(2,1)S(1)}, u32[]{:S(2)}) copy-start(bf16[128,2048]{1,0:T(8,128)(2,1)S(1)} %collective-permute-done.12.refs_7_) | copy-start | bytes 1572868
  397.5 36.7 %collective-permute-start.3 = (bf16[128,2048]{1,0:T(8,128)(2,1)S(1)}, bf16[128,2048]{1,0:T(8,128)(2,1)}, u32[]{:S(2)}, u32[]{:S(2)}) collective-permute-start(bf16[128,2048]{1,0:T(8,128)(2,1)S(1)} %get-tuple-element.155.refs_0_), channel_id=1, source_target_pairs={{0,16},{4,20},{8,24},{12,28},{16,0},{20,4},{24,8},{28,12},{1,17},{... | collective-permute-start | bytes 1572872 | tf_op jit(solution)/shard_map/ppermute | solution.py:1207
  398.8 36.1 %collective-permute-start.1 = (bf16[128,2048]{1,0:T(8,128)(2,1)S(1)}, bf16[128,2048]{1,0:T(8,128)(2,1)}, u32[]{:S(2)}, u32[]{:S(2)}) collective-permute-start(bf16[128,2048]{1,0:T(8,128)(2,1)S(1)} %get-tuple-element.155.refs_0_), channel_id=1, source_target_pairs={{0,8},{4,12},{8,16},{12,20},{16,24},{20,28},{24,0},{28,4},{1,9},{5... | collective-permute-start | bytes 1572872 | tf_op jit(solution)/shard_map/ppermute | solution.py:1207
  398.9 37.4 %collective-permute-start = (bf16[128,2048]{1,0:T(8,128)(2,1)S(1)}, bf16[128,2048]{1,0:T(8,128)(2,1)S(1)}, u32[]{:S(2)}, u32[]{:S(2)}) collective-permute-start(bf16[128,2048]{1,0:T(8,128)(2,1)S(1)} %get-tuple-element.155.refs_0_), channel_id=1, source_target_pairs={{0,4},{4,0},{8,12},{12,8},{16,20},{20,16},{24,28},{28,24},{1,5},{5... | collective-permute-start | bytes 1572872 | tf_op jit(solution)/shard_map/ppermute | solution.py:1211
  400.8 31.9 %copy-start.51 = (bf16[128,2048]{1,0:T(8,128)(2,1)}, bf16[128,2048]{1,0:T(8,128)(2,1)S(1)}, u32[]{:S(2)}) copy-start(bf16[128,2048]{1,0:T(8,128)(2,1)S(1)} %collective-permute-done.7.refs_9_) | copy-start | bytes 1572868
  400.8 36.1 %collective-permute-start.13 = (bf16[128,2048]{1,0:T(8,128)(2,1)S(1)}, bf16[128,2048]{1,0:T(8,128)(2,1)S(1)}, u32[]{:S(2)}, u32[]{:S(2)}) collective-permute-start(bf16[128,2048]{1,0:T(8,128)(2,1)S(1)} %collective-permute-done.12.refs_7_), channel_id=1, source_target_pairs={{0,4},{4,0},{8,12},{12,8},{16,20},{20,16},{24,28},{28,24},{1,5},{5... | collective-permute-start | bytes 1572872 | tf_op jit(solution)/shard_map/ppermute | solution.py:1211
  407.9 31.2 %copy-start.9 = (f32[8,8,256]{2,1,0:T(8,128)S(1)}, f32[8,8,256]{2,1,0:T(8,128)}, u32[]{:S(2)}) copy-start(f32[8,8,256]{2,1,0:T(8,128)} %pad.12.w_ref) | copy-start | bytes 196612
  432.8 22.3 %collective-permute-start.11 = (bf16[128,2048]{1,0:T(8,128)(2,1)}, bf16[128,2048]{1,0:T(8,128)(2,1)}, u32[]{:S(2)}, u32[]{:S(2)}) collective-permute-start(bf16[128,2048]{1,0:T(8,128)(2,1)} %collective-permute-done.10.refs_5_), channel_id=1, source_target_pairs={{0,4},{4,0},{8,12},{12,8},{16,20},{20,16},{24,28},{28,24},{1,5},{5... | collective-permute-start | bytes 1572872 | tf_op jit(solution)/shard_map/ppermute | solution.py:1211
  434.2 24.9 %collective-permute-start.9 = (bf16[128,2048]{1,0:T(8,128)(2,1)}, bf16[128,2048]{1,0:T(8,128)(2,1)}, u32[]{:S(2)}, u32[]{:S(2)}) collective-permute-start(bf16[128,2048]{1,0:T(8,128)(2,1)} %collective-permute-done.8.refs_3_), channel_id=1, source_target_pairs={{0,4},{4,0},{8,12},{12,8},{16,20},{20,16},{24,28},{28,24},{1,5},{5... | collective-permute-start | bytes 1572872 | tf_op jit(solution)/shard_map/ppermute | solution.py:1211
  434.9 35.5 %collective-permute-start.6 = (bf16[128,2048]{1,0:T(8,128)(2,1)}, bf16[128,2048]{1,0:T(8,128)(2,1)}, u32[]{:S(2)}, u32[]{:S(2)}) collective-permute-start(bf16[128,2048]{1,0:T(8,128)(2,1)} %collective-permute-done.5.refs_6_), channel_id=1, source_target_pairs={{0,4},{4,0},{8,12},{12,8},{16,20},{20,16},{24,28},{28,24},{1,5},{5... | collective-permute-start | bytes 1572872 | tf_op jit(solution)/shard_map/ppermute | solution.py:1211
  436.3 45.4 %collective-permute-start.4 = (bf16[128,2048]{1,0:T(8,128)(2,1)}, bf16[128,2048]{1,0:T(8,128)(2,1)}, u32[]{:S(2)}, u32[]{:S(2)}) collective-permute-start(bf16[128,2048]{1,0:T(8,128)(2,1)} %collective-permute-done.3.refs_4_), channel_id=1, source_target_pairs={{0,4},{4,0},{8,12},{12,8},{16,20},{20,16},{24,28},{28,24},{1,5},{5... | collective-permute-start | bytes 1572872 | tf_op jit(solution)/shard_map/ppermute | solution.py:1211
  437.9 54.3 %collective-permute-start.2 = (bf16[128,2048]{1,0:T(8,128)(2,1)}, bf16[128,2048]{1,0:T(8,128)(2,1)}, u32[]{:S(2)}, u32[]{:S(2)}) collective-permute-start(bf16[128,2048]{1,0:T(8,128)(2,1)} %collective-permute-done.1.refs_2_), channel_id=1, source_target_pairs={{0,4},{4,0},{8,12},{12,8},{16,20},{20,16},{24,28},{28,24},{1,5},{5... | collective-permute-start | bytes 1572872 | tf_op jit(solution)/shard_map/ppermute | solution.py:1211
  529.5 630.8 %reduce-scatter.6.cloned.1.call-start = ((), (), s32[]{:S(2)}) async-start(), calls=%async_computation.9 | async-start | bytes 20971520 | tf_op jit(solution)/shard_map/reduce_scatter | solution.py:1305
  529.5 36.0 %collective-permute-start.15 = (bf16[256,2048]{1,0:T(8,128)(2,1)}, bf16[256,2048]{1,0:T(8,128)(2,1)S(1)}, u32[]{:S(2)}, u32[]{:S(2)}) collective-permute-start(bf16[256,2048]{1,0:T(8,128)(2,1)} %copy-done.20), channel_id=1, source_target_pairs={{0,4},{4,0},{8,12},{12,8},{16,20},{20,16},{24,28},{28,24},{1,5},{5... | collective-permute-start | bytes 3145736 | tf_op jit(solution)/shard_map/ppermute | solution.py:1211
  531.1 47.2 %collective-permute-start.16 = (bf16[256,2048]{1,0:T(8,128)(2,1)S(1)}, bf16[256,2048]{1,0:T(8,128)(2,1)S(1)}, u32[]{:S(2)}, u32[]{:S(2)}) collective-permute-start(bf16[256,2048]{1,0:T(8,128)(2,1)S(1)} %get-tuple-element.118), channel_id=1, source_target_pairs={{0,4},{4,0},{8,12},{12,8},{16,20},{20,16},{24,28},{28,24},{1,5},{5... | collective-permute-start | bytes 3145736 | tf_op jit(solution)/shard_map/ppermute | solution.py:1211
  531.6 67.5 %collective-permute-start.17 = (bf16[256,2048]{1,0:T(8,128)(2,1)S(1)}, bf16[256,2048]{1,0:T(8,128)(2,1)S(1)}, u32[]{:S(2)}, u32[]{:S(2)}) collective-permute-start(bf16[256,2048]{1,0:T(8,128)(2,1)S(1)} %get-tuple-element.119), channel_id=1, source_target_pairs={{0,4},{4,0},{8,12},{12,8},{16,20},{20,16},{24,28},{28,24},{1,5},{5... | collective-permute-start | bytes 3145736 | tf_op jit(solution)/shard_map/ppermute | solution.py:1211
  565.5 33.6 %copy-start.34 = (bf16[256,2048]{1,0:T(8,128)(2,1)}, bf16[256,2048]{1,0:T(8,128)(2,1)S(1)}, u32[]{:S(2)}) copy-start(bf16[256,2048]{1,0:T(8,128)(2,1)S(1)} %collective-permute-done.15) | copy-start | bytes 3145732
  578.3 21.8 %copy-start.37 = (bf16[256,2048]{1,0:T(8,128)(2,1)}, bf16[256,2048]{1,0:T(8,128)(2,1)S(1)}, u32[]{:S(2)}) copy-start(bf16[256,2048]{1,0:T(8,128)(2,1)S(1)} %collective-permute-done.16) | copy-start | bytes 3145732
  746.0 414.3 %reduce-scatter.8.cloned.1.call-start = ((), (), s32[]{:S(2)}) async-start(), calls=%async_computation.10 | async-start | bytes 20971520 | tf_op jit(solution)/shard_map/reduce_scatter | solution.py:1305
  746.8 9.3 copy-start.2
  746.8 9.3 copy-start.36
  746.8 12.7 %copy-start.41 = (f32[1,2048]{1,0:T(1,128)S(1)}, f32[1,2048]{1,0:T(1,128)}, u32[]{:S(2)}) copy-start(f32[1,2048]{1,0:T(1,128)} %copy-done.40) | copy-start | bytes 24580
  746.8 12.7 %copy-start.43 = (f32[256]{0:T(256)S(1)}, f32[256]{0:T(256)}, u32[]{:S(2)}) copy-start(f32[256]{0:T(256)} %copy-done.42) | copy-start | bytes 3076
  746.8 23.1 %collective-permute-start.14 = (bf16[256,2048]{1,0:T(8,128)(2,1)}, bf16[256,2048]{1,0:T(8,128)(2,1)}, u32[]{:S(2)}, u32[]{:S(2)}) collective-permute-start(bf16[256,2048]{1,0:T(8,128)(2,1)} %copy-done.19), channel_id=1, source_target_pairs={{0,4},{4,0},{8,12},{12,8},{16,20},{20,16},{24,28},{28,24},{1,5},{5... | collective-permute-start | bytes 3145736 | tf_op jit(solution)/shard_map/ppermute | solution.py:1211
  750.3 49.6 %collective-permute-start.19 = (bf16[256,2048]{1,0:T(8,128)(2,1)}, bf16[256,2048]{1,0:T(8,128)(2,1)}, u32[]{:S(2)}, u32[]{:S(2)}) collective-permute-start(bf16[256,2048]{1,0:T(8,128)(2,1)} %add_convert_fusion.2), channel_id=1, source_target_pairs={{0,16},{4,20},{8,24},{12,28},{16,0},{20,4},{24,8},{28,12},{1,17},{... | collective-permute-start | bytes 3145736 | tf_op jit(solution)/shard_map/ppermute | solution.py:1215
  756.1 69.9 %collective-permute-start.18 = (bf16[256,2048]{1,0:T(8,128)(2,1)}, bf16[256,2048]{1,0:T(8,128)(2,1)}, u32[]{:S(2)}, u32[]{:S(2)}) collective-permute-start(bf16[256,2048]{1,0:T(8,128)(2,1)} %add_convert_fusion.3), channel_id=1, source_target_pairs={{0,24},{4,28},{8,0},{12,4},{16,8},{20,12},{24,16},{28,20},{1,25},{... | collective-permute-start | bytes 3145736 | tf_op jit(solution)/shard_map/ppermute | solution.py:1215
  757.5 68.5 %collective-permute-start.20 = (bf16[256,2048]{1,0:T(8,128)(2,1)}, bf16[256,2048]{1,0:T(8,128)(2,1)}, u32[]{:S(2)}, u32[]{:S(2)}) collective-permute-start(bf16[256,2048]{1,0:T(8,128)(2,1)} %add_convert_fusion.1), channel_id=1, source_target_pairs={{0,8},{4,12},{8,16},{12,20},{16,24},{20,28},{24,0},{28,4},{1,9},{5... | collective-permute-start | bytes 3145736 | tf_op jit(solution)/shard_map/ppermute | solution.py:1215
  964.5 22.1 %copy-start.6 = (f32[256,128]{1,0:T(8,128)S(1)}, f32[256,128]{1,0:T(8,128)}, u32[]{:S(2)}) copy-start(f32[256,128]{1,0:T(8,128)} %copy-done.5) | copy-start | bytes 393220
  964.5 22.1 %copy-start.8 = (f32[256,128]{1,0:T(8,128)S(1)}, f32[256,128]{1,0:T(8,128)}, u32[]{:S(2)}) copy-start(f32[256,128]{1,0:T(8,128)} %copy-done.7) | copy-start | bytes 393220
  964.5 22.1 %copy-start.11 = (f32[8,128]{1,0:T(8,128)S(1)}, f32[8,128]{1,0:T(8,128)}, u32[]{:S(2)}) copy-start(f32[8,128]{1,0:T(8,128)} %copy-done.10) | copy-start | bytes 12292
  964.5 22.2 %copy-start.13 = (f32[8,128]{1,0:T(8,128)S(1)}, f32[8,128]{1,0:T(8,128)}, u32[]{:S(2)}) copy-start(f32[8,128]{1,0:T(8,128)} %copy-done.12) | copy-start | bytes 12292
  964.5 22.2 %copy-start.15 = (f32[2,256]{1,0:T(2,128)S(1)}, f32[2,256]{1,0:T(2,128)}, u32[]{:S(2)}) copy-start(f32[2,256]{1,0:T(2,128)} %copy-done.14) | copy-start | bytes 6148
  993.2 29.5 %slice-start = ((s8[8388608]{0:T(1024)(128)(4,1)}), s8[4194304]{0:T(1024)(128)(4,1)S(1)}, s32[]{:S(2)}) async-start(s8[8388608]{0:T(1024)(128)(4,1)} %bitcast.70), calls=%async_computation.11 | async-start | bytes 8388608
  1011.3 11.4 slice-start.1
  1025.1 9.0 copy-start.17
  (22 other events, 42.6 us)
Sparse Core Ops, SparseCore 0:
  9.5 75.4 all-gather.4
  87.2 104.6 all-gather.6
  194.0 105.8 all-gather.8
  302.0 105.8 all-gather.10
  529.6 125.0 reduce-scatter.3
  746.1 123.2 reduce-scatter.5
  872.0 125.0 reduce-scatter.7
